TPU v7x, 32 devices: a whole 2x2x4 slice. The times are simulated.
32 devices in a mesh: dp: 4 (over y, x), expert: 4 (over z), tensor: 2 (over core).
Axes of the slice: x: 2, y: 2, z: 4, core: 2. Of those that a mesh axis runs over, the one named last changes fastest.
Arguments:
- block_input: bfloat16 [2048, 2048], P(('dp', 'expert')), may hold values from -24 to 24
- attn_gain: bfloat16 [2048], P(('dp', 'expert')), may hold values from 0.5 to 1.5
- query_weight: bfloat16 [2048, 2048], P(('dp', 'expert'), 'tensor'), may hold values from -1 to 1
- key_weight: bfloat16 [2048, 2048], P(('dp', 'expert'), 'tensor'), may hold values from -16 to 16
- value_weight: bfloat16 [2048, 2048], P(('dp', 'expert'), 'tensor'), may hold values from -0.125 to 0.125
- output_weight: bfloat16 [2048, 2048], P('tensor', ('dp', 'expert')), may hold values from -0.75 to 0.75
- ffn_gain: bfloat16 [2048], P(('dp', 'expert')), may hold values from 0.5 to 1.5
- router_weight: bfloat16 [2048, 16], P(('dp', 'expert')), may hold values from -8 to 8
- expert_gate: bfloat16 [16, 2048, 1408], P('expert', 'dp', 'tensor'), may hold values from -0.125 to 0.125
- expert_up: bfloat16 [16, 2048, 1408], P('expert', 'dp', 'tensor'), may hold values from -0.125 to 0.125
- expert_down: bfloat16 [16, 1408, 2048], P('expert', 'tensor', 'dp'), may hold values from -1.25 to 1.25
- shared_gate: bfloat16 [2048, 2816], P(('dp', 'expert'), 'tensor'), may hold values from -0.125 to 0.125
- shared_up: bfloat16 [2048, 2816], P(('dp', 'expert'), 'tensor'), may hold values from -0.125 to 0.125
- shared_down: bfloat16 [2816, 2048], P('tensor', ('dp', 'expert')), may hold values from -0.109375 to 0.109375
- segments: int32 [16, 128], P(('dp', 'expert')), may hold values from 0 to 2, never falling along the last dimension, each value on 1 to 64 neighbouring positions
- routes: int32 [2048, 6], P(('dp', 'expert')), may hold values from 0 to 15, all different within a row; in each aligned block of 128 rows (0 to 127, 128 to 255, ...) at most 96 rows name the same one
- cotangent: bfloat16 [2048, 2048], P(('dp', 'expert')), may hold values from -6 to 6
Outputs:
- block_output: bfloat16 [2048, 2048], P(('dp', 'expert'))
- input_grad: float32 [2048, 2048], P(('dp', 'expert'))
- attn_gain_grad: float32 [2048], P(('dp', 'expert'))
- query_grad: float32 [2048, 2048], P(('dp', 'expert'), 'tensor')
- key_grad: float32 [2048, 2048], P(('dp', 'expert'), 'tensor')
- value_grad: float32 [2048, 2048], P(('dp', 'expert'), 'tensor')
- output_grad: float32 [2048, 2048], P('tensor', ('dp', 'expert'))
- ffn_gain_grad: float32 [2048], P(('dp', 'expert'))
- router_grad: float32 [2048, 16], P(('dp', 'expert'))
- expert_gate_grad: float32 [16, 2048, 1408], P('expert', 'dp', 'tensor')
- expert_up_grad: float32 [16, 2048, 1408], P('expert', 'dp', 'tensor')
- expert_down_grad: float32 [16, 1408, 2048], P('expert', 'tensor', 'dp')
- shared_gate_grad: float32 [2048, 2816], P(('dp', 'expert'), 'tensor')
- shared_up_grad: float32 [2048, 2816], P(('dp', 'expert'), 'tensor')
- shared_down_grad: float32 [2816, 2048], P('tensor', ('dp', 'expert'))
Inputs may be any that keep to these rules, and one draw needn't show every extreme that they name: `segments`: within each row the numbers never fall; each document holds 1 to 64 positions, one exactly 64. `routes`: each token names 6 different experts; among the 128 rows of one device no expert is named by more than 96 rows, a bound that some block reaches.
All inputs are finite; a program needn't handle non-finite values.
Results may differ from a plain program's by a relative error of at most 0.019.
The roundings to bfloat16 on the way count: a program that leaves them out, or rounds other values in their place, can miss the bound.
Values may be sent and summed in bfloat16 or wider, within the bound.
A program may use at most 320 MiB of HBM per device.

v0:
```python
import math

import jax
import jax.numpy as jnp
from jax import lax
from jax.sharding import PartitionSpec as P

D = 2048
HD = 128
TOPK = 6


epsilon = 1e-06
rope_base = 10000.0
masked_score = -1e30


def rms_scale(vector):
    return lax.rsqrt(jnp.mean(vector * vector, axis=-1, keepdims=True) + epsilon)


def rope_tables(count, width):
    half_width = width // 2
    frequency = rope_base ** (-jnp.arange(half_width, dtype=jnp.float32) / half_width)
    angles = jnp.arange(count, dtype=jnp.float32)[:, None] * frequency[None, :]
    return (jnp.cos(angles)[:, None, :], jnp.sin(angles)[:, None, :])


def rotate(vector, cosine, sine_table):
    half_width = vector.shape[-1] // 2
    first_half = vector[..., :half_width]
    second_half = vector[..., half_width:]
    return jnp.concatenate(
        [
            first_half * cosine - second_half * sine_table,
            first_half * sine_table + second_half * cosine,
        ],
        axis=-1,
    )


def unrotate(vector, cosine, sine_table):
    half_width = vector.shape[-1] // 2
    first_half = vector[..., :half_width]
    second_half = vector[..., half_width:]
    return jnp.concatenate(
        [
            first_half * cosine + second_half * sine_table,
            second_half * cosine - first_half * sine_table,
        ],
        axis=-1,
    )


def silu_parts(before):
    sigmoid_val = jax.nn.sigmoid(before)
    return (before * sigmoid_val, sigmoid_val * (1.0 + before * (1.0 - sigmoid_val)))


def masked_scores(query_rot, key_rot, allowed):
    scores = jnp.einsum(
        "qhd,khd->hqk", query_rot, key_rot, preferred_element_type=jnp.float32
    ) / math.sqrt(query_rot.shape[-1])
    return jnp.where(allowed[None], scores, masked_score)


def send_out(flat_rows, experts_here, owners, cap_rows):
    model_width = flat_rows.shape[1]
    arrived = lax.all_to_all(
        flat_rows.reshape(experts_here, owners, cap_rows, model_width),
        "expert",
        split_axis=1,
        concat_axis=1,
        tiled=True,
    )
    return arrived.reshape(experts_here, owners * cap_rows, model_width)


def body(
    block_input,
    attn_gain,
    query_weight,
    key_weight,
    value_weight,
    output_weight,
    ffn_gain,
    router_weight,
    expert_gate,
    expert_up,
    expert_down,
    shared_gate,
    shared_up,
    shared_down,
    segments,
    routes,
    cotangent,
):
    (
        full_query,
        full_key,
        full_value,
        full_sgate,
        full_sup,
        gain_attn,
        gain_ffn,
        full_router,
        full_output,
        full_sdown,
    ) = (
        lax.all_gather(query_weight, ("dp", "expert"), axis=0, tiled=True),
        lax.all_gather(key_weight, ("dp", "expert"), axis=0, tiled=True),
        lax.all_gather(value_weight, ("dp", "expert"), axis=0, tiled=True),
        lax.all_gather(shared_gate, ("dp", "expert"), axis=0, tiled=True),
        lax.all_gather(shared_up, ("dp", "expert"), axis=0, tiled=True),
        lax.all_gather(attn_gain, ("dp", "expert"), axis=0, tiled=True),
        lax.all_gather(ffn_gain, ("dp", "expert"), axis=0, tiled=True),
        lax.all_gather(router_weight, ("dp", "expert"), axis=0, tiled=True),
        lax.all_gather(output_weight, ("dp", "expert"), axis=1, tiled=True),
        lax.all_gather(shared_down, ("dp", "expert"), axis=1, tiled=True),
    )
    seq_len = block_input.shape[0]
    total_experts = router_weight.shape[1]
    experts_here = expert_gate.shape[0]
    owners = lax.axis_size("expert")
    cap_rows = 2 * seq_len * TOPK // total_experts
    local_gate, local_up, local_down = (
        lax.all_gather(expert_gate, "dp", axis=1, tiled=True),
        lax.all_gather(expert_up, "dp", axis=1, tiled=True),
        lax.all_gather(expert_down, "dp", axis=2, tiled=True),
    )
    heads_here = full_query.shape[1] // HD
    gain_one = gain_attn.astype(jnp.float32)
    gain_two = gain_ffn.astype(jnp.float32)
    input_f = block_input.astype(jnp.float32)
    scale_one = rms_scale(input_f)
    normed_one = (input_f * scale_one * gain_one).astype(jnp.bfloat16)
    cosine, sine_table = rope_tables(seq_len, HD)
    query_pre = jnp.dot(normed_one, full_query, preferred_element_type=jnp.float32).reshape(
        seq_len, heads_here, HD
    )
    key_pre = jnp.dot(normed_one, full_key, preferred_element_type=jnp.float32).reshape(
        seq_len, heads_here, HD
    )
    query_rot = rotate(query_pre, cosine, sine_table).astype(jnp.bfloat16)
    key_rot = rotate(key_pre, cosine, sine_table).astype(jnp.bfloat16)
    value_rows = (
        jnp.dot(normed_one, full_value, preferred_element_type=jnp.float32)
        .astype(jnp.bfloat16)
        .reshape(seq_len, heads_here, HD)
    )
    position = jnp.arange(seq_len)
    segment_row = segments[0]
    allowed = (position[:, None] >= position[None, :]) & (
        segment_row[:, None] == segment_row[None, :]
    )
    scores = masked_scores(query_rot, key_rot, allowed)
    top_score = jnp.max(scores, axis=-1, keepdims=True)
    shifted = jnp.exp(scores - top_score)
    row_total = jnp.sum(shifted, axis=-1, keepdims=True)
    log_total = top_score + jnp.log(row_total)
    prob_low = (shifted / row_total).astype(jnp.bfloat16)
    mixed_rows = (
        jnp.einsum("hqk,khd->qhd", prob_low, value_rows, preferred_element_type=jnp.float32)
        .astype(jnp.bfloat16)
        .reshape(seq_len, heads_here * HD)
    )
    attn_part = jnp.dot(mixed_rows, full_output, preferred_element_type=jnp.float32)
    attn_total = lax.psum(attn_part, "tensor")
    hidden_one = input_f + attn_total
    scale_two = rms_scale(hidden_one)
    normed_two = (hidden_one * scale_two * gain_two).astype(jnp.bfloat16)
    logits = jnp.dot(normed_two, full_router, preferred_element_type=jnp.float32)
    router_probs = jax.nn.softmax(logits, axis=-1)
    expert_ids = jnp.arange(total_experts, dtype=jnp.int32)
    route_match = routes[:, :, None] == expert_ids[None, None, :]
    route_hot = route_match.astype(jnp.float32)
    gate_probs = jnp.sum(route_hot * router_probs[:, None, :], axis=-1)
    flat_hot = route_match.astype(jnp.int32).reshape(seq_len * TOPK, total_experts)
    rank_table = jnp.cumsum(flat_hot, axis=0) - 1
    slot_of = jnp.sum(rank_table * flat_hot, axis=1)
    flat_routes = routes.reshape(-1)
    owner_of = flat_routes // experts_here
    local_of = flat_routes % experts_here
    target = local_of * (owners * cap_rows) + owner_of * cap_rows + slot_of
    token_of = jnp.arange(seq_len * TOPK) // TOPK
    buffer_rows = experts_here * owners * cap_rows
    send_rows = jnp.zeros((buffer_rows, D), jnp.bfloat16).at[target].set(normed_two[token_of])
    owner_rows = send_out(send_rows, experts_here, owners, cap_rows)
    gate_pre = jnp.einsum(
        "erd,edf->erf", owner_rows, local_gate, preferred_element_type=jnp.float32
    )
    up_pre = jnp.einsum("erd,edf->erf", owner_rows, local_up, preferred_element_type=jnp.float32)
    silu_gate, slope_gate = silu_parts(gate_pre)
    act_rows = (silu_gate * up_pre).astype(jnp.bfloat16)
    part_rows = jnp.einsum(
        "erf,efd->erd", act_rows, local_down, preferred_element_type=jnp.float32
    ).astype(jnp.bfloat16)
    back_rows = lax.all_to_all(
        part_rows.reshape(experts_here, owners, cap_rows, D),
        "expert",
        split_axis=1,
        concat_axis=1,
        tiled=True,
    )
    copies = back_rows.reshape(buffer_rows, D)[target].reshape(seq_len, TOPK, D)
    routed_part = jnp.einsum("sk,skd->sd", gate_probs, copies, preferred_element_type=jnp.float32)
    shared_gpre = jnp.dot(normed_two, full_sgate, preferred_element_type=jnp.float32)
    shared_upre = jnp.dot(normed_two, full_sup, preferred_element_type=jnp.float32)
    silu_shared, slope_shared = silu_parts(shared_gpre)
    shared_act = (silu_shared * shared_upre).astype(jnp.bfloat16)
    shared_part = jnp.dot(shared_act, full_sdown, preferred_element_type=jnp.float32)
    ffn_total = lax.psum((shared_part + routed_part).astype(jnp.bfloat16), "tensor").astype(
        jnp.float32
    )
    block_output = (hidden_one + ffn_total).astype(jnp.bfloat16)
    grad_out = cotangent.astype(jnp.float32)
    grad_sact = jnp.einsum("sd,fd->sf", cotangent, full_sdown, preferred_element_type=jnp.float32)
    grad_sgate = (grad_sact * shared_upre * slope_shared).astype(jnp.bfloat16)
    grad_sup = (grad_sact * silu_shared).astype(jnp.bfloat16)
    sdown_full = jnp.einsum("sf,sd->fd", shared_act, cotangent, preferred_element_type=jnp.float32)
    sgate_full = jnp.einsum("sd,sf->df", normed_two, grad_sgate, preferred_element_type=jnp.float32)
    sup_full = jnp.einsum("sd,sf->df", normed_two, grad_sup, preferred_element_type=jnp.float32)
    grad_normed_two = jnp.einsum(
        "sf,df->sd", grad_sgate, full_sgate, preferred_element_type=jnp.float32
    )
    grad_normed_two = grad_normed_two + jnp.einsum(
        "sf,df->sd", grad_sup, full_sup, preferred_element_type=jnp.float32
    )
    grad_copy = (gate_probs.reshape(-1)[:, None] * grad_out[token_of]).astype(jnp.bfloat16)
    send_grads = jnp.zeros((buffer_rows, D), jnp.bfloat16).at[target].set(grad_copy)
    owner_grads = send_out(send_grads, experts_here, owners, cap_rows)
    grad_act = jnp.einsum(
        "erd,efd->erf", owner_grads, local_down, preferred_element_type=jnp.float32
    )
    grad_gate_pre = (grad_act * up_pre * slope_gate).astype(jnp.bfloat16)
    grad_up_pre = (grad_act * silu_gate).astype(jnp.bfloat16)
    down_local = jnp.einsum(
        "erf,erd->efd", act_rows, owner_grads, preferred_element_type=jnp.float32
    )
    gate_local = jnp.einsum(
        "erd,erf->edf", owner_rows, grad_gate_pre, preferred_element_type=jnp.float32
    )
    up_local = jnp.einsum(
        "erd,erf->edf", owner_rows, grad_up_pre, preferred_element_type=jnp.float32
    )
    grad_rows = jnp.einsum(
        "erf,edf->erd", grad_gate_pre, local_gate, preferred_element_type=jnp.float32
    )
    grad_rows = grad_rows + jnp.einsum(
        "erf,edf->erd", grad_up_pre, local_up, preferred_element_type=jnp.float32
    )
    rows_back = lax.all_to_all(
        grad_rows.reshape(experts_here, owners, cap_rows, D).astype(jnp.bfloat16),
        "expert",
        split_axis=1,
        concat_axis=1,
        tiled=True,
    ).astype(jnp.float32)
    grad_normed_two = grad_normed_two + jnp.sum(
        rows_back.reshape(buffer_rows, D)[target].reshape(seq_len, TOPK, D), axis=1
    )
    gate_dot_part = jnp.einsum("skd,sd->sk", copies, grad_out, preferred_element_type=jnp.float32)
    grad_normed_two, gate_grads = (
        lax.psum(grad_normed_two.astype(jnp.bfloat16), "tensor").astype(jnp.float32),
        lax.psum(gate_dot_part.astype(jnp.bfloat16), "tensor").astype(jnp.float32),
    )
    grad_rprobs = jnp.sum(route_hot * gate_grads[:, :, None], axis=1)
    grad_logits = (
        router_probs * (grad_rprobs - jnp.sum(grad_rprobs * router_probs, axis=-1, keepdims=True))
    ).astype(jnp.bfloat16)
    router_full = jnp.einsum(
        "sd,se->de", normed_two, grad_logits, preferred_element_type=jnp.float32
    )
    grad_normed_two = grad_normed_two + jnp.einsum(
        "se,de->sd", grad_logits, full_router, preferred_element_type=jnp.float32
    )
    ffn_gain_full = jnp.sum(grad_normed_two * hidden_one * scale_two, axis=0)
    weighted_two = grad_normed_two * gain_two
    cube_two = scale_two * scale_two * scale_two
    grad_hidden = (
        grad_out
        + scale_two * weighted_two
        - hidden_one * cube_two * jnp.mean(hidden_one * weighted_two, axis=-1, keepdims=True)
    )
    grad_attn = grad_hidden.astype(jnp.bfloat16)
    output_full = jnp.einsum("sc,sd->cd", mixed_rows, grad_attn, preferred_element_type=jnp.float32)
    grad_mixed = (
        jnp.einsum("sd,cd->sc", grad_attn, full_output, preferred_element_type=jnp.float32)
        .astype(jnp.bfloat16)
        .reshape(seq_len, heads_here, HD)
    )
    prob_again = jnp.exp(masked_scores(query_rot, key_rot, allowed) - log_total)
    grad_probs = jnp.einsum(
        "qhd,khd->hqk", grad_mixed, value_rows, preferred_element_type=jnp.float32
    )
    grad_scores = (
        prob_again * (grad_probs - jnp.sum(prob_again * grad_probs, axis=-1, keepdims=True))
    ).astype(jnp.bfloat16)
    value_grad_rows = (
        jnp.einsum(
            "hqk,qhd->khd",
            prob_again.astype(jnp.bfloat16),
            grad_mixed,
            preferred_element_type=jnp.float32,
        )
        .astype(jnp.bfloat16)
        .reshape(seq_len, heads_here * HD)
    )
    inverse_root = 1.0 / math.sqrt(HD)
    grad_qrot = (
        jnp.einsum("hqk,khd->qhd", grad_scores, key_rot, preferred_element_type=jnp.float32)
        * inverse_root
    )
    grad_krot = (
        jnp.einsum("hqk,qhd->khd", grad_scores, query_rot, preferred_element_type=jnp.float32)
        * inverse_root
    )
    grad_qpre = (
        unrotate(grad_qrot, cosine, sine_table)
        .astype(jnp.bfloat16)
        .reshape(seq_len, heads_here * HD)
    )
    grad_kpre = (
        unrotate(grad_krot, cosine, sine_table)
        .astype(jnp.bfloat16)
        .reshape(seq_len, heads_here * HD)
    )
    query_full = jnp.einsum("sd,sc->dc", normed_one, grad_qpre, preferred_element_type=jnp.float32)
    key_full = jnp.einsum("sd,sc->dc", normed_one, grad_kpre, preferred_element_type=jnp.float32)
    value_full = jnp.einsum(
        "sd,sc->dc", normed_one, value_grad_rows, preferred_element_type=jnp.float32
    )
    grad_normed_one = jnp.einsum(
        "sc,dc->sd", grad_qpre, full_query, preferred_element_type=jnp.float32
    )
    grad_normed_one = grad_normed_one + jnp.einsum(
        "sc,dc->sd", grad_kpre, full_key, preferred_element_type=jnp.float32
    )
    grad_normed_one = grad_normed_one + jnp.einsum(
        "sc,dc->sd", value_grad_rows, full_value, preferred_element_type=jnp.float32
    )
    grad_normed_one = lax.psum(grad_normed_one.astype(jnp.bfloat16), "tensor").astype(jnp.float32)
    attn_gain_full = jnp.sum(grad_normed_one * input_f * scale_one, axis=0)
    weighted_one = grad_normed_one * gain_one
    cube_one = scale_one * scale_one * scale_one
    input_grad = (
        grad_hidden
        + scale_one * weighted_one
        - input_f * cube_one * jnp.mean(input_f * weighted_one, axis=-1, keepdims=True)
    )
    (
        query_grad,
        key_grad,
        value_grad,
        shared_gate_grad,
        shared_up_grad,
        attn_gain_grad,
        ffn_gain_grad,
        router_grad,
        output_grad,
        shared_down_grad,
    ) = (
        lax.psum_scatter(query_full, ("dp", "expert"), scatter_dimension=0, tiled=True),
        lax.psum_scatter(key_full, ("dp", "expert"), scatter_dimension=0, tiled=True),
        lax.psum_scatter(value_full, ("dp", "expert"), scatter_dimension=0, tiled=True),
        lax.psum_scatter(sgate_full, ("dp", "expert"), scatter_dimension=0, tiled=True),
        lax.psum_scatter(sup_full, ("dp", "expert"), scatter_dimension=0, tiled=True),
        lax.psum_scatter(attn_gain_full, ("dp", "expert"), scatter_dimension=0, tiled=True),
        lax.psum_scatter(ffn_gain_full, ("dp", "expert"), scatter_dimension=0, tiled=True),
        lax.psum_scatter(router_full, ("dp", "expert"), scatter_dimension=0, tiled=True),
        lax.psum_scatter(output_full, ("dp", "expert"), scatter_dimension=1, tiled=True),
        lax.psum_scatter(sdown_full, ("dp", "expert"), scatter_dimension=1, tiled=True),
    )
    expert_gate_grad, expert_up_grad, expert_down_grad = (
        lax.psum_scatter(
            gate_local.astype(jnp.bfloat16), "dp", scatter_dimension=1, tiled=True
        ).astype(jnp.float32),
        lax.psum_scatter(
            up_local.astype(jnp.bfloat16), "dp", scatter_dimension=1, tiled=True
        ).astype(jnp.float32),
        lax.psum_scatter(
            down_local.astype(jnp.bfloat16), "dp", scatter_dimension=2, tiled=True
        ).astype(jnp.float32),
    )
    return (
        block_output,
        input_grad,
        attn_gain_grad,
        query_grad,
        key_grad,
        value_grad,
        output_grad,
        ffn_gain_grad,
        router_grad,
        expert_gate_grad,
        expert_up_grad,
        expert_down_grad,
        shared_gate_grad,
        shared_up_grad,
        shared_down_grad,
    )


def solution(mesh):
    return jax.shard_map(
        body,
        mesh=mesh,
        in_specs=(
            P(("dp", "expert"), None),
            P(("dp", "expert")),
            P(("dp", "expert"), "tensor"),
            P(("dp", "expert"), "tensor"),
            P(("dp", "expert"), "tensor"),
            P("tensor", ("dp", "expert")),
            P(("dp", "expert")),
            P(("dp", "expert"), None),
            P("expert", "dp", "tensor"),
            P("expert", "dp", "tensor"),
            P("expert", "tensor", "dp"),
            P(("dp", "expert"), "tensor"),
            P(("dp", "expert"), "tensor"),
            P("tensor", ("dp", "expert")),
            P(("dp", "expert"), None),
            P(("dp", "expert"), None),
            P(("dp", "expert"), None),
        ),
        out_specs=(
            P(("dp", "expert"), None),
            P(("dp", "expert"), None),
            P(("dp", "expert")),
            P(("dp", "expert"), "tensor"),
            P(("dp", "expert"), "tensor"),
            P(("dp", "expert"), "tensor"),
            P("tensor", ("dp", "expert")),
            P(("dp", "expert")),
            P(("dp", "expert"), None),
            P("expert", "dp", "tensor"),
            P("expert", "dp", "tensor"),
            P("expert", "tensor", "dp"),
            P(("dp", "expert"), "tensor"),
            P(("dp", "expert"), "tensor"),
            P("tensor", ("dp", "expert")),
        ),
        check_vma=False,
    )
```

profile of v0, /device:TPU:16, one launch (start us, length us, event | category | flops | bytes accessed | tf_op | source)
XLA Modules:
  0.0 3361.8 jit_solution(7577024188678822233)
XLA Ops:
  10.9 36.5 %all-gather = bf16[16,1,128]{2,1,0:T(2,128)(2,1)S(1)} all-gather(bf16[1,1,128]{2,1,0:T(2,128)(2,1)} %bitcast.170), channel_id=1, replica_groups=mesh['dp'=4,'expert'=4,'tensor'=2] {'dp','expert'}, dimensions={0}, use_global_device_ids=true | all-gather | bytes 4352 | tf_op jit(solution)/shard_map/all_gather | solution.py:115
  50.3 37.4 %all-gather.15.cloned.1.call-done = bf16[2048,1024]{1,0:T(8,128)(2,1)} async-done(((bf16[128,1024]{1,0:T(8,128)(2,1)}), bf16[2048,1024]{1,0:T(8,128)(2,1)}) %all-gather.15.cloned.1.call-update) | async-done | bytes 4194320 | tf_op jit(solution)/shard_map/all_gather | solution.py:110
  90.9 73.7 %all-gather.17.cloned.1.call-done = bf16[2048,1024]{1,0:T(8,128)(2,1)} async-done(((bf16[128,1024]{1,0:T(8,128)(2,1)}), bf16[2048,1024]{1,0:T(8,128)(2,1)}) %all-gather.17.cloned.1.call-update) | async-done | bytes 4194320 | tf_op jit(solution)/shard_map/all_gather | solution.py:111
  169.8 71.8 %all-gather.13.cloned.1.call-done = bf16[2048,1024]{1,0:T(8,128)(2,1)} async-done(((bf16[128,1024]{1,0:T(8,128)(2,1)}), bf16[2048,1024]{1,0:T(8,128)(2,1)}) %all-gather.13.cloned.1.call-update) | async-done | bytes 4194320 | tf_op jit(solution)/shard_map/all_gather | solution.py:112
  245.6 85.5 %all-gather.19.cloned.1.call-done = bf16[1024,2048]{1,0:T(8,128)(2,1)} async-done(((bf16[1024,128]{1,0:T(8,128)(2,1)}), bf16[1024,2048]{1,0:T(8,128)(2,1)}) %all-gather.19.cloned.1.call-update) | async-done | bytes 4194320 | tf_op jit(solution)/shard_map/all_gather | solution.py:118
  337.3 34.4 %all-gather.1 = bf16[16,1,128]{2,1,0:T(2,128)(2,1)S(1)} all-gather(bf16[1,1,128]{2,1,0:T(2,128)(2,1)S(1)} %bitcast.171), channel_id=1, replica_groups=mesh['dp'=4,'expert'=4,'tensor'=2] {'dp','expert'}, dimensions={0}, use_global_device_ids=true | all-gather | bytes 4352 | tf_op jit(solution)/shard_map/all_gather | solution.py:116
  376.6 24.5 scatter_custom_fusion
  418.6 127.4 %all-to-all-done = bf16[4,4,96,2048]{3,2,0,1:T(8,128)(2,1)} async-done(((bf16[4,4,96,2048]{3,2,0,1:T(8,128)(2,1)}), bf16[4,4,96,2048]{3,2,0,1:T(8,128)(2,1)}, u32[]{:S(2)}, u32[]{:S(2)}) %all-to-all-start) | async-done | bytes 6291488 | tf_op jit(solution)/shard_map/all_to_all | solution.py:69
  578.2 101.9 %all-gather.31.cloned.1.call-done = bf16[4,704,2048]{2,1,0:T(8,128)(2,1)} async-done(((bf16[4,704,512]{2,1,0:T(8,128)(2,1)}), bf16[4,704,2048]{2,1,0:T(8,128)(2,1)}) %all-gather.31.cloned.1.call-update) | async-done | bytes 11534352 | tf_op jit(solution)/shard_map/all_gather | solution.py:129
  698.8 211.5 %all_gather.48 = bf16[2048,16]{0,1:T(8,128)(2,1)S(1)} all-gather(bf16[128,16]{0,1:T(8,128)(2,1)S(1)} %copy-done.36), channel_id=1, replica_groups=mesh['dp'=4,'expert'=4,'tensor'=2] {'dp','expert'}, dimensions={0}, use_global_device_ids=true | all-gather | bytes 69632 | tf_op jit(solution)/shard_map/all_gather | solution.py:117
  942.2 18.8 scatter_custom_fusion.1
  978.6 201.1 %all-to-all-done.2 = bf16[4,4,96,2048]{3,2,0,1:T(8,128)(2,1)} async-done(((bf16[4,4,96,2048]{3,2,0,1:T(8,128)(2,1)}), bf16[4,4,96,2048]{3,2,0,1:T(8,128)(2,1)}, u32[]{:S(2)}, u32[]{:S(2)}) %all-to-all-start.2) | async-done | bytes 6291488 | tf_op jit(solution)/shard_map/all_to_all | solution.py:69
  1259.9 109.2 %all-to-all-done.3 = bf16[4,4,96,2048]{3,2,0,1:T(8,128)(2,1)} async-done(((bf16[4,4,96,2048]{3,2,0,1:T(8,128)(2,1)}), bf16[4,4,96,2048]{3,2,0,1:T(8,128)(2,1)}, u32[]{:S(2)}, u32[]{:S(2)}) %all-to-all-start.3) | async-done | bytes 6291488 | tf_op jit(solution)/shard_map/all_to_all | solution.py:252
  1537.3 73.1 %all-reduce.2 = (f32[2048]{0:T(1024)S(1)}, f32[2048]{0:T(1024)S(1)}) all-reduce(f32[2048]{0:T(1024)S(1)} %get-tuple-element.17, f32[2048]{0:T(1024)S(1)} %get-tuple-element.15), channel_id=2, replica_groups=mesh['dp'=4,'expert'=4,'tensor'=2] {'dp','expert'}, use_global_device_ids=true, to_apply=%region_24.25.clone | all-reduce | flops 4096 | bytes 32768
  1621.4 74.0 %reduce-scatter.22.cloned.1.call-done = bf16[4,512,704]{1,2,0:T(8,128)(2,1)} async-done(((bf16[4,2048,704]{1,2,0:T(8,128)(2,1)}), bf16[4,512,704]{1,2,0:T(8,128)(2,1)}) %reduce-scatter.22.cloned.1.call-update) | async-done | bytes 2883600 | tf_op jit(solution)/shard_map/reduce_scatter | solution.py:375
  1700.5 109.8 %reduce-scatter.24.cloned.1.call-done = bf16[4,512,704]{1,2,0:T(8,128)(2,1)} async-done(((bf16[4,2048,704]{1,2,0:T(8,128)(2,1)}), bf16[4,512,704]{1,2,0:T(8,128)(2,1)}) %reduce-scatter.24.cloned.1.call-update) | async-done | bytes 2883600 | tf_op jit(solution)/shard_map/reduce_scatter | solution.py:378
  1815.5 70.1 %reduce-scatter.20.cloned.1.call-done = f32[128,16]{0,1:T(8,128)} async-done(((f32[2048,16]{0,1:T(8,128)}), f32[128,16]{0,1:T(8,128)}) %reduce-scatter.20.cloned.1.call-update) | async-done | bytes 8208 | tf_op jit(solution)/shard_map/reduce_scatter | solution.py:370
  1885.6 247.1 %reduce-scatter.28.cloned.1.call-done = f32[128,1408]{1,0:T(8,128)} async-done(((f32[2048,1408]{1,0:T(8,128)}), f32[128,1408]{1,0:T(8,128)}) %reduce-scatter.28.cloned.1.call-update) | async-done | bytes 720912 | tf_op jit(solution)/shard_map/reduce_scatter | solution.py:366
  2132.7 246.4 %reduce-scatter.30.cloned.1.call-done = f32[128,1408]{1,0:T(8,128)} async-done(((f32[2048,1408]{1,0:T(8,128)}), f32[128,1408]{1,0:T(8,128)}) %reduce-scatter.30.cloned.1.call-update) | async-done | bytes 720912 | tf_op jit(solution)/shard_map/reduce_scatter | solution.py:367
  2379.1 246.2 %reduce-scatter.32.cloned.1.call-done = f32[1408,128]{1,0:T(8,128)} async-done(((f32[1408,2048]{1,0:T(8,128)}), f32[1408,128]{1,0:T(8,128)}) %reduce-scatter.32.cloned.1.call-update) | async-done | bytes 720912 | tf_op jit(solution)/shard_map/reduce_scatter | solution.py:372
  2625.3 180.5 %reduce-scatter.16.cloned.1.call-done = f32[128,1024]{1,0:T(8,128)} async-done(((f32[2048,1024]{1,0:T(8,128)}), f32[128,1024]{1,0:T(8,128)}) %reduce-scatter.16.cloned.1.call-update) | async-done | bytes 524304 | tf_op jit(solution)/shard_map/reduce_scatter | solution.py:365
  2805.8 182.7 %reduce-scatter.18.cloned.1.call-done = f32[1024,128]{1,0:T(8,128)} async-done(((f32[1024,2048]{1,0:T(8,128)}), f32[1024,128]{1,0:T(8,128)}) %reduce-scatter.18.cloned.1.call-update) | async-done | bytes 524304 | tf_op jit(solution)/shard_map/reduce_scatter | solution.py:371
  2988.6 182.7 %reduce-scatter.14.cloned.1.call-done = f32[128,1024]{1,0:T(8,128)} async-done(((f32[2048,1024]{1,0:T(8,128)}), f32[128,1024]{1,0:T(8,128)}) %reduce-scatter.14.cloned.1.call-update) | async-done | bytes 524304 | tf_op jit(solution)/shard_map/reduce_scatter | solution.py:364
  3171.3 182.7 %reduce-scatter.12.cloned.1.call-done = f32[128,1024]{1,0:T(8,128)} async-done(((f32[2048,1024]{1,0:T(8,128)}), f32[128,1024]{1,0:T(8,128)}) %reduce-scatter.12.cloned.1.call-update) | async-done | bytes 524304 | tf_op jit(solution)/shard_map/reduce_scatter | solution.py:363
  (260 shorter events, 415.2 us)
Async XLA Ops:
  8.8 155.9 %all-gather.17.cloned.1.call-start = ((), (), s32[]{:S(2)}) async-start(), calls=%async_computation.17 | async-start | bytes 4456448 | tf_op jit(solution)/shard_map/all_gather | solution.py:111
  9.5 232.1 %all-gather.13.cloned.1.call-start = ((), (), s32[]{:S(2)}) async-start(), calls=%async_computation.15 | async-start | bytes 4456448 | tf_op jit(solution)/shard_map/all_gather | solution.py:112
  10.2 320.8 %all-gather.19.cloned.1.call-start = ((), (), s32[]{:S(2)}) async-start(), calls=%async_computation.18 | async-start | bytes 4456448 | tf_op jit(solution)/shard_map/all_gather | solution.py:118
  10.8 363.2 %all-reduce.8.cloned.1.call-start = ((), (), s32[]{:S(2)}) async-start(), calls=%async_computation.19 | async-start | bytes 2097152 | tf_op jit(solution)/shard_map/psum | solution.py:168
  335.0 217.5 %all-gather.27.cloned.1.call-start = ((), (), s32[]{:S(2)}) async-start(), calls=%async_computation.23 | async-start | bytes 14417920 | tf_op jit(solution)/shard_map/all_gather | solution.py:127
  335.6 229.4 %all-gather.29.cloned.1.call-start = ((), (), s32[]{:S(2)}) async-start(), calls=%async_computation.24 | async-start | bytes 14417920 | tf_op jit(solution)/shard_map/all_gather | solution.py:128
  336.2 343.9 %all-gather.31.cloned.1.call-start = ((), (), s32[]{:S(2)}) async-start(), calls=%async_computation.25 | async-start | bytes 14417920 | tf_op jit(solution)/shard_map/all_gather | solution.py:129
  417.9 818.4 %all-gather.21.cloned.1.call-start = ((), (), s32[]{:S(2)}) async-start(), calls=%async_computation.20 | async-start | bytes 6127616 | tf_op jit(solution)/shard_map/all_gather | solution.py:113
  692.0 218.6 %all-to-all-start.1 = ((bf16[4,4,96,2048]{3,2,0,1:T(8,128)(2,1)}), bf16[4,4,96,2048]{3,2,0,1:T(8,128)(2,1)}, u32[]{:S(2)}, u32[]{:S(2)}) async-start(bf16[4,4,96,2048]{3,2,0,1:T(8,128)(2,1)} %copy.148), calls=%async_computation.1 | async-start | bytes 12582912 | tf_op jit(solution)/shard_map/all_to_all | solution.py:198
  697.9 542.9 %all-gather.23.cloned.1.call-start = ((), (), s32[]{:S(2)}) async-start(), calls=%async_computation.21 | async-start | bytes 6127616 | tf_op jit(solution)/shard_map/all_gather | solution.py:114
  967.8 211.9 %all-to-all-start.2 = ((bf16[4,4,96,2048]{3,2,0,1:T(8,128)(2,1)}), bf16[4,4,96,2048]{3,2,0,1:T(8,128)(2,1)}, u32[]{:S(2)}, u32[]{:S(2)}) async-start(bf16[4,4,96,2048]{3,2,0,1:T(8,128)(2,1)} %copy.151), calls=%async_computation.2 | async-start | bytes 12582912 | tf_op jit(solution)/shard_map/all_to_all | solution.py:69
  977.9 267.4 %all-gather.25.cloned.1.call-start = ((), (), s32[]{:S(2)}) async-start(), calls=%async_computation.22 | async-start | bytes 6127616 | tf_op jit(solution)/shard_map/all_gather | solution.py:119
  1236.1 193.6 %all-reduce.10.cloned.1.call-start = ((), (), s32[]{:S(2)}) async-start(), calls=%async_computation.26 | async-start | bytes 1048576 | tf_op jit(solution)/shard_map/psum | solution.py:264
  1455.1 160.7 %reduce-scatter.26.cloned.1.call-start = ((), (), s32[]{:S(2)}) async-start(), calls=%async_computation.34 | async-start | bytes 14417920 | tf_op jit(solution)/shard_map/reduce_scatter | solution.py:381
  1466.6 228.8 %reduce-scatter.22.cloned.1.call-start = ((), (), s32[]{:S(2)}) async-start(), calls=%async_computation.32 | async-start | bytes 14417920 | tf_op jit(solution)/shard_map/reduce_scatter | solution.py:375
  1478.5 331.8 %reduce-scatter.24.cloned.1.call-start = ((), (), s32[]{:S(2)}) async-start(), calls=%async_computation.33 | async-start | bytes 14417920 | tf_op jit(solution)/shard_map/reduce_scatter | solution.py:378
  1489.9 395.7 %reduce-scatter.20.cloned.1.call-start = ((), (), s32[]{:S(2)}) async-start(), calls=%async_computation.31 | async-start | bytes 139264 | tf_op jit(solution)/shard_map/reduce_scatter | solution.py:370
  1490.8 641.9 %reduce-scatter.28.cloned.1.call-start = ((), (), s32[]{:S(2)}) async-start(), calls=%async_computation.35 | async-start | bytes 12255232 | tf_op jit(solution)/shard_map/reduce_scatter | solution.py:366
  1497.8 881.3 %reduce-scatter.30.cloned.1.call-start = ((), (), s32[]{:S(2)}) async-start(), calls=%async_computation.36 | async-start | bytes 12255232 | tf_op jit(solution)/shard_map/reduce_scatter | solution.py:367
  1505.0 1120.3 %reduce-scatter.32.cloned.1.call-start = ((), (), s32[]{:S(2)}) async-start(), calls=%async_computation.37 | async-start | bytes 12255232 | tf_op jit(solution)/shard_map/reduce_scatter | solution.py:372
  1513.1 1292.7 %reduce-scatter.16.cloned.1.call-start = ((), (), s32[]{:S(2)}) async-start(), calls=%async_computation.29 | async-start | bytes 8912896 | tf_op jit(solution)/shard_map/reduce_scatter | solution.py:365
  1518.8 1469.7 %reduce-scatter.18.cloned.1.call-start = ((), (), s32[]{:S(2)}) async-start(), calls=%async_computation.30 | async-start | bytes 8912896 | tf_op jit(solution)/shard_map/reduce_scatter | solution.py:371
  1524.4 1646.9 %reduce-scatter.14.cloned.1.call-start = ((), (), s32[]{:S(2)}) async-start(), calls=%async_computation.28 | async-start | bytes 8912896 | tf_op jit(solution)/shard_map/reduce_scatter | solution.py:364
  1529.1 1824.9 %reduce-scatter.12.cloned.1.call-start = ((), (), s32[]{:S(2)}) async-start(), calls=%async_computation.27 | async-start | bytes 8912896 | tf_op jit(solution)/shard_map/reduce_scatter | solution.py:363
  (46 other events, 2185.5 us)
Sparse Core Ops, SparseCore 0:
  11.6 76.0 all-gather.14
  90.4 74.1 all-gather.16
  167.4 74.1 all-gather.12
  244.2 86.8 all-gather.18
  335.1 18.7 all-reduce.7
  1409.1 20.4 all-reduce.9
  1455.3 20.6 all-reduce.11
Sparse Core Ops, SparseCore 1:
  337.3 112.5 all-gather.26
  451.6 113.4 all-gather.28
  566.7 113.4 all-gather.30
  682.9 197.5 all-gather.20
  883.3 90.5 all-gather.22
  981.4 201.6 all-gather.24
  1466.7 112.8 reduce-scatter.25
  1582.5 112.8 reduce-scatter.21
  1698.3 111.9 reduce-scatter.23
  1813.1 72.4 reduce-scatter.19
  1888.3 244.3 reduce-scatter.27
  2135.6 243.4 reduce-scatter.29
  2381.8 243.4 reduce-scatter.31
  2628.2 177.6 reduce-scatter.15
  2808.7 179.8 reduce-scatter.17
  2991.4 179.8 reduce-scatter.13
  3174.2 179.8 reduce-scatter.11
where the time goes:
time: 3370 us; the launch traced here: 3360 us
  waiting for transfers between devices  2550 us (76%)
  blocking collectives  358 us (11%)
  matrix products  216 us (6%)
  local copies, waits for them, and re-layouts  123 us (4%)
  other arithmetic  57.7 us (2%)
  starting transfers between devices  36.7 us (1%)
    all_to_all x2, waiting for transfers between devices, send_out(): lax.all_to_all(flat_rows.reshape(experts_here, owners, cap_rows, model_wi...  329 us
    reduce_scatter x1, waiting for transfers between devices, body(): lax.psum_scatter(sgate_full, ('dp', 'expert'), scatter_dimension=0, tiled...  247 us
    reduce_scatter x1, waiting for transfers between devices, body(): lax.psum_scatter(sup_full, ('dp', 'expert'), scatter_dimension=0, tiled=T...  246 us
    reduce_scatter x1, waiting for transfers between devices, body(): lax.psum_scatter(sdown_full, ('dp', 'expert'), scatter_dimension=1, tiled...  246 us
    all_gather x1, blocking collectives, body(): lax.all_gather(router_weight, ('dp', 'expert'), axis=0, tiled=True)  212 us
    reduce_scatter x1, waiting for transfers between devices, body(): lax.psum_scatter(output_full, ('dp', 'expert'), scatter_dimension=1, tile...  183 us
    reduce_scatter x1, waiting for transfers between devices, body(): lax.psum_scatter(query_full, ('dp', 'expert'), scatter_dimension=0, tiled...  183 us
    reduce_scatter x1, waiting for transfers between devices, body(): lax.psum_scatter(key_full, ('dp', 'expert'), scatter_dimension=0, tiled=T...  183 us
  transfers between devices with their start and end apart: 28, of which 20 were waited for; matrix products, arithmetic and copies ran while one was open for 10% of the time, Pallas kernels for 0%

commit v1 on v0

v1 whole, which is shorter than its diff:
```python
import functools
import math

import jax
import jax.numpy as jnp
from jax import lax
from jax.experimental import pallas as pl
from jax.experimental.pallas import tpu as pltpu
from jax.sharding import PartitionSpec as P

MESH = pl.DeviceIdType.MESH
F32 = jnp.float32

D = 2048
HD = 128
TOPK = 6


epsilon = 1e-06
rope_base = 10000.0
scatter_order = (46, 68, 63, 64, 18, 10, 11, 84, 88, 89, 19, 54, 9, 74, 45, 36, 38, 73, 70, 20, 83, 90, 28, 55, 37, 12, 48, 30, 65, 56, 78, 27, 47, 66, 39, 79, 91, 14, 0, 29, 13, 76, 69, 1, 21, 41, 16, 57, 75, 40, 49, 86, 3, 71, 58, 23, 43, 2, 92, 31, 42, 85, 67, 51, 32, 59, 77, 22, 25, 50, 33, 87, 5, 44, 61, 4, 15, 60, 24, 52, 34, 80, 81, 6, 17, 26, 72, 53, 62, 35, 7, 82, 8)
gather_starts = (2.97, 4.29, 2.32, 3.19, 2.3, 2.4, 5.08, 6.72, 5.91, 6.5, 6.76, 5.24)
masked_score = -1e30


class Leaf:
    def __init__(self, shape, dtype, form, first, n):
        self.shape, self.dtype, self.form, self.first, self.n = shape, dtype, form, first, n
        rows = shape[-2]
        if form == "rows":
            self.out = (4 * n * rows, shape[1])
        elif form == "cols":
            self.out = (shape[0], 4 * n * shape[1])
        elif form == "expert":
            self.out = (shape[0], shape[1], 4 * shape[2])
        elif form == "tokens":
            self.out = (n * rows, shape[1])

    def view(self, ref, d, e, half=None):
        if self.form == "rows":
            r = self.shape[0]
            s, k = (d * self.n + e) * r, r
            if half is not None:
                k = r // 2
                s = s + half * k
            return ref.at[pl.ds(pl.multiple_of(s, k), k), :]
        if self.form == "cols":
            c = self.shape[1]
            s = pl.multiple_of((d * self.n + e) * c, c)
            k = self.shape[0] // 2
            rows = slice(None) if half is None else pl.ds(half * k, k)
            return ref.at[rows, pl.ds(s, c)]
        if self.form == "tokens":
            r = self.shape[0]
            s = pl.multiple_of(e * r, r)
            if half is None:
                return ref.at[pl.ds(s, r), :]
            c = self.shape[1] // 2
            return ref.at[pl.ds(s, r), pl.ds(pl.multiple_of(half * c, c), c)]
        c = self.shape[2]
        k = self.shape[0] // 2
        heads = slice(None) if half is None else pl.ds(half * k, k)
        return ref.at[heads, :, pl.ds(pl.multiple_of(d * c, c), c)]

    def own(self, ref, half=None):
        if half is None:
            return ref
        if self.form == "tokens":
            c = self.shape[1] // 2
            return ref.at[:, pl.ds(pl.multiple_of(half * c, c), c)]
        k = self.shape[0] // 2
        return ref.at[pl.ds(half * k, k)]


def gather_kernel(leaves, n, starts, *refs):
    m = len(leaves)
    ins, outs = refs[:m], refs[m : 2 * m]
    stages = refs[2 * m : 3 * m]
    in_sem, out_sem, send_sem, recv_sem = refs[3 * m :]
    d, e, t = lax.axis_index("dp"), lax.axis_index("expert"), lax.axis_index("tensor")
    dx = d + 1 - 2 * lax.rem(d, 2)
    dy = lax.rem(d + 2, 4)
    dd = lax.rem(dx + 2, 4)
    near = {"x": {"dp": dx}, "y": {"dp": dy}, "r": {"expert": e + 1}, "l": {"expert": e - 1},
            "c": {"tensor": 1 - t}}
    has = {"r": e < n - 1, "l": e > 0}

    barrier = pltpu.get_barrier_semaphore()
    for side in ("x", "y", "c"):
        pl.semaphore_signal(barrier, inc=1, device_id=near[side], device_id_type=MESH)
    for side in ("r", "l"):
        @pl.when(has[side])
        def _():
            pl.semaphore_signal(barrier, inc=1, device_id=near[side], device_id_type=MESH)
    pl.semaphore_wait(barrier, 3 + has["r"].astype(jnp.int32) + has["l"].astype(jnp.int32))

    for i in range(m):
        pltpu.make_async_copy(ins[i], stages[i], in_sem.at[i]).start()

    count = [0]
    table = {}

    def slot(key):
        if key not in table:
            table[key] = len(table)
        return table[key]

    def copy(src, dst, side, key):
        k = slot(key)
        return pltpu.make_async_remote_copy(
            src_ref=src, dst_ref=dst, send_sem=send_sem.at[k], recv_sem=recv_sem.at[k],
            device_id=near[side], device_id_type=MESH)

    sends = []

    def send(i, dd_, ee_, half, side, key, own=False, cond=None):
        leaf = leaves[i]
        dst = leaf.view(outs[i], dd_, ee_, half)
        src = leaf.own(ins[i], half) if own else dst
        c = copy(src, dst, side, key)
        if cond is None:
            c.start()
        else:
            pl.when(cond)(c.start)
        sends.append((c, cond))

    def arrive(i, dd_, ee_, half, key, cond=None):
        leaf = leaves[i]
        dst = leaf.view(outs[i], dd_, ee_, half)
        c = copy(dst, dst, "x", key)
        if cond is None:
            c.wait_recv()
        else:
            pl.when(cond)(c.wait_recv)

    work = []

    def plane(i, ee_, at, tag, cond, own):
        def s0():
            for half, side in ((0, "x"), (1, "y"), (1, "x"), (0, "y")):
                send(i, d, ee_, half, side, (i, tag, half, side), own=own, cond=cond)
        def s1():
            arrive(i, dx, ee_, 0, (i, tag, 0, "x"), cond)
            send(i, dx, ee_, 0, "y", (i, tag, 0, "fy"), cond=cond)
            arrive(i, dy, ee_, 1, (i, tag, 1, "y"), cond)
            send(i, dy, ee_, 1, "x", (i, tag, 1, "fx"), cond=cond)
        def s2():
            arrive(i, dx, ee_, 1, (i, tag, 1, "x"), cond)
            arrive(i, dy, ee_, 0, (i, tag, 0, "y"), cond)
        def s3():
            arrive(i, dd, ee_, 0, (i, tag, 0, "fy"), cond)
            arrive(i, dd, ee_, 1, (i, tag, 1, "fx"), cond)
        for k, f in enumerate((s0, s1, s2, s3)):
            work.append((at + k, f))

    def line(i, dd_, at, tag, own, then=None):
        def s0():
            for side in ("r", "l"):
                send(i, dd_, e, None, side, (i, tag, side, 1), own=own, cond=has[side])
        work.append((at, s0))
        for k in range(1, n):
            def step(k=k):
                for side, o, there in (("r", e - k, e >= k), ("l", e + k, e + k < n)):
                    arrive(i, dd_, o, None, (i, tag, side, k), there)
                    if k < n - 1:
                        go = jnp.logical_and(there, has[side])
                        send(i, dd_, o, None, side, (i, tag, side, k + 1), cond=go)
            work.append((at + k, step))

    def tokens(i, at):
        def s0():
            for side in ("r", "l"):
                send(i, d, e, t, side, (i, side, 1), own=True, cond=has[side])
        work.append((at, s0))
        for k in range(1, n):
            def step(k=k):
                for side, o, there in (("r", e - k, e >= k), ("l", e + k, e + k < n)):
                    arrive(i, d, o, t, (i, side, k), there)
                    if k < n - 1:
                        go = jnp.logical_and(there, has[side])
                        send(i, d, o, t, side, (i, side, k + 1), cond=go)
                    send(i, d, o, t, "c", (i, "c", side, k), cond=there)
            def last(k=k):
                for side, o, there in (("r", e - k, e >= k), ("l", e + k, e + k < n)):
                    arrive(i, d, o, 1 - t, (i, "c", side, k), there)
            work.append((at + k, step))
            work.append((at + k + 1, last))

    for i, leaf in enumerate(leaves):
        at = starts[i]
        if leaf.form == "tokens":
            tokens(i, at)
            continue
        if leaf.form == "expert":
            plane(i, 0, at, "p", None, True)
        elif leaf.first == "xy":
            plane(i, e, at, "p", None, True)
            line(i, d, at, "z0", True)
            line(i, dx, at + 2.2, "zx", False)
            line(i, dy, at + 2.2, "zy", False)
            line(i, dd, at + 3.2, "zd", False)
        else:
            plane(i, e, at, "p", None, True)
            line(i, d, at, "z0", True)
            for k in range(1, n):
                plane(i, e - k, at + k + 0.5, ("pr", k), e >= k, False)
                plane(i, e + k, at + k + 0.5, ("pl", k), e + k < n, False)

    def settle():
        for i in range(m):
            pltpu.make_async_copy(ins[i], stages[i], in_sem.at[i]).wait()
            pltpu.make_async_copy(stages[i], leaves[i].view(outs[i], d, e), out_sem.at[i]).start()
    work.append((1.2, settle))
    for _, f in sorted(work, key=lambda w: w[0]):
        f()
    for c, cond in sends:
        if cond is None:
            c.wait_send()
        else:
            pl.when(cond)(c.wait_send)
    for i in range(m):
        pltpu.make_async_copy(stages[i], leaves[i].view(outs[i], d, e), out_sem.at[i]).wait()
    assert len(table) <= recv_sem.shape[0], len(table)


def gather(arrays, forms, firsts, n, starts):
    leaves = [Leaf(a.shape, a.dtype, f, o, n) for a, f, o in zip(arrays, forms, firsts)]
    total = 0
    for leaf in leaves:
        plane, line = 6, 2 * (n - 1)
        if leaf.form == "tokens":
            total += 2 * line
            continue
        total += plane if leaf.form == "expert" else plane + 4 * line if leaf.first == "xy" else plane * (2 * n - 1) + line
    m = len(leaves)
    anyspace = pl.BlockSpec(memory_space=pl.ANY)
    return pl.pallas_call(
        functools.partial(gather_kernel, leaves, n, starts),
        out_shape=[jax.ShapeDtypeStruct(leaf.out, leaf.dtype) for leaf in leaves],
        in_specs=[anyspace] * m,
        out_specs=[anyspace] * m,
        scratch_shapes=[pltpu.VMEM(leaf.shape, leaf.dtype) for leaf in leaves] + [
            pltpu.SemaphoreType.DMA((m,)), pltpu.SemaphoreType.DMA((m,)),
            pltpu.SemaphoreType.DMA((total,)), pltpu.SemaphoreType.DMA((total,))],
        compiler_params=pltpu.CompilerParams(
            collective_id=0, has_side_effects=True, vmem_limit_bytes=40 << 20),
    )(*arrays)


message_rows = 5632
ring_slots = {"x": 3, "y": 3, "z": 4}


def scatter_items(dense, units, n):
    ends = [k // 2 if k % 2 == 0 else n - 1 - k // 2 for k in range(n)]
    items = []
    for i, (_, first) in enumerate(dense):
        names = [("z", t) for t in ends] if first == "z" else []
        names += [("p", s) for s in ("y1", "x1", "x2", "y2")]
        names += [("z", t) for t in ends] if first != "z" else []
        items += [("d", i) + name for name in names] + [("d", i, "out", 0)]
    for u in range(units):
        items += [("e", u, "p", s) for s in ("y1", "x1", "x2", "y2")] + [("e", u, "out", 0)]
    return items


def scatter_kernel(dense, units, n, order, *refs):
    m = len(dense)
    lefts, rights = refs[:m], refs[m : 2 * m]
    exp_left = refs[2 * m : 2 * m + 3]
    rows_all, grads_in = refs[2 * m + 3 : 2 * m + 5]
    refs = refs[2 * m + 5 :]
    outs, refs = refs[: m + 3], refs[m + 3 :]
    landed, refs = refs[: 3 * m + 2], refs[3 * m + 2 :]
    bufs = dict(zip("xyz", refs[:3]))
    held, tall, wide = refs[3:6]
    stage_sem, load_sem, recv_sem = refs[6:9]
    send_sems = dict(zip("xyz", refs[9:12]))
    d, e = lax.axis_index("dp"), lax.axis_index("expert")
    dx = d + 1 - 2 * lax.rem(d, 2)
    dy = lax.rem(d + 2, 4)
    dd = lax.rem(dx + 2, 4)
    after, before = e < n - 1, e > 0

    barrier = pltpu.get_barrier_semaphore()
    for dev in ({"dp": dx}, {"dp": dy}):
        pl.semaphore_signal(barrier, inc=1, device_id=dev, device_id_type=MESH)
    for cond, dev in ((after, {"expert": e + 1}), (before, {"expert": e - 1})):
        @pl.when(cond)
        def _():
            pl.semaphore_signal(barrier, inc=1, device_id=dev, device_id_type=MESH)
    pl.semaphore_wait(barrier, 2 + after.astype(jnp.int32) + before.astype(jnp.int32))
    held[...] = jnp.zeros_like(held)

    def when(cond, f):
        if cond is None:
            f()
        else:
            pl.when(cond)(f)

    sems = {}

    def sem_of(key, count=1):
        if key not in sems:
            sems[key] = sum(c for _, c in sems.values()), count
        return sems[key][0]

    turns = {"x": 0, "y": 0, "z": 0}
    pending = {}

    def slot(side):
        k = turns[side] % ring_slots[side]
        turns[side] += 1
        if (side, k) in pending:
            c, cond = pending.pop((side, k))
            when(cond, c.wait_send)
        return k

    def send(side, k, rows, dst, sem, dev, cond=None):
        c = pltpu.make_async_remote_copy(
            src_ref=bufs[side].at[k, pl.ds(0, rows)], dst_ref=dst,
            send_sem=send_sems[side].at[k], recv_sem=recv_sem.at[sem],
            device_id=dev, device_id_type=MESH)
        when(cond, c.start)
        pending[(side, k)] = (c, cond)

    seen = set()

    def arrived(key, view, sem, cond=None):
        if key in seen:
            return
        seen.add(key)
        c = pltpu.make_async_remote_copy(
            src_ref=view, dst_ref=view, send_sem=recv_sem.at[sem], recv_sem=recv_sem.at[sem],
            device_id={"dp": dx}, device_id_type=MESH)
        when(cond, c.wait_recv)

    class Loads:
        def __init__(self):
            self.list = []

        def add(self, src, k, off, cond=None):
            rows = src.shape[0]
            c = pltpu.make_async_copy(src, held.at[k, pl.ds(off, rows)], load_sem.at[len(self.list)])
            when(cond, c.start)
            self.list.append((c, cond))

        def wait(self):
            for c, cond in self.list:
                when(cond, c.wait)

    def dense_piece(i, d_, e_, half, put):
        kind = dense[i][0]
        block = d_ * n + e_
        if kind == "rows":
            width = rights[i].shape[1]
            r = lefts[i].shape[0] // (4 * n)
            left = lefts[i][pl.ds(pl.multiple_of(block * r + half * (r // 2), r // 2), r // 2), :]
            for c in range(0, width, 256):
                w = min(256, width - c)
                res = jnp.dot(left, rights[i][:, c : c + w], preferred_element_type=F32)
                for k in range(0, w, 128):
                    put((c + k) // 128 * (r // 2), res[:, k : k + 128], c + k)
        else:
            half_rows = lefts[i].shape[0] // 2
            right = rights[i][:, pl.ds(pl.multiple_of(block * 128, 128), 128)]
            step = half_rows // 2
            for r in range(0, half_rows, step):
                left = lefts[i][pl.ds(pl.multiple_of(half * half_rows + r, 16), step), :]
                put(r, jnp.dot(left, right, preferred_element_type=F32), 0)

    def half_rows_of(i):
        if dense[i][0] == "rows":
            return lefts[i].shape[0] // (8 * n) * rights[i].shape[1] // 128
        return lefts[i].shape[0] // 2

    def total(value, row, adds):
        rows = value.shape[0]
        for k, off, flag in adds:
            more = held[k, pl.ds(pl.multiple_of(off + row, 16), rows), :].astype(F32)
            value = value + (more if flag is None else jnp.where(flag, more, 0.0))
        return value

    def into(side, k, base, adds):
        def put(row, value, col):
            value = total(value, row, adds)
            start = pl.multiple_of(base + row, 16)
            bufs[side][k, pl.ds(start, value.shape[0]), :] = value.astype(jnp.bfloat16)
        return put

    out_busy = {}

    def out_wait(which):
        if which in out_busy:
            out_busy.pop(which).wait()

    def dense_step(i, stage, arg):
        z_land, first_land, second_land = landed[3 * i : 3 * i + 3]
        z_first = dense[i][1] == "z"
        hb = half_rows_of(i)
        z_rows = (8 if z_first else 2) * hb
        z_sem = sem_of(("z", i), 2 * n)
        groups = 1 if z_first else n
        p_sem = {s: sem_of((s, i)) for s in ("y1", "x1", "x2", "y2")}
        place = {"y1": (first_land, 0, 2), "x1": (first_land, 1, 2), "x2": (second_land, 0, 1), "y2": (second_land, 1, 1)}

        def view(s, g0, gs, sub):
            land, which, pieces = place[s]
            if sub is None:
                return land.at[which, pl.ds(0, groups * pieces * hb)]
            return land.at[which, pl.ds(pl.multiple_of((g0 * pieces + sub) * hb, hb), gs * hb)]

        def plane_arrived(s):
            arrived((s, i), view(s, 0, 0, None), p_sem[s])

        def own_line(ld, k, off, d_, half, rows):
            for side, there in ((0, after), (1, before)):
                arrived(("own", i, side), z_land.at[side, e], z_sem + side * n + e, there)
                src = z_land.at[side, e, pl.ds(pl.multiple_of((2 * d_ + half) * hb, hb), rows)]
                ld.add(src, k + side, off, there)

        def plane_out(ld, g):
            for s in ("y1", "x1", "x2", "y2"):
                plane_arrived(s)
            ld.add(view("y1", g, 1, 1), 2, 0)
            ld.add(view("x1", g, 1, 1), 2, hb)
            ld.add(view("x2", g, 1, 0), 3, 0)
            ld.add(view("y2", g, 1, 0), 3, hb)

        if stage == "z":
            t = arg
            side = 1 - (e + n - t) // n
            more = jnp.logical_or(jnp.logical_and(e > t, after), jnp.logical_and(e < t, before))
            cond = e != t
            k = slot("z")
            def go():
                ld = Loads()
                land = z_land.at[side, t]
                arrived(("pass", i, t), land, z_sem + side * n + t, more)
                ld.add(land, 0, 0, more)
                if not z_first:
                    plane_out(ld, t)
                ld.wait()
                if z_first:
                    def one(h, _):
                        dense_piece(i, h // 2, t, h % 2, into("z", k, h * hb, [(0, h * hb, more)]))
                        return 0
                    lax.fori_loop(0, 8, one, 0)
                else:
                    def one(h, _):
                        dense_piece(i, d, t, h, into("z", k, h * hb, [(0, h * hb, more), (2, h * hb, None), (3, h * hb, None)]))
                        return 0
                    lax.fori_loop(0, 2, one, 0)
            if not z_first:
                for s in ("y1", "x1", "x2", "y2"):
                    plane_arrived(s)
            pl.when(cond)(go)
            send("z", k, z_rows, z_land.at[side, t], z_sem + side * n + t, {"expert": e - 1 + 2 * side}, cond)
        elif stage == "p":
            s = arg
            link = s[0]
            dev = {"dp": dy if link == "y" else dx}
            half = 0 if s in ("y1", "x2") else 1
            k = slot(link)
            ld = Loads()
            if s in ("y1", "x1"):
                owners = (dd, dy if link == "y" else dx)
                if z_first:
                    for q, o in enumerate(owners):
                        own_line(ld, 0, q * hb, o, half, hb)
                    ld.wait()
                    for q, o in enumerate(owners):
                        dense_piece(i, o, e, half, into(link, k, q * hb, [(0, q * hb, after), (1, q * hb, before)]))
                else:
                    def one(g, _):
                        for q, o in enumerate(owners):
                            dense_piece(i, o, g, half, into(link, k, (2 * g + q) * hb, []))
                        return 0
                    lax.fori_loop(0, n, one, 0)
                send(link, k, groups * 2 * hb, view(s, 0, 0, None), p_sem[s], dev)
            else:
                o = dx if link == "x" else dy
                prior = "y1" if s == "x2" else "x1"
                plane_arrived(prior)
                if z_first:
                    own_line(ld, 0, 0, o, half, hb)
                    ld.add(view(prior, 0, 1, 0), 2, 0)
                    ld.wait()
                    dense_piece(i, o, e, half, into(link, k, 0, [(0, 0, after), (1, 0, before), (2, 0, None)]))
                else:
                    ld.add(view(prior, 0, 0, None), 2, 0)
                    ld.wait()
                    def one(g, _):
                        dense_piece(i, o, g, half, into(link, k, g * hb, [(2, 2 * g * hb, None)]))
                        return 0
                    lax.fori_loop(0, n, one, 0)
                send(link, k, groups * hb, view(s, 0, 0, None), p_sem[s], dev)
        else:
            ld = Loads()
            if z_first:
                own_line(ld, 0, 0, d, 0, 2 * hb)
                plane_out(ld, 0)
            else:
                for side, there in ((0, after), (1, before)):
                    arrived(("own", i, side), z_land.at[side, e], z_sem + side * n + e, there)
                    ld.add(z_land.at[side, e], side, 0, there)
                plane_out(ld, e)
            rows = dense[i][0] == "rows"
            which = "wide" if rows else "tall"
            out_wait(which)
            ld.wait()
            def one(h, _):
                adds = [(0, h * hb, after), (1, h * hb, before), (2, h * hb, None), (3, h * hb, None)]
                def put(row, value, col):
                    value = total(value, row, adds)
                    if rows:
                        r = value.shape[0]
                        wide[pl.ds(pl.multiple_of(h * r, r), r), col : col + 128] = value
                    else:
                        tall[0, pl.ds(pl.multiple_of(h * hb + row, 16), value.shape[0]), 0:128] = value
                dense_piece(i, d, e, h, put)
                return 0
            lax.fori_loop(0, 2, one, 0)
            if rows:
                src = wide.at[:, pl.ds(0, outs[i].shape[1])]
            else:
                src = tall.at[0, pl.ds(0, outs[i].shape[0]), pl.ds(0, 128)]
            c = pltpu.make_async_copy(src, outs[i], stage_sem.at[0 if rows else 1])
            c.start()
            out_busy[which] = c

    first_exp, second_exp = landed[3 * m], landed[3 * m + 1]

    def expert_step(u, stage, s):
        a, q = u // 2, u % 2
        rows, width = exp_left[a].shape[1], outs[m + a].shape[2]
        tiles = width // 128
        piece = rows * tiles
        step = rows // 4
        sem = {s_: sem_of((s_, "e", u)) for s_ in ("y1", "x1", "x2", "y2")}
        place = {"y1": (first_exp, 0, 2), "x1": (first_exp, 1, 2), "x2": (second_exp, 0, 1), "y2": (second_exp, 1, 1)}

        def view(s_, sub=None):
            land, which, pieces = place[s_]
            if sub is None:
                return land.at[u, which]
            return land.at[u, which, pl.ds(sub * piece, piece)]

        def one_piece(j, d_, put):
            def body(r, _):
                left = exp_left[a][j, pl.ds(pl.multiple_of(r * step, 16), step), :]
                cols = pl.ds(pl.multiple_of(d_ * width, 128), width)
                right = grads_in[j, :, cols] if a == 2 else rows_all[:, cols]
                res = jnp.dot(left, right, preferred_element_type=F32)
                for c in range(tiles):
                    put(c * rows + r * step, res[:, c * 128 : (c + 1) * 128], (r * step, c * 128))
                return 0
            lax.fori_loop(0, 4, body, 0)

        def get(s_):
            arrived((s_, "e", u), view(s_), sem[s_])

        ld = Loads()
        if stage == "p":
            link = s[0]
            dev = {"dp": dy if link == "y" else dx}
            j = q if s in ("y1", "x2") else q + 2
            k = slot(link)
            if s in ("y1", "x1"):
                for b, o in enumerate((dd, dy if link == "y" else dx)):
                    one_piece(j, o, into(link, k, b * piece, []))
                send(link, k, 2 * piece, view(s), sem[s], dev)
            else:
                prior = "y1" if s == "x2" else "x1"
                get(prior)
                ld.add(view(prior, 0), 0, 0)
                ld.wait()
                one_piece(j, dx if link == "x" else dy, into(link, k, 0, [(0, 0, None)]))
                send(link, k, piece, view(s), sem[s], dev)
        else:
            for b, (j, one, two) in enumerate(((q, "y1", "x2"), (q + 2, "x1", "y2"))):
                get(one)
                get(two)
                ld.add(view(one, 1), 2 * b, 0)
                ld.add(view(two, 0), 2 * b + 1, 0)
            out_wait("tall")
            ld.wait()
            for b, j in enumerate((q, q + 2)):
                adds = [(2 * b, 0, None), (2 * b + 1, 0, None)]
                def put(row, value, at):
                    value = total(value, row, adds)
                    r, c = at
                    tall[b, pl.ds(pl.multiple_of(r, 16), value.shape[0]), c : c + 128] = value
                one_piece(j, d, put)
            cs = [pltpu.make_async_copy(tall.at[b, pl.ds(0, rows), pl.ds(0, width)], outs[m + a].at[q + 2 * b], stage_sem.at[1 + b]) for b in range(2)]
            for c in cs:
                c.start()
            class Both:
                def wait(self):
                    for c in cs:
                        c.wait()
            out_busy["tall"] = Both()

    items = scatter_items(dense, units, n)
    for kind, i, stage, arg in [items[k] for k in order] if order else items:
        (dense_step if kind == "d" else expert_step)(i, stage, arg)
    for c, cond in pending.values():
        when(cond, c.wait_send)
    for which in list(out_busy):
        out_wait(which)
    assert sum(c for _, c in sems.values()) <= recv_sem.shape[0]


def scatter(dense, lefts, rights, exp_left, rows_all, grads_in, n, order, cid):
    m, units = len(dense), 6
    bf = jnp.bfloat16
    outs, landed = [], []
    for (kind, first), a, b in zip(dense, lefts, rights):
        if kind == "rows":
            r = a.shape[0] // (4 * n)
            shape, hb = (r, b.shape[1]), r // 2 * b.shape[1] // 128
        else:
            shape, hb = (a.shape[0], 128), a.shape[0] // 2
        outs.append(jax.ShapeDtypeStruct(shape, F32))
        g, z = (1, 8) if first == "z" else (n, 2)
        landed += [jax.ShapeDtypeStruct((2, n, z * hb, 128), bf),
                   jax.ShapeDtypeStruct((2, g * 2 * hb, 128), bf),
                   jax.ShapeDtypeStruct((2, g * hb, 128), bf)]
    here, rows = exp_left[0].shape[:2]
    width = rows_all.shape[1] // 4
    outs += [jax.ShapeDtypeStruct((here, rows, width), F32)] * 3
    piece = rows * width // 128
    landed += [jax.ShapeDtypeStruct((units, 2, 2 * piece, 128), bf),
               jax.ShapeDtypeStruct((units, 2, piece, 128), bf)]
    anyspace, vmem = pl.BlockSpec(memory_space=pl.ANY), pl.BlockSpec(memory_space=pltpu.VMEM)
    count = m * (2 * n + 4) + 4 * units
    res = pl.pallas_call(
        functools.partial(scatter_kernel, dense, units, n, order),
        out_shape=outs + landed,
        in_specs=[vmem] * (2 * m + 5),
        out_specs=[anyspace] * (len(outs) + len(landed)),
        scratch_shapes=[pltpu.VMEM((ring_slots[s], message_rows, 128), bf) for s in "xyz"] + [
            pltpu.VMEM((4, message_rows, 128), bf),
            pltpu.VMEM((2, max(rows, max(o.shape[0] for o in outs[:m])), width), F32),
            pltpu.VMEM((128, max(o.shape[1] for o in outs[:m])), F32),
            pltpu.SemaphoreType.DMA((3,)), pltpu.SemaphoreType.DMA((8,)),
            pltpu.SemaphoreType.DMA((count,)),
        ] + [pltpu.SemaphoreType.DMA((ring_slots[s],)) for s in "xyz"],
        compiler_params=pltpu.CompilerParams(
            collective_id=cid, has_side_effects=True, vmem_limit_bytes=60 << 20),
    )(*lefts, *rights, *exp_left, rows_all, grads_in)
    return res[: m + 3]


def rms_scale(vector):
    return lax.rsqrt(jnp.mean(vector * vector, axis=-1, keepdims=True) + epsilon)


def rope_tables(count, width):
    half_width = width // 2
    frequency = rope_base ** (-jnp.arange(half_width, dtype=jnp.float32) / half_width)
    angles = jnp.arange(count, dtype=jnp.float32)[:, None] * frequency[None, :]
    return (jnp.cos(angles)[:, None, :], jnp.sin(angles)[:, None, :])


def rotate(vector, cosine, sine_table):
    half_width = vector.shape[-1] // 2
    first_half = vector[..., :half_width]
    second_half = vector[..., half_width:]
    return jnp.concatenate(
        [
            first_half * cosine - second_half * sine_table,
            first_half * sine_table + second_half * cosine,
        ],
        axis=-1,
    )


def unrotate(vector, cosine, sine_table):
    half_width = vector.shape[-1] // 2
    first_half = vector[..., :half_width]
    second_half = vector[..., half_width:]
    return jnp.concatenate(
        [
            first_half * cosine + second_half * sine_table,
            second_half * cosine - first_half * sine_table,
        ],
        axis=-1,
    )


def dots(left, right, *dims):
    return lax.dot_general(left, right, dims, preferred_element_type=F32)


def silu_parts(before):
    sigmoid_val = jax.nn.sigmoid(before)
    return (before * sigmoid_val, sigmoid_val * (1.0 + before * (1.0 - sigmoid_val)))


def masked_scores(query_rot, key_rot, allowed):
    scores = dots(query_rot, key_rot, ((2,), (2,)), ((1,), (1,))) / math.sqrt(query_rot.shape[-1])
    return jnp.where(allowed[None], scores, masked_score)


def body(
    block_input,
    attn_gain,
    query_weight,
    key_weight,
    value_weight,
    output_weight,
    ffn_gain,
    router_weight,
    expert_gate,
    expert_up,
    expert_down,
    shared_gate,
    shared_up,
    shared_down,
    segments,
    routes,
    cotangent,
):
    both = ("dp", "expert")
    small = jnp.concatenate([router_weight, attn_gain[:, None], ffn_gain[:, None]], axis=1).T
    flip_gate, flip_up = jnp.swapaxes(expert_gate, 1, 2), jnp.swapaxes(expert_up, 1, 2)
    kernels = output_weight.shape[1] % 128 == 0 and lax.axis_size("dp") == 4
    if kernels:
        small = jnp.pad(small, ((0, -small.shape[0] % 32), (0, 0)))
        arrays = (query_weight, key_weight, value_weight, output_weight, small, cotangent,
                  shared_gate, shared_up, shared_down, flip_gate, flip_up, expert_down)
        forms = ("rows",) * 3 + ("cols", "cols", "tokens", "rows", "rows", "cols") + ("expert",) * 3
        firsts = ("xy",) * 7 + ("z",) * 2 + ("xy",) * 3
        (full_query, full_key, full_value, full_output, full_small, grads_all,
         full_sgate, full_sup, full_sdown, local_gate, local_up, local_down) = gather(
            arrays, forms, firsts, lax.axis_size("expert"), gather_starts)
    else:
        full_small = lax.all_gather(small, both, axis=1, tiled=True)
        full_query = lax.all_gather(query_weight, both, axis=0, tiled=True)
        full_key = lax.all_gather(key_weight, both, axis=0, tiled=True)
        full_value = lax.all_gather(value_weight, both, axis=0, tiled=True)
        full_output = lax.all_gather(output_weight, both, axis=1, tiled=True)
        full_sgate = lax.all_gather(shared_gate, both, axis=0, tiled=True)
        full_sup = lax.all_gather(shared_up, both, axis=0, tiled=True)
        full_sdown = lax.all_gather(shared_down, both, axis=1, tiled=True)
        grads_all = lax.all_gather(cotangent, "expert", axis=0, tiled=True)
        local_gate = lax.all_gather(flip_gate, "dp", axis=2, tiled=True)
        local_up = lax.all_gather(flip_up, "dp", axis=2, tiled=True)
        local_down = lax.all_gather(expert_down, "dp", axis=2, tiled=True)
    seq_len = block_input.shape[0]
    total_experts = router_weight.shape[1]
    experts_here = expert_gate.shape[0]
    owners = lax.axis_size("expert")
    here = lax.axis_index("expert")
    all_rows = owners * seq_len
    router_rows = full_small[:total_experts]
    gain_attn = full_small[total_experts]
    gain_ffn = full_small[total_experts + 1]
    routes_all = lax.all_gather(routes, "expert", axis=0, tiled=True)
    heads_here = full_query.shape[1] // HD
    gain_one = gain_attn.astype(jnp.float32)
    gain_two = gain_ffn.astype(jnp.float32)
    input_f = block_input.astype(jnp.float32)
    scale_one = rms_scale(input_f)
    normed_one = (input_f * scale_one * gain_one).astype(jnp.bfloat16)
    cosine, sine_table = rope_tables(seq_len, HD)
    query_pre = jnp.dot(normed_one, full_query, preferred_element_type=jnp.float32).reshape(
        seq_len, heads_here, HD
    )
    key_pre = jnp.dot(normed_one, full_key, preferred_element_type=jnp.float32).reshape(
        seq_len, heads_here, HD
    )
    query_rot = rotate(query_pre, cosine, sine_table).astype(jnp.bfloat16)
    key_rot = rotate(key_pre, cosine, sine_table).astype(jnp.bfloat16)
    value_rows = (
        jnp.dot(normed_one, full_value, preferred_element_type=jnp.float32)
        .astype(jnp.bfloat16)
        .reshape(seq_len, heads_here, HD)
    )
    position = jnp.arange(seq_len)
    segment_row = segments[0]
    allowed = (position[:, None] >= position[None, :]) & (
        segment_row[:, None] == segment_row[None, :]
    )
    scores = masked_scores(query_rot, key_rot, allowed)
    top_score = jnp.max(scores, axis=-1, keepdims=True)
    shifted = jnp.exp(scores - top_score)
    row_total = jnp.sum(shifted, axis=-1, keepdims=True)
    log_total = top_score + jnp.log(row_total)
    prob_low = (shifted / row_total).astype(jnp.bfloat16)
    mixed_rows = (
        jnp.transpose(dots(prob_low, value_rows, ((2,), (0,)), ((0,), (1,))), (1, 0, 2))
        .astype(jnp.bfloat16)
        .reshape(seq_len, heads_here * HD)
    )
    attn_part = jnp.dot(mixed_rows, full_output, preferred_element_type=jnp.float32)
    attn_total = lax.psum(attn_part, "tensor")
    hidden_one = input_f + attn_total
    scale_two = rms_scale(hidden_one)
    normed_two = (hidden_one * scale_two * gain_two).astype(jnp.bfloat16)
    rows_all = lax.all_gather(normed_two, "expert", axis=0, tiled=True)
    logits = dots(rows_all, router_rows, ((1,), (1,)), ((), ()))
    probs_all = jax.nn.softmax(logits, axis=-1)
    expert_ids = jnp.arange(total_experts, dtype=jnp.int32)
    named = jnp.any(routes_all[:, :, None] == expert_ids[None, None, :], axis=1)
    gates_all = jnp.where(named, probs_all, 0.0)
    gates_here = lax.dynamic_slice_in_dim(gates_all, here * experts_here, experts_here, axis=1)
    gate_pre = jnp.transpose(dots(rows_all, local_gate, ((1,), (2,)), ((), ())), (1, 0, 2))
    up_pre = jnp.transpose(dots(rows_all, local_up, ((1,), (2,)), ((), ())), (1, 0, 2))
    silu_gate, slope_gate = silu_parts(gate_pre)
    act_rows = (silu_gate * up_pre).astype(jnp.bfloat16)
    part_rows = dots(act_rows, local_down, ((2,), (1,)), ((0,), (0,))).astype(jnp.bfloat16)
    routed_all = sum(
        gates_here[:, j : j + 1] * part_rows[j].astype(F32) for j in range(experts_here)
    )
    shared_gpre = jnp.dot(normed_two, full_sgate, preferred_element_type=jnp.float32)
    shared_upre = jnp.dot(normed_two, full_sup, preferred_element_type=jnp.float32)
    silu_shared, slope_shared = silu_parts(shared_gpre)
    shared_act = (silu_shared * shared_upre).astype(jnp.bfloat16)
    shared_part = jnp.dot(shared_act, full_sdown, preferred_element_type=jnp.float32)
    routed_part = lax.psum_scatter(routed_all, "expert", scatter_dimension=0, tiled=True)
    ffn_total = lax.psum(shared_part + routed_part, "tensor")
    block_output = (hidden_one + ffn_total).astype(jnp.bfloat16)
    grad_out = cotangent.astype(jnp.float32)
    grad_sact = dots(cotangent, full_sdown, ((1,), (1,)), ((), ()))
    grad_sgate = (grad_sact * shared_upre * slope_shared).astype(jnp.bfloat16)
    grad_sup = (grad_sact * silu_shared).astype(jnp.bfloat16)
    grad_normed_two = dots(grad_sgate, full_sgate, ((1,), (1,)), ((), ()))
    grad_normed_two = grad_normed_two + dots(grad_sup, full_sup, ((1,), (1,)), ((), ()))
    grads_wide = grads_all.astype(jnp.float32)
    owner_grads = (jnp.transpose(gates_here)[:, :, None] * grads_wide[None]).astype(jnp.bfloat16)
    grad_act = dots(owner_grads, local_down, ((2,), (2,)), ((0,), (0,)))
    grad_gate_pre = (grad_act * up_pre * slope_gate).astype(jnp.bfloat16)
    grad_up_pre = (grad_act * silu_gate).astype(jnp.bfloat16)
    grad_rows = dots(grad_gate_pre, local_gate, ((0, 2), (0, 1)), ((), ()))
    grad_rows = grad_rows + dots(grad_up_pre, local_up, ((0, 2), (0, 1)), ((), ()))
    gate_dots = jnp.sum(part_rows.astype(jnp.float32) * grads_wide[None], axis=-1)
    dots_wide = jnp.zeros((all_rows, total_experts), jnp.float32)
    dots_wide = lax.dynamic_update_slice(
        dots_wide, jnp.transpose(gate_dots), (0, here * experts_here)
    )
    rows_back = lax.psum_scatter(
        jnp.concatenate([grad_rows, dots_wide], axis=1),
        "expert", scatter_dimension=0, tiled=True,
    )
    rows_back = jnp.concatenate(
        [rows_back[:, :D] + grad_normed_two, rows_back[:, D:]], axis=1)
    rows_back = lax.psum(rows_back, "tensor")
    grad_normed_two = rows_back[:, :D]
    named_own = jnp.any(routes[:, :, None] == expert_ids[None, None, :], axis=1)
    grad_rprobs = jnp.where(named_own, rows_back[:, D:], 0.0)
    router_probs = lax.dynamic_slice_in_dim(probs_all, here * seq_len, seq_len, axis=0)
    grad_logits = (
        router_probs * (grad_rprobs - jnp.sum(grad_rprobs * router_probs, axis=-1, keepdims=True))
    ).astype(jnp.bfloat16)
    router_full = dots(normed_two, grad_logits, ((0,), (0,)), ((), ()))
    grad_normed_two = grad_normed_two + dots(grad_logits, router_rows, ((1,), (0,)), ((), ()))
    ffn_gain_full = jnp.sum(grad_normed_two * hidden_one * scale_two, axis=0)
    weighted_two = grad_normed_two * gain_two
    cube_two = scale_two * scale_two * scale_two
    grad_hidden = (
        grad_out
        + scale_two * weighted_two
        - hidden_one * cube_two * jnp.mean(hidden_one * weighted_two, axis=-1, keepdims=True)
    )
    grad_attn = grad_hidden.astype(jnp.bfloat16)
    grad_mixed = (
        dots(grad_attn, full_output, ((1,), (1,)), ((), ()))
        .astype(jnp.bfloat16)
        .reshape(seq_len, heads_here, HD)
    )
    prob_again = jnp.exp(masked_scores(query_rot, key_rot, allowed) - log_total)
    grad_probs = dots(grad_mixed, value_rows, ((2,), (2,)), ((1,), (1,)))
    grad_scores = (
        prob_again * (grad_probs - jnp.sum(prob_again * grad_probs, axis=-1, keepdims=True))
    ).astype(jnp.bfloat16)
    value_grad_rows = (
        jnp.transpose(dots(prob_again.astype(jnp.bfloat16), grad_mixed, ((1,), (0,)), ((0,), (1,))), (1, 0, 2))
        .astype(jnp.bfloat16)
        .reshape(seq_len, heads_here * HD)
    )
    inverse_root = 1.0 / math.sqrt(HD)
    grad_qrot = (
        jnp.transpose(dots(grad_scores, key_rot, ((2,), (0,)), ((0,), (1,))), (1, 0, 2))
        * inverse_root
    )
    grad_krot = (
        jnp.transpose(dots(grad_scores, query_rot, ((1,), (0,)), ((0,), (1,))), (1, 0, 2))
        * inverse_root
    )
    grad_qpre = (
        unrotate(grad_qrot, cosine, sine_table)
        .astype(jnp.bfloat16)
        .reshape(seq_len, heads_here * HD)
    )
    grad_kpre = (
        unrotate(grad_krot, cosine, sine_table)
        .astype(jnp.bfloat16)
        .reshape(seq_len, heads_here * HD)
    )
    grad_normed_one = dots(grad_qpre, full_query, ((1,), (1,)), ((), ()))
    grad_normed_one = grad_normed_one + dots(grad_kpre, full_key, ((1,), (1,)), ((), ()))
    grad_normed_one = grad_normed_one + dots(value_grad_rows, full_value, ((1,), (1,)), ((), ()))
    grad_normed_one = lax.psum(grad_normed_one.astype(jnp.bfloat16), "tensor").astype(jnp.float32)
    attn_gain_full = jnp.sum(grad_normed_one * input_f * scale_one, axis=0)
    weighted_one = grad_normed_one * gain_one
    cube_one = scale_one * scale_one * scale_one
    input_grad = (
        grad_hidden
        + scale_one * weighted_one
        - input_f * cube_one * jnp.mean(input_f * weighted_one, axis=-1, keepdims=True)
    )
    small_full = jnp.concatenate(
        [router_full, attn_gain_full[:, None], ffn_gain_full[:, None]], axis=1)
    small_grad = lax.psum_scatter(small_full, both, scatter_dimension=0, tiled=True)
    router_grad = small_grad[:, :total_experts]
    attn_gain_grad = small_grad[:, total_experts]
    ffn_gain_grad = small_grad[:, total_experts + 1]
    one_t, two_t = normed_one.T, normed_two.T
    lefts = (one_t, one_t, one_t, mixed_rows.T, two_t, two_t, shared_act.T)
    rights = (grad_qpre, grad_kpre, value_grad_rows, grad_attn, grad_sgate, grad_sup, cotangent)
    exp_left = tuple(jnp.swapaxes(v, 1, 2) for v in (grad_gate_pre, grad_up_pre, act_rows))
    dense = (("rows", "z"),) * 3 + (("cols", "z"), ("rows", "z"), ("rows", "p"), ("cols", "p"))
    if kernels:
        (query_grad, key_grad, value_grad, output_grad, shared_gate_grad, shared_up_grad,
         shared_down_grad, expert_gate_grad, expert_up_grad, expert_down_grad) = scatter(
            dense, lefts, rights, exp_left, rows_all, owner_grads, owners, scatter_order, 1)
    else:
        sums = []
        for (kind, _), left, right in zip(dense, lefts, rights):
            part = jnp.dot(left, right, preferred_element_type=F32)
            dim = 0 if kind == "rows" else 1
            sums.append(lax.psum_scatter(part, both, scatter_dimension=dim, tiled=True))
        for left, right in zip(exp_left, (rows_all, rows_all, owner_grads)):
            dims = (((2,), (0,)), ((), ())) if right.ndim == 2 else (((2,), (1,)), ((0,), (0,)))
            part = lax.dot_general(left, right, dims, preferred_element_type=F32)
            part = lax.psum_scatter(
                part.astype(jnp.bfloat16), "dp", scatter_dimension=2, tiled=True)
            sums.append(part.astype(F32))
        (query_grad, key_grad, value_grad, output_grad, shared_gate_grad, shared_up_grad,
         shared_down_grad, expert_gate_grad, expert_up_grad, expert_down_grad) = sums
    return (
        block_output,
        input_grad,
        attn_gain_grad,
        query_grad,
        key_grad,
        value_grad,
        output_grad,
        ffn_gain_grad,
        router_grad,
        jnp.swapaxes(expert_gate_grad, 1, 2),
        jnp.swapaxes(expert_up_grad, 1, 2),
        expert_down_grad,
        shared_gate_grad,
        shared_up_grad,
        shared_down_grad,
    )


def solution(mesh):
    return jax.shard_map(
        body,
        mesh=mesh,
        in_specs=(
            P(("dp", "expert"), None),
            P(("dp", "expert")),
            P(("dp", "expert"), "tensor"),
            P(("dp", "expert"), "tensor"),
            P(("dp", "expert"), "tensor"),
            P("tensor", ("dp", "expert")),
            P(("dp", "expert")),
            P(("dp", "expert"), None),
            P("expert", "dp", "tensor"),
            P("expert", "dp", "tensor"),
            P("expert", "tensor", "dp"),
            P(("dp", "expert"), "tensor"),
            P(("dp", "expert"), "tensor"),
            P("tensor", ("dp", "expert")),
            P(("dp", "expert"), None),
            P(("dp", "expert"), None),
            P(("dp", "expert"), None),
        ),
        out_specs=(
            P(("dp", "expert"), None),
            P(("dp", "expert"), None),
            P(("dp", "expert")),
            P(("dp", "expert"), "tensor"),
            P(("dp", "expert"), "tensor"),
            P(("dp", "expert"), "tensor"),
            P("tensor", ("dp", "expert")),
            P(("dp", "expert")),
            P(("dp", "expert"), None),
            P("expert", "dp", "tensor"),
            P("expert", "dp", "tensor"),
            P("expert", "tensor", "dp"),
            P(("dp", "expert"), "tensor"),
            P(("dp", "expert"), "tensor"),
            P("tensor", ("dp", "expert")),
        ),
        check_vma=False,
    )
```

time: 3370 us -> 1390 us (0.41)
  waiting for transfers between devices: 2550 us -> 182 us
  Pallas kernels: 0 us -> 919 us
  blocking collectives: 358 us -> 11.8 us
  local copies, waits for them, and re-layouts: 123 us -> 54.9 us
  matrix products: 216 us -> 156 us
  starting transfers between devices: 36.7 us -> 0.69 us
    reduce_scatter x11 -> x3, waiting for transfers between devices: 1720 us -> 107 us  [the longest x1 79.2 us: body(): lax.psum_scatter(jnp.concatenate([grad_rows, dots_wide], axis=1), 'expert...]
    pallas_call x0 -> x2, Pallas kernels: none -> 919 us  [the longest x1 483 us: scatter(): pl.pallas_call(functools.partial(scatter_kernel, dense, units, n, order),...]
    all_to_all x4 -> x0, waiting for transfers between devices: 438 us -> none  [the longest x2 329 us: send_out(): lax.all_to_all(flat_rows.reshape(experts_here, owners, cap_rows, model_wi...]
    all_gather x10 -> x1, waiting for transfers between devices: 371 us -> 29.1 us  [body(): rows_all = lax.all_gather(normed_two, 'expert', axis=0, tiled=True)]
    all_gather x3 -> x1, blocking collectives: 282 us -> 11.8 us  [body(): routes_all = lax.all_gather(routes, 'expert', axis=0, tiled=True)]
    unnamed x1 -> x0, blocking collectives: 73.1 us -> none
    dot_general x34 -> x22, matrix products: 190 us -> 135 us  [dots(): return lax.dot_general(left, right, dims, preferred_element_type=F32)]
    reshape x8 -> x2, local copies, waits for them, and re-layouts: 41.5 us -> 1.97 us  [the longest x1 1.8 us: body(): value_grad_rows = jnp.transpose(dots(prob_again.astype(jnp.bfloat16), gra...]
  transfers between devices with their start and end apart: 28 -> 7, of which waited for: 20 -> 6; matrix products, arithmetic and copies ran while one was open for 10% -> 6% of each run, Pallas kernels for 0% -> 35%
where the time goes in v1:
time: 1390 us; the launch traced here: 1380 us
  Pallas kernels  919 us (66%)
  waiting for transfers between devices  182 us (13%)
  matrix products  156 us (11%)
  local copies, waits for them, and re-layouts  54.9 us (4%)
  other arithmetic  40.7 us (3%)
  between operations  15.2 us (1%)
    pallas_call x1, Pallas kernels, scatter(): pl.pallas_call(functools.partial(scatter_kernel, dense, units, n, order),...  483 us
    pallas_call x1, Pallas kernels, gather(): pl.pallas_call(functools.partial(gather_kernel, leaves, n, starts), out_s...  436 us
    dot_general x22, matrix products, dots(): return lax.dot_general(left, right, dims, preferred_element_type=F32)  135 us
    reduce_scatter x1, waiting for transfers between devices, body(): lax.psum_scatter(jnp.concatenate([grad_rows, dots_wide], axis=1), 'expert...  79.2 us
    unnamed x131, local copies, waits for them, and re-layouts  40.5 us
    all_gather x1, waiting for transfers between devices, body(): rows_all = lax.all_gather(normed_two, 'expert', axis=0, tiled=True)  29.1 us
    reduce_scatter x1, waiting for transfers between devices, body(): lax.psum_scatter(routed_all, 'expert', scatter_dimension=0, tiled=True)  27.9 us
  transfers between devices with their start and end apart: 7, of which 6 were waited for; matrix products, arithmetic and copies ran while one was open for 6% of the time, Pallas kernels for 35%

profile of v1, /device:TPU:16, one launch (start us, length us, event | category | flops | bytes accessed | tf_op | source)
XLA Modules:
  0.0 1380.8 jit_solution(9362317488342931796)
XLA Ops:
  24.2 436.3 %shard_map.280 = (bf16[2048,1024]{1,0:T(8,128)(2,1)}, bf16[2048,1024]{1,0:T(8,128)(2,1)}, bf16[2048,1024]{1,0:T(8,128)(2,1)}, bf16[1024,2048]{1,0:T(8,128)(2,1)}...) custom-call(bf16[128,1024]{1,0:T(8,128)(2,1)S(1)} %copy-done.8, ...), custom_call_target="tpu_custom_call" | custom-call | tf_op jit(solution)/shard_map/pallas_call | solution.py:237
  460.6 3.1 fusion.33
  463.7 3.0 convolution_bitcast_fusion.1
  473.3 22.1 %all-reduce.6.cloned.1.call-done = f32[128,2048]{1,0:T(8,128)} async-done(((f32[128,2048]{1,0:T(8,128)}), f32[128,2048]{1,0:T(8,128)}) %all-reduce.6.cloned.1.call-update) | async-done | bytes 1048592 | tf_op jit(solution)/shard_map/psum | solution.py:798
  499.1 11.8 all_gather.6
  515.5 29.1 %all-gather.2.cloned.1.call-done.refs_17_ = bf16[512,2048]{1,0:T(8,128)(2,1)} async-done(((bf16[128,2048]{1,0:T(8,128)(2,1)}), bf16[512,2048]{1,0:T(8,128)(2,1)}) %all-gather.2.cloned.1.call-update) | async-done | bytes 2097168 | tf_op jit(solution)/shard_map/all_gather | solution.py:802
  549.2 12.1 fusion.82
  561.4 9.1 fusion.27
  570.4 19.2 %fusion.7 = (bf16[4,704,512]{2,1,0:T(8,128)(2,1)}, bf16[4,704,512]{2,1,0:T(8,128)(2,1)}, bf16[4,704,512]{2,1,0:T(8,128)(2,1)}, f32[512,4,704]{0,2,1:T(8,128)}) fusion(f32[512,4,704]{0,2,1:T(8,128)S(1)} %fusion.27, f32[4,512,704]{1,2,0:T(8,128)} %fusion.82, bf16[4,704,2048]{2,1,0:T(8,128)(2,1)} %get-tuple-element.46, bf16[512,2048]{1,0:T(8,128)(2,1)S(1)} %copy-done.23), kind=kOutput, calls=%fused_computation.14 | convolution fusion | flops 5927206912 | bytes 39583744 | tf_op jit(solution)/shard_map/dot_general | solution.py:693
  589.6 32.6 %multiply_convert_fusion = (bf16[4,512,2048]{2,1,0:T(8,128)(2,1)}, f32[4,512]{1,0:T(4,128)S(1)}, bf16[4,512,2048]{2,1,0:T(8,128)(2,1)}) fusion(f32[512,2048]{1,0:T(8,128)} %convert_element_type.158, f32[4,512]{1,0:T(4,128)S(1)} %copy.131, bf16[4,704,2048]{2,1,0:T(8,128)(2,1)} %get-tuple-element.47, f32[512,4,704]{0,2,1:T(8,128)} %get-tuple-element.117, ...), kind=kOutput, calls=%fused_computation.1 | convolution fusion | flops 5939394560 | bytes 44056576 | tf_op jit(solution)/shard_map/dot_general | solution.py:693
  622.2 5.7 fusion.17
  629.6 15.8 %fusion.21 = f32[512,2048,1]{1,0,2:T(8,128)S(1)} fusion(bf16[4,704,2048]{2,1,0:T(8,128)(2,1)} %get-tuple-element.45, f32[4,512,704]{1,2,0:T(8,128)} %fusion.82, f32[512,4,704]{0,2,1:T(8,128)} %get-tuple-element.117, f32[512,4,704]{0,2,1:T(8,128)} %copy-done.54), kind=kOutput, calls=%fused_computation.41 | convolution fusion | flops 5919997952 | bytes 33030144 | tf_op jit(solution)/shard_map/dot_general | solution.py:693
  645.4 12.6 bitcast_add_fusion
  660.5 3.7 fusion.91
  664.2 3.8 fusion.90
  668.1 5.7 multiply_convert_fusion.4
  677.5 27.9 %reduce-scatter.4.cloned.1.call-done = f32[128,2048]{1,0:T(8,128)} async-done(((f32[512,2048]{1,0:T(8,128)}), f32[128,2048]{1,0:T(8,128)}) %reduce-scatter.4.cloned.1.call-update) | async-done | bytes 1048592 | tf_op jit(solution)/shard_map/reduce_scatter | solution.py:822
  705.4 5.1 convolution_add_fusion.4
  710.5 79.2 %reduce-scatter.6.cloned.1.call-done = f32[128,2064]{1,0:T(8,128)} async-done(((f32[512,2064]{1,0:T(8,128)}), f32[128,2064]{1,0:T(8,128)}) %reduce-scatter.6.cloned.1.call-update) | async-done | bytes 1056784 | tf_op jit(solution)/shard_map/reduce_scatter | solution.py:843
  789.7 5.3 fusion.23
  804.6 13.4 all-reduce.10.cloned.1.call-done
  848.7 10.2 all-reduce.8.cloned.1.call-done
  865.3 483.0 %shard_map.281 = (f32[128,1024]{1,0:T(8,128)}, f32[128,1024]{1,0:T(8,128)}, f32[128,1024]{1,0:T(8,128)}, f32[1024,128]{1,0:T(8,128)}, f32[128,1408]{1,0:T(8,128)...) custom-call(bf16[2048,128]{1,0:T(8,128)(2,1)} %copy.149.refs_0_.refs, ...), custom_call_target="tpu_custom_call" | custom-call | tf_op jit(solution)/shard_map/pallas_call | solution.py:637
  1358.4 6.4 copy.217
  (217 shorter events, 109.4 us)
Async XLA Ops:
  7.2 488.2 %all-reduce.6.cloned.1.call-start = ((), (), s32[]{:S(2)}) async-start(), calls=%async_computation.3 | async-start | bytes 2097152 | tf_op jit(solution)/shard_map/psum | solution.py:798
  7.2 453.3 %copy-start.12 = (bf16[128,2048]{1,0:T(8,128)(2,1)S(1)}, bf16[128,2048]{1,0:T(8,128)(2,1)}, u32[]{:S(2)}) copy-start(bf16[128,2048]{1,0:T(8,128)(2,1)} %param.17) | copy-start | bytes 1572868
  9.1 457.8 %copy-start.49 = (f32[128]{0:T(128)}, f32[128]{0:T(128)S(1)}, u32[]{:S(2)}) copy-start(f32[128]{0:T(128)S(1)} %get-tuple-element.104) | copy-start | bytes 1540
  10.2 457.9 %copy-start.42 = (f32[128,64]{1,0:T(8,128)}, f32[128,64]{1,0:T(8,128)S(1)}, u32[]{:S(2)}) copy-start(f32[128,64]{1,0:T(8,128)S(1)} %get-tuple-element.107) | copy-start | bytes 98308
  10.2 457.9 %copy-start.44 = (f32[128,64]{1,0:T(8,128)}, f32[128,64]{1,0:T(8,128)S(1)}, u32[]{:S(2)}) copy-start(f32[128,64]{1,0:T(8,128)S(1)} %get-tuple-element.108) | copy-start | bytes 98308
  473.2 71.4 %all-gather.2.cloned.1.call-start = ((), (), s32[]{:S(2)}) async-start(), calls=%async_computation.4 | async-start | bytes 2621440 | tf_op jit(solution)/shard_map/all_gather | solution.py:802
  499.1 206.3 %reduce-scatter.4.cloned.1.call-start = ((), (), s32[]{:S(2)}) async-start(), calls=%async_computation.5 | async-start | bytes 5242880 | tf_op jit(solution)/shard_map/reduce_scatter | solution.py:822
  547.5 271.6 %copy-start.35 = (f32[512,16]{1,0:T(8,128)}, f32[512,16]{1,0:T(8,128)S(1)}, u32[]{:S(2)}) copy-start(f32[512,16]{1,0:T(8,128)S(1)} %fusion.57) | copy-start | bytes 98308
  549.2 12.1 copy-start.23
  570.4 19.2 %copy-start.54 = (f32[512,4,704]{0,2,1:T(8,128)}, f32[512,4,704]{0,2,1:T(8,128)S(1)}, u32[]{:S(2)}) copy-start(f32[512,4,704]{0,2,1:T(8,128)S(1)} %fusion.27) | copy-start | bytes 17301508
  627.9 161.8 %reduce-scatter.6.cloned.1.call-start = ((), (), s32[]{:S(2)}) async-start(), calls=%async_computation.6 | async-start | bytes 5570560 | tf_op jit(solution)/shard_map/reduce_scatter | solution.py:843
  660.5 157.5 %all-reduce.10.cloned.1.call-start = ((), (), s32[]{:S(2)}) async-start(), calls=%async_computation.9 | async-start | bytes 4325376 | tf_op jit(solution)/shard_map/psum | solution.py:823
  664.2 10.3 slice-start
  796.1 23.0 %copy-start.51 = (f32[128]{0:T(128)S(1)}, f32[128]{0:T(128)}, u32[]{:S(2)}) copy-start(f32[128]{0:T(128)} %copy-done.50) | copy-start | bytes 1540
  796.1 62.9 %all-reduce.8.cloned.1.call-start = ((), (), s32[]{:S(2)}) async-start(), calls=%async_computation.7 | async-start | bytes 1048576 | tf_op jit(solution)/shard_map/psum | solution.py:905
  797.4 24.3 %copy-start.46 = (pred[128,16]{1,0:T(32,128)(4,1)}, pred[128,16]{1,0:T(32,128)(4,1)S(1)}, u32[]{:S(2)}) copy-start(pred[128,16]{1,0:T(32,128)(4,1)S(1)} %copy.134) | copy-start | bytes 6148
  824.6 8.4 copy-start.26
  824.6 8.4 copy-start.43
  824.6 8.4 copy-start.45
  827.6 9.1 copy-start.32
  836.7 22.3 %copy-start.13 = (bf16[128,2048]{1,0:T(8,128)(2,1)S(1)}, bf16[128,2048]{1,0:T(8,128)(2,1)}, u32[]{:S(2)}) copy-start(bf16[128,2048]{1,0:T(8,128)(2,1)} %param.17) | copy-start | bytes 1572868
  836.7 25.1 %copy-start.27 = (f32[128,2048]{1,0:T(8,128)S(1)}, f32[128,2048]{1,0:T(8,128)}, u32[]{:S(2)}) copy-start(f32[128,2048]{1,0:T(8,128)} %get-tuple-element.70) | copy-start | bytes 3145732
  839.0 509.3 %reduce-scatter.8.cloned.1.call-start = ((), (), s32[]{:S(2)}) async-start(), calls=%async_computation.8 | async-start | bytes 208896 | tf_op jit(solution)/shard_map/reduce_scatter | solution.py:916
  1358.4 9.2 slice-start.2
  (43 other events, 137.9 us)
Sparse Core Ops, SparseCore 0:
  473.3 21.9 all-reduce.5
  499.2 45.3 all-gather.1
  628.0 77.2 reduce-scatter.3
  708.1 81.5 reduce-scatter.5
  796.2 21.7 all-reduce.9
  839.1 19.7 all-reduce.7
  861.9 74.3 reduce-scatter.7

commit v2 on v1

--- a/solution.py
+++ b/solution.py
@@ -9,18 +9,19 @@
 from jax.sharding import PartitionSpec as P
 
 MESH = pl.DeviceIdType.MESH
-F32 = jnp.float32
-
+F32, BF = jnp.float32, jnp.bfloat16
+DP, EXPERT, TENSOR = "dp", "expert", "tensor"
+BOTH = (DP, EXPERT)
 D = 2048
 HD = 128
-TOPK = 6
 
 
 epsilon = 1e-06
 rope_base = 10000.0
-scatter_order = (46, 68, 63, 64, 18, 10, 11, 84, 88, 89, 19, 54, 9, 74, 45, 36, 38, 73, 70, 20, 83, 90, 28, 55, 37, 12, 48, 30, 65, 56, 78, 27, 47, 66, 39, 79, 91, 14, 0, 29, 13, 76, 69, 1, 21, 41, 16, 57, 75, 40, 49, 86, 3, 71, 58, 23, 43, 2, 92, 31, 42, 85, 67, 51, 32, 59, 77, 22, 25, 50, 33, 87, 5, 44, 61, 4, 15, 60, 24, 52, 34, 80, 81, 6, 17, 26, 72, 53, 62, 35, 7, 82, 8)
-gather_starts = (2.97, 4.29, 2.32, 3.19, 2.3, 2.4, 5.08, 6.72, 5.91, 6.5, 6.76, 5.24)
 masked_score = -1e30
+gather_starts = (1.91, 2.48, 3.88, 2.78, 2.0, 1.0, 1.1)
+scatter_order = (46, 77, 72, 73, 18, 10, 11, 93, 97, 98, 19, 54, 9, 83, 45, 36, 38, 82, 79, 20, 92, 99, 28, 55, 37, 12, 48, 30, 74, 56, 87, 27, 47, 75, 39, 88, 100, 14, 0, 63, 29, 13, 85, 78, 1, 64, 21, 41, 16, 57, 84, 40, 49, 95, 3, 66, 80, 58, 23, 43, 2, 65, 101, 31, 42, 94, 76, 51, 32, 59, 86, 22, 25, 50, 33, 96, 5, 68, 44, 61, 4, 67, 15, 60, 24, 52, 34, 89, 90, 6, 69, 17, 26, 81, 53, 62, 35, 7, 70, 91, 8, 71)
+middle_order = (49, 25, 26, 27, 33, 37, 45, 46, 5, 34, 50, 6, 35, 99, 7, 8, 21, 47, 53, 48, 57, 84, 100, 101, 13, 69, 17, 18, 70, 80, 88, 0, 1, 36, 102, 73, 51, 52, 38, 39, 89, 29, 30, 65, 61, 74, 114, 28, 41, 42, 43, 66, 129, 85, 81, 82, 9, 10, 11, 12, 95, 71, 72, 103, 40, 31, 32, 90, 91, 22, 19, 20, 44, 115, 23, 24, 75, 76, 62, 2, 118, 67, 68, 77, 3, 4, 78, 79, 54, 55, 56, 86, 87, 63, 64, 96, 97, 104, 110, 14, 15, 83, 92, 93, 94, 16, 119, 58, 59, 60, 105, 106, 116, 111, 98, 107, 108, 109, 125, 117, 112, 120, 113, 121, 122, 123, 124, 126, 130, 127, 131, 128, 132, 133)
 
 
 class Leaf:
@@ -77,12 +78,12 @@
     ins, outs = refs[:m], refs[m : 2 * m]
     stages = refs[2 * m : 3 * m]
     in_sem, out_sem, send_sem, recv_sem = refs[3 * m :]
-    d, e, t = lax.axis_index("dp"), lax.axis_index("expert"), lax.axis_index("tensor")
+    d, e, t = lax.axis_index(DP), lax.axis_index(EXPERT), lax.axis_index(TENSOR)
     dx = d + 1 - 2 * lax.rem(d, 2)
     dy = lax.rem(d + 2, 4)
     dd = lax.rem(dx + 2, 4)
-    near = {"x": {"dp": dx}, "y": {"dp": dy}, "r": {"expert": e + 1}, "l": {"expert": e - 1},
-            "c": {"tensor": 1 - t}}
+    near = {"x": {DP: dx}, "y": {DP: dy}, "r": {EXPERT: e + 1}, "l": {EXPERT: e - 1},
+            "c": {TENSOR: 1 - t}}
     has = {"r": e < n - 1, "l": e > 0}
 
     barrier = pltpu.get_barrier_semaphore()
@@ -243,7 +244,7 @@
             pltpu.SemaphoreType.DMA((m,)), pltpu.SemaphoreType.DMA((m,)),
             pltpu.SemaphoreType.DMA((total,)), pltpu.SemaphoreType.DMA((total,))],
         compiler_params=pltpu.CompilerParams(
-            collective_id=0, has_side_effects=True, vmem_limit_bytes=40 << 20),
+            collective_id=0, has_side_effects=True, vmem_limit_bytes=60 << 20),
     )(*arrays)
 
 
@@ -268,24 +269,24 @@
     m = len(dense)
     lefts, rights = refs[:m], refs[m : 2 * m]
     exp_left = refs[2 * m : 2 * m + 3]
-    rows_all, grads_in = refs[2 * m + 3 : 2 * m + 5]
-    refs = refs[2 * m + 5 :]
+    rows_all, grads_in, extra = refs[2 * m + 3 : 2 * m + 6]
+    refs = refs[2 * m + 6 :]
     outs, refs = refs[: m + 3], refs[m + 3 :]
     landed, refs = refs[: 3 * m + 2], refs[3 * m + 2 :]
     bufs = dict(zip("xyz", refs[:3]))
     held, tall, wide = refs[3:6]
     stage_sem, load_sem, recv_sem = refs[6:9]
     send_sems = dict(zip("xyz", refs[9:12]))
-    d, e = lax.axis_index("dp"), lax.axis_index("expert")
+    d, e = lax.axis_index(DP), lax.axis_index(EXPERT)
     dx = d + 1 - 2 * lax.rem(d, 2)
     dy = lax.rem(d + 2, 4)
     dd = lax.rem(dx + 2, 4)
     after, before = e < n - 1, e > 0
 
     barrier = pltpu.get_barrier_semaphore()
-    for dev in ({"dp": dx}, {"dp": dy}):
+    for dev in ({DP: dx}, {DP: dy}):
         pl.semaphore_signal(barrier, inc=1, device_id=dev, device_id_type=MESH)
-    for cond, dev in ((after, {"expert": e + 1}), (before, {"expert": e - 1})):
+    for cond, dev in ((after, {EXPERT: e + 1}), (before, {EXPERT: e - 1})):
         @pl.when(cond)
         def _():
             pl.semaphore_signal(barrier, inc=1, device_id=dev, device_id_type=MESH)
@@ -332,7 +333,7 @@
         seen.add(key)
         c = pltpu.make_async_remote_copy(
             src_ref=view, dst_ref=view, send_sem=recv_sem.at[sem], recv_sem=recv_sem.at[sem],
-            device_id={"dp": dx}, device_id_type=MESH)
+            device_id={DP: dx}, device_id_type=MESH)
         when(cond, c.wait_recv)
 
     class Loads:
@@ -367,7 +368,11 @@
             step = half_rows // 2
             for r in range(0, half_rows, step):
                 left = lefts[i][pl.ds(pl.multiple_of(half * half_rows + r, 16), step), :]
-                put(r, jnp.dot(left, right, preferred_element_type=F32), 0)
+                res = jnp.dot(left, right, preferred_element_type=F32)
+                if i == m - 1:
+                    at = pl.ds(pl.multiple_of(half * half_rows + r, 16), step)
+                    res = res + extra[at, pl.ds(pl.multiple_of(block * 128, 128), 128)]
+                put(r, res, 0)
 
     def half_rows_of(i):
         if dense[i][0] == "rows":
@@ -455,11 +460,11 @@
                 for s in ("y1", "x1", "x2", "y2"):
                     plane_arrived(s)
             pl.when(cond)(go)
-            send("z", k, z_rows, z_land.at[side, t], z_sem + side * n + t, {"expert": e - 1 + 2 * side}, cond)
+            send("z", k, z_rows, z_land.at[side, t], z_sem + side * n + t, {EXPERT: e - 1 + 2 * side}, cond)
         elif stage == "p":
             s = arg
             link = s[0]
-            dev = {"dp": dy if link == "y" else dx}
+            dev = {DP: dy if link == "y" else dx}
             half = 0 if s in ("y1", "x2") else 1
             k = slot(link)
             ld = Loads()
@@ -563,7 +568,7 @@
         ld = Loads()
         if stage == "p":
             link = s[0]
-            dev = {"dp": dy if link == "y" else dx}
+            dev = {DP: dy if link == "y" else dx}
             j = q if s in ("y1", "x2") else q + 2
             k = slot(link)
             if s in ("y1", "x1"):
@@ -611,7 +616,7 @@
     assert sum(c for _, c in sems.values()) <= recv_sem.shape[0]
 
 
-def scatter(dense, lefts, rights, exp_left, rows_all, grads_in, n, order, cid):
+def scatter(dense, lefts, rights, extra, exp_left, rows_all, grads_in, n, order, cid):
     m, units = len(dense), 6
     bf = jnp.bfloat16
     outs, landed = [], []
@@ -637,7 +642,7 @@
     res = pl.pallas_call(
         functools.partial(scatter_kernel, dense, units, n, order),
         out_shape=outs + landed,
-        in_specs=[vmem] * (2 * m + 5),
+        in_specs=[vmem] * (2 * m + 6),
         out_specs=[anyspace] * (len(outs) + len(landed)),
         scratch_shapes=[pltpu.VMEM((ring_slots[s], message_rows, 128), bf) for s in "xyz"] + [
             pltpu.VMEM((4, message_rows, 128), bf),
@@ -648,8 +653,455 @@
         ] + [pltpu.SemaphoreType.DMA((ring_slots[s],)) for s in "xyz"],
         compiler_params=pltpu.CompilerParams(
             collective_id=cid, has_side_effects=True, vmem_limit_bytes=60 << 20),
-    )(*lefts, *rights, *exp_left, rows_all, grads_in)
+    )(*lefts, *rights, *exp_left, rows_all, grads_in, extra)
     return res[: m + 3]
+
+
+def pair_kernel(part, total, other, send_sem, recv_sem):
+    t = lax.axis_index(TENSOR)
+    partner = {TENSOR: 1 - t}
+    barrier = pltpu.get_barrier_semaphore()
+    pl.semaphore_signal(barrier, inc=1, device_id=partner, device_id_type=MESH)
+    pl.semaphore_wait(barrier, 1)
+    rows = part.shape[0] // 4
+    copies = []
+    for k in range(4):
+        piece = pl.ds(k * rows, rows)
+        c = pltpu.make_async_remote_copy(
+            src_ref=part.at[piece], dst_ref=other.at[piece], send_sem=send_sem.at[k],
+            recv_sem=recv_sem.at[k], device_id=partner, device_id_type=MESH)
+        c.start()
+        copies.append(c)
+    for k, c in enumerate(copies):
+        c.wait_recv()
+        piece = pl.ds(k * rows, rows)
+        total[piece, :] = part[piece, :].astype(F32) + other[piece, :].astype(F32)
+    for c in copies:
+        c.wait_send()
+
+
+def pair_sum(part, cid):
+    vmem = pl.BlockSpec(memory_space=pltpu.VMEM)
+    return pl.pallas_call(
+        pair_kernel,
+        out_shape=jax.ShapeDtypeStruct(part.shape, F32),
+        in_specs=[vmem],
+        out_specs=vmem,
+        scratch_shapes=[pltpu.VMEM(part.shape, part.dtype),
+                        pltpu.SemaphoreType.DMA((4,)), pltpu.SemaphoreType.DMA((4,))],
+        compiler_params=pltpu.CompilerParams(collective_id=cid, has_side_effects=True),
+    )(part)
+
+
+def across(a, b):
+    return lax.dot_general(a, b, (((1,), (1,)), ((), ())), preferred_element_type=F32)
+
+
+def times(a, b):
+    return jnp.dot(a, b, preferred_element_type=F32)
+
+
+def middle_items(n, here):
+    items = [("join",)]
+    for k in range(1, n):
+        items.append(("rows", k))
+    items.append(("gates",))
+    for i in range(3):
+        items += [("plane", 12 + i, s) for s in range(4)]
+        items += [("line", i, b, k) for b in range(4) for k in range(n)]
+    for j in range(here):
+        for a in range(3):
+            items += [("plane", 3 * j + a, s) for s in range(4)]
+        items += [("load", j), ("front", j), ("back", j)]
+    items += [("shared_load", v) for v in range(2)] + [("shared", v) for v in range(2)]
+    return items + [("settle",), ("fold_start",), ("fold_lines",), ("fold_shared",), ("fold_end",)]
+
+
+def middle_kernel(n, order, *refs):
+    (part, inp, gain, router, named, cot, gate_in, up_in, down_in, sg_in, su_in, sd_in) = refs[:12]
+    refs = refs[12:]
+    (hidden, normed, rows_all, probs, few, gn2, ffn, act_t, ggp_t, gup_t, copies_out,
+     gsg, gsu, sact_t) = refs[:14]
+    exp_land, sh_land = refs[14:17], refs[17:20]
+    refs = refs[20:]
+    (other, weights, gates, back, routed, gpre, upre, act, grad, copy_buf, turned, eye,
+     sh_stage, dot_sums, fold_other, fold_own, fold_out, fold_in, few_other, few_out, few_in,
+     ffn_own, gn_own) = refs[:23]
+    (pair_send, pair_recv, row_send, row_recv, plane_send, plane_recv, line_send, line_recv,
+     load_sem, out_sem, stage_sem, zsend, zrecv) = refs[23:]
+    ins = (gate_in, up_in, down_in)
+    sh_ins = (sg_in, su_in, sd_in)
+    here, hid, width = gate_in.shape
+    toks = inp.shape[0]
+    alltoks = n * toks
+    D_ = inp.shape[1]
+    half = D_ // 2
+    d, e, t = lax.axis_index(DP), lax.axis_index(EXPERT), lax.axis_index(TENSOR)
+    dx = d + 1 - 2 * lax.rem(d, 2)
+    dy = lax.rem(d + 2, 4)
+    dd = lax.rem(dx + 2, 4)
+    after, before = e < n - 1, e > 0
+    near = {"x": {DP: dx}, "y": {DP: dy}, "r": {EXPERT: e + 1}, "l": {EXPERT: e - 1},
+            "c": {TENSOR: 1 - t}}
+    peers = [lax.rem(e + k, n) for k in range(1, n)]
+    mine = pl.ds(pl.multiple_of(t * half, half), half)
+    theirs = pl.ds(pl.multiple_of((1 - t) * half, half), half)
+
+    barrier = pltpu.get_barrier_semaphore()
+    for dev in [near["x"], near["y"], near["c"]] + [{EXPERT: p} for p in peers]:
+        pl.semaphore_signal(barrier, inc=1, device_id=dev, device_id_type=MESH)
+    pl.semaphore_wait(barrier, 3 + n - 1)
+
+    def when(cond, f):
+        if cond is None:
+            f()
+        else:
+            pl.when(cond)(f)
+
+    sends = []
+
+    def remote(src, dst, ssem, rsem, dev, cond=None, start=True):
+        c = pltpu.make_async_remote_copy(
+            src_ref=src, dst_ref=dst, send_sem=ssem, recv_sem=rsem, device_id=dev,
+            device_id_type=MESH)
+        if start:
+            when(cond, c.start)
+            sends.append((c, cond))
+        return c
+
+    def block(p):
+        return pl.ds(pl.multiple_of(p * toks, toks), toks)
+
+    first = [remote(part.at[pl.ds(k * (toks // 2), toks // 2)], other.at[pl.ds(k * (toks // 2), toks // 2)],
+                    pair_send.at[k], pair_recv.at[k], near["c"]) for k in range(2)]
+    for i in range(3):
+        pltpu.make_async_copy(sh_ins[i], sh_stage.at[i], stage_sem.at[i]).start()
+
+    def join():
+        for k, c in enumerate(first):
+            c.wait_recv()
+            p = pl.ds(k * (toks // 2), toks // 2)
+            h = inp[p, :].astype(F32) + (part[p, :] + other[p, :])
+            scale = lax.rsqrt(jnp.mean(h * h, axis=-1, keepdims=True) + epsilon)
+            hidden[p, :] = h
+            rows = (h * scale * gain[...]).astype(jnp.bfloat16)
+            normed[p, :] = rows
+            rows_all[pl.ds(pl.multiple_of(e * toks + k * (toks // 2), toks // 2), toks // 2), :] = rows
+        for k, p in enumerate(peers):
+            remote(normed.at[:, mine], rows_all.at[block(e), mine], row_send.at[k], row_recv.at[k], {EXPERT: p})
+
+    def rows_step(k):
+        o = lax.rem(e + n - k, n)
+        view = rows_all.at[block(o), mine]
+        remote(view, view, row_send.at[k - 1], row_recv.at[k - 1], near["c"], start=False).wait_recv()
+        remote(view, view, row_send.at[n - 1 + k - 1], row_recv.at[n - 1 + k - 1], near["c"])
+
+    def gates_step():
+        for k in range(1, n):
+            o = lax.rem(e + n - k, n)
+            view = rows_all.at[block(o), theirs]
+            remote(view, view, row_send.at[n - 1 + k - 1], row_recv.at[n - 1 + k - 1], near["c"], start=False).wait_recv()
+        logits = across(rows_all[...], router[...])
+        lane = lax.broadcasted_iota(jnp.int32, logits.shape, 1)
+        logits = jnp.where(lane < 4 * n, logits, -1e30)
+        top = jnp.max(logits, axis=-1, keepdims=True)
+        ex = jnp.exp(logits - top)
+        pr = ex / jnp.sum(ex, axis=-1, keepdims=True)
+        gates[...] = pr * named[...].astype(F32)
+        back[...] = jnp.zeros_like(back)
+        routed[...] = jnp.zeros_like(routed)
+        dot_sums[...] = jnp.zeros_like(dot_sums)
+        ffn_own[...] = jnp.zeros_like(ffn_own)
+        gn_own[...] = jnp.zeros_like(gn_own)
+        r = lax.broadcasted_iota(jnp.int32, eye.shape, 0)
+        c = lax.broadcasted_iota(jnp.int32, eye.shape, 1)
+        eye[...] = jnp.where(r == c, 1.0, 0.0).astype(jnp.bfloat16)
+        own = block(e)
+        probs[...] = (across(rows_all[own, :], router[...]))
+
+    def plane_view(i, o, h):
+        if i < 12:
+            k = hid // 2
+            return exp_land[i % 3].at[i // 3, pl.ds(h * k, k), pl.ds(pl.multiple_of(o * width, width), width)]
+        k = sh_land[i - 12].shape[0] // 2
+        return sh_land[i - 12].at[pl.ds(h * k, k), pl.ds(pl.multiple_of((o * n + e) * 128, 128), 128)]
+
+    def plane_own(i, h):
+        if i < 12:
+            k = hid // 2
+            return ins[i % 3].at[i // 3, pl.ds(h * k, k)]
+        k = sh_land[i - 12].shape[0] // 2
+        return sh_ins[i - 12].at[pl.ds(h * k, k)]
+
+    kinds = ("x0", "y1", "x1", "y0", "f0", "f1")
+
+    def plane_copy(i, o, h, side, kind, own=False, start=True):
+        s = 6 * i + kinds.index(kind)
+        dst = plane_view(i, o, h)
+        return remote(plane_own(i, h) if own else dst, dst, plane_send.at[s], plane_recv.at[s], near[side], start=start)
+
+    def plane_step(i, s):
+        if s == 0:
+            plane_copy(i, d, 0, "x", "x0", own=True)
+            plane_copy(i, d, 1, "y", "y1", own=True)
+            plane_copy(i, d, 1, "x", "x1", own=True)
+            plane_copy(i, d, 0, "y", "y0", own=True)
+        elif s == 1:
+            plane_copy(i, dx, 0, "x", "x0", start=False).wait_recv()
+            plane_copy(i, dx, 0, "y", "f0")
+            plane_copy(i, dy, 1, "x", "y1", start=False).wait_recv()
+            plane_copy(i, dy, 1, "x", "f1")
+        elif s == 2:
+            plane_copy(i, dx, 1, "x", "x1", start=False).wait_recv()
+            plane_copy(i, dy, 0, "x", "y0", start=False).wait_recv()
+        else:
+            plane_copy(i, dd, 0, "x", "f0", start=False).wait_recv()
+            plane_copy(i, dd, 1, "x", "f1", start=False).wait_recv()
+
+    def line_view(i, o, eo):
+        return sh_land[i].at[:, pl.ds(pl.multiple_of((o * n + eo) * 128, 128), 128)]
+
+    def line_step(i, b, k):
+        o = (d, dx, dy, dd)[b]
+        base = (i * 4 + b) * 2 * (n - 1)
+
+        def copy(eo, side, hop, own=False, cond=None, start=True):
+            s = base + (0 if side == "r" else n - 1) + hop - 1
+            dst = line_view(i, o, eo)
+            return remote(sh_ins[i] if own else dst, dst, line_send.at[s], line_recv.at[s], near[side], cond, start)
+
+        if k == 0:
+            copy(e, "r", 1, b == 0, after)
+            copy(e, "l", 1, b == 0, before)
+            return
+        for side, eo, there, has in (("r", e - k, e >= k, after), ("l", e + k, e + k < n, before)):
+            when(there, copy(eo, side, k, start=False).wait_recv)
+            if k < n - 1:
+                copy(eo, side, k + 1, cond=jnp.logical_and(there, has))
+
+    loads = {}
+
+    def load(j):
+        cs = []
+        for a in range(3):
+            for q, o in enumerate((d, dx, dy, dd)):
+                cols = pl.ds(pl.multiple_of(o * width, width), width)
+                src = ins[a].at[j] if q == 0 else exp_land[a].at[j, :, cols]
+                c = pltpu.make_async_copy(src, weights.at[j % 2, a, :, cols], load_sem.at[j % 2, 4 * a + q])
+                c.start()
+                cs.append(c)
+        loads[j] = cs
+
+    writes = []
+    waiting = {}
+
+    def write(src, dst, k):
+        c = pltpu.make_async_copy(src, dst, out_sem.at[k])
+        c.start()
+        waiting[k] = c
+
+    def free(k):
+        if k in waiting:
+            waiting.pop(k).wait()
+
+    def ffn_front(rows, count, w):
+        step = min(256, count)
+        def pre(m, _):
+            r = pl.ds(pl.multiple_of(m * step, step), step)
+            x = rows[r, :]
+            g = across(x, w(0))
+            u = across(x, w(1))
+            gpre[r, :] = g
+            upre[r, :] = u
+            act[r, :] = (g * jax.nn.sigmoid(g) * u).astype(jnp.bfloat16)
+            return 0
+        lax.fori_loop(0, count // step, pre, 0)
+
+    def front(j):
+        for c in loads.pop(j):
+            c.wait()
+        w = lambda a: weights[j % 2, a]
+        ffn_front(rows_all, alltoks, w)
+        free(3)
+        lane = lax.broadcasted_iota(jnp.int32, (256, 128), 1)
+        def out(k, _):
+            m, c = k // 4, k % 4
+            r = pl.ds(pl.multiple_of(m * 256, 256), 256)
+            cols = pl.ds(pl.multiple_of(c * 512, 512), 512)
+            piece = times(act[r, :], weights[j % 2, 2, :, cols]).astype(jnp.bfloat16).astype(F32)
+            gt = gates[r, :][:, j : j + 1]
+            ct = cot[r, cols].astype(F32)
+            routed[r, cols] += gt * piece
+            dot = jnp.sum(piece * ct, axis=-1, keepdims=True)
+            dot_sums[r, :] += jnp.where(lane == e * here + j, dot, 0.0)
+            copy_buf[r, cols] = (gt * ct).astype(jnp.bfloat16)
+            return 0
+        lax.fori_loop(0, alltoks // 256 * 4, out, 0)
+        write(copy_buf, copies_out.at[j], 3)
+        free(0)
+        turned[0] = across(eye[...], act[...]).astype(jnp.bfloat16)
+        write(turned.at[0], act_t.at[j], 0)
+
+    def ffn_back(rows, count, w):
+        step = min(256, count)
+        def pre(m, _):
+            r = pl.ds(pl.multiple_of(m * step, step), step)
+            ga = across(rows[r, :], w(2))
+            g, u = gpre[r, :], upre[r, :]
+            s = jax.nn.sigmoid(g)
+            grad[0, r, :] = (ga * u * (s * (1.0 + g * (1.0 - s)))).astype(jnp.bfloat16)
+            grad[1, r, :] = (ga * (g * s)).astype(jnp.bfloat16)
+            return 0
+        lax.fori_loop(0, count // step, pre, 0)
+
+    def back_step(j):
+        ffn_back(copy_buf, alltoks, lambda a: weights[j % 2, a])
+        def out(k, _):
+            m, c = k // 4, k % 4
+            r = pl.ds(pl.multiple_of(m * 256, 256), 256)
+            cols = pl.ds(pl.multiple_of(c * 512, 512), 512)
+            back[r, cols] += (times(grad[0, r, :], weights[j % 2, 0, :, cols])
+                              + times(grad[1, r, :], weights[j % 2, 1, :, cols]))
+            return 0
+        lax.fori_loop(0, alltoks // 256 * 4, out, 0)
+        for q, dst in ((0, ggp_t), (1, gup_t)):
+            free(1 + q)
+            turned[1 + q] = across(eye[...], grad[q]).astype(jnp.bfloat16)
+            write(turned.at[1 + q], dst.at[j], 1 + q)
+
+    def shared_load(v):
+        cs = []
+        for a in range(3):
+            c = pltpu.make_async_copy(sh_land[a].at[pl.ds(v * hid, hid)], weights.at[v, a], load_sem.at[v, a])
+            c.start()
+            cs.append(c)
+        loads["s", v] = cs
+
+    def shared(v):
+        for c in loads.pop(("s", v)):
+            c.wait()
+        free(3)
+        w = lambda a: weights[v, a]
+        own = block(e)
+        ffn_front(normed, toks, w)
+        for c in range(4):
+            ffn_own[:, c * 512 : (c + 1) * 512] += times(act[0:toks, :], weights[v, 2, :, c * 512 : (c + 1) * 512])
+        sact_t[pl.ds(v * hid, hid), :] = across(eye[...], act[0:toks, :]).astype(jnp.bfloat16)
+        copy_buf[0:toks, :] = cot[own, :]
+        ffn_back(copy_buf, toks, w)
+        for c in range(4):
+            gn_own[:, c * 512 : (c + 1) * 512] += (
+                times(grad[0, 0:toks, :], weights[v, 0, :, c * 512 : (c + 1) * 512])
+                + times(grad[1, 0:toks, :], weights[v, 1, :, c * 512 : (c + 1) * 512]))
+        gsg[v] = grad[0, 0:toks, :]
+        gsu[v] = grad[1, 0:toks, :]
+
+    def settle():
+        for i in range(3):
+            pltpu.make_async_copy(sh_ins[i], sh_stage.at[i], stage_sem.at[i]).wait()
+            pltpu.make_async_copy(sh_stage.at[i], line_view(i, d, e), stage_sem.at[i]).start()
+        for i in range(3):
+            pltpu.make_async_copy(sh_stage.at[i], line_view(i, d, e), stage_sem.at[i]).wait()
+
+    def fold_start():
+        for k, p in enumerate(peers + [e]):
+            remote(back.at[block(p), theirs], fold_other.at[0, block(p)], pair_send.at[2 + k], pair_recv.at[2 + k], near["c"])
+            remote(dot_sums.at[block(p)], few_other.at[block(p)], pair_send.at[2 + n + k], pair_recv.at[2 + n + k], near["c"])
+        base = 2 + 2 * n
+        for k, p in enumerate(peers + [e]):
+            remote(routed.at[block(p), theirs], fold_other.at[1, block(p)], pair_send.at[base + k], pair_recv.at[base + k], near["c"])
+
+    def got(view, k):
+        remote(view, view, pair_send.at[k], pair_recv.at[k], near["c"], start=False).wait_recv()
+
+    def fold_shared():
+        base = 2 + 3 * n
+        for q, src in enumerate((gn_own, ffn_own)):
+            remote(src.at[:, theirs], fold_own.at[q], pair_send.at[base + q], pair_recv.at[base + q], near["c"])
+
+    def fold_lines():
+        for k, p in enumerate(peers):
+            got(fold_other.at[0, block(p)], 2 + k)
+            got(few_other.at[block(p)], 2 + n + k)
+            fold_out[0, k] = (back[block(p), mine] + fold_other[0, block(p), :]).astype(jnp.bfloat16)
+            few_out[k] = (dot_sums[block(p), :] + few_other[block(p), :]).astype(jnp.bfloat16)
+            remote(fold_out.at[0, k], fold_in.at[0, k], zsend.at[k], zrecv.at[k], {EXPERT: p})
+            remote(few_out.at[k], few_in.at[k], zsend.at[n - 1 + k], zrecv.at[n - 1 + k], {EXPERT: p})
+        for k, p in enumerate(peers):
+            got(fold_other.at[1, block(p)], 2 + 2 * n + k)
+            fold_out[1, k] = (routed[block(p), mine] + fold_other[1, block(p), :]).astype(jnp.bfloat16)
+            remote(fold_out.at[1, k], fold_in.at[1, k], zsend.at[2 * (n - 1) + k], zrecv.at[2 * (n - 1) + k], {EXPERT: p})
+
+    def fold_end():
+        for src, q, base in ((back, 0, 2), (routed, 1, 2 + 2 * n)):
+            got(fold_other.at[q, block(e)], base + n - 1)
+            got(fold_own.at[q], 2 + 3 * n + q)
+            dst, own = ((gn2, gn_own), (ffn, ffn_own))[q]
+            dst[:, mine] = (src[block(e), mine] + fold_other[q, block(e), :]) + (own[:, mine] + fold_own[q])
+        got(few_other.at[block(e)], 2 + n + n - 1)
+        few[...] = dot_sums[block(e), :] + few_other[block(e), :]
+        for k in range(n - 1):
+            s = n - 1 + k
+            remote(few_in.at[k], few_in.at[k], zsend.at[s], zrecv.at[s], near["c"], start=False).wait_recv()
+            few[...] += few_in[k].astype(F32)
+        for q, dst in ((0, gn2), (1, ffn)):
+            for k in range(n - 1):
+                s = 2 * (n - 1) * q + k
+                remote(fold_in.at[q, k], fold_in.at[q, k], zsend.at[s], zrecv.at[s], near["c"], start=False).wait_recv()
+                dst[:, mine] += fold_in[q, k].astype(F32)
+            s = 2 + 3 * n + 2 + q
+            remote(dst.at[:, mine], dst.at[:, mine], pair_send.at[s], pair_recv.at[s], near["c"])
+        for q, dst in ((0, gn2), (1, ffn)):
+            got(dst.at[:, theirs], 2 + 3 * n + 2 + q)
+
+    steps = {"join": join, "rows": rows_step, "gates": gates_step, "plane": plane_step, "line": line_step,
+             "load": load, "front": front, "back": back_step, "shared_load": shared_load, "shared": shared,
+             "settle": settle, "fold_start": fold_start, "fold_shared": fold_shared, "fold_lines": fold_lines,
+             "fold_end": fold_end}
+    items = middle_items(n, here)
+    for name, *args in [items[k] for k in order]:
+        steps[name](*args)
+    for k in list(waiting):
+        free(k)
+    for c, cond in sends:
+        when(cond, c.wait_send)
+
+
+def middle(part, inp, gain, router, named, cot, experts, shared_t, n, order, cid):
+    bf, dma, vm = jnp.bfloat16, pltpu.SemaphoreType.DMA, pltpu.VMEM
+    toks, width = inp.shape
+    here, hid, cut = experts[0].shape
+    al = n * toks
+    sh = shared_t[0].shape[0]
+    S = jax.ShapeDtypeStruct
+    vmem, anyspace = pl.BlockSpec(memory_space=pltpu.VMEM), pl.BlockSpec(memory_space=pl.ANY)
+    outs = [
+        (S((toks, width), F32), vmem), (S((toks, width), bf), vmem), (S((al, width), bf), vmem),
+        (S((toks, 128), F32), vmem), (S((toks, 128), F32), vmem), (S((toks, width), F32), vmem),
+        (S((toks, width), F32), vmem), (S((here, hid, al), bf), anyspace), (S((here, hid, al), bf), anyspace),
+        (S((here, hid, al), bf), anyspace), (S((here, al, width), bf), anyspace),
+        (S((2, toks, hid), bf), vmem), (S((2, toks, hid), bf), vmem), (S((2 * hid, toks), bf), vmem),
+    ] + [(S((here, hid, width), bf), anyspace)] * 3 + [(S((sh, width), bf), anyspace)] * 3
+    scratch = [
+        vm((toks, width), F32), vm((2, 3, hid, width), bf), vm((al, 128), F32), vm((al, width), F32),
+        vm((al, width), F32), vm((al, hid), F32), vm((al, hid), F32), vm((al, hid), bf), vm((2, al, hid), bf),
+        vm((al, width), bf), vm((3, hid, al), bf), vm((hid, hid), bf), vm((3, sh, 128), bf), vm((al, 128), F32),
+        vm((2, al, width // 2), F32), vm((2, toks, width // 2), F32), vm((2, n - 1, toks, width // 2), bf),
+        vm((2, n - 1, toks, width // 2), bf), vm((al, 128), F32), vm((n - 1, toks, 128), bf),
+        vm((n - 1, toks, 128), bf), vm((toks, width), F32), vm((toks, width), F32),
+        dma((6 + 3 * n,)), dma((6 + 3 * n,)), dma((2 * n,)), dma((2 * n,)), dma((90,)), dma((90,)),
+        dma((24 * (n - 1),)), dma((24 * (n - 1),)), dma((2, 12)), dma((4,)), dma((3,)),
+        dma((3 * (n - 1),)), dma((3 * (n - 1),)),
+    ]
+    res = pl.pallas_call(
+        functools.partial(middle_kernel, n, order),
+        out_shape=[s for s, _ in outs], out_specs=[b for _, b in outs],
+        in_specs=[vmem] * 6 + [anyspace] * 6,
+        scratch_shapes=scratch,
+        compiler_params=pltpu.CompilerParams(
+            collective_id=cid, has_side_effects=True, vmem_limit_bytes=67043328),
+    )(part, inp, gain, router, named, cot, *experts, *shared_t)
+    return res[:14]
 
 
 def rms_scale(vector):
@@ -701,6 +1153,74 @@
 def masked_scores(query_rot, key_rot, allowed):
     scores = dots(query_rot, key_rot, ((2,), (2,)), ((1,), (1,))) / math.sqrt(query_rot.shape[-1])
     return jnp.where(allowed[None], scores, masked_score)
+
+
+def turn(array, by, axis):
+    return lax.dynamic_slice_in_dim(
+        jnp.concatenate([array, array], axis=axis), by, array.shape[axis], axis=axis)
+
+
+def plain_middle(attn_part, input_f, gain_two, router_rows, named_all, grads_all, cotangent,
+                 expert_weights, full_sgate, full_sup, full_sdown):
+    here = lax.axis_index(EXPERT)
+    local_gate, local_up, local_down = expert_weights
+    experts_here = local_gate.shape[0]
+    hidden_one = input_f + lax.psum(attn_part, TENSOR)
+    normed_two = (hidden_one * rms_scale(hidden_one) * gain_two).astype(BF)
+    rows_all = lax.all_gather(normed_two, EXPERT, axis=0, tiled=True)
+    probs_all = jax.nn.softmax(dots(rows_all, router_rows, ((1,), (1,)), ((), ())), axis=-1)
+    gates_here = lax.dynamic_slice_in_dim(
+        probs_all * named_all, here * experts_here, experts_here, axis=1)
+    gate_pre = dots(local_gate, rows_all, ((2,), (1,)), ((), ()))
+    up_pre = dots(local_up, rows_all, ((2,), (1,)), ((), ()))
+    silu_gate, slope_gate = silu_parts(gate_pre)
+    act_t = (silu_gate * up_pre).astype(BF)
+    part_rows = dots(act_t, local_down, ((1,), (1,)), ((0,), (0,))).astype(BF).astype(F32)
+    routed = sum(gates_here[:, j : j + 1] * part_rows[j] for j in range(experts_here))
+    grads_wide = grads_all.astype(F32)
+    owner_grads = (jnp.transpose(gates_here)[:, :, None] * grads_wide[None]).astype(BF)
+    gate_dots = jnp.sum(part_rows * grads_wide[None], axis=-1)
+    dots_wide = lax.dynamic_update_slice(
+        jnp.zeros_like(probs_all), jnp.transpose(gate_dots), (0, here * experts_here))
+    grad_act = dots(local_down, owner_grads, ((2,), (2,)), ((0,), (0,)))
+    ggp_t = (grad_act * up_pre * slope_gate).astype(BF)
+    gup_t = (grad_act * silu_gate).astype(BF)
+    grad_rows = dots(ggp_t, local_gate, ((0, 1), (0, 1)), ((), ()))
+    grad_rows = grad_rows + dots(gup_t, local_up, ((0, 1), (0, 1)), ((), ()))
+    shared_gpre = jnp.dot(normed_two, full_sgate, preferred_element_type=F32)
+    shared_upre = jnp.dot(normed_two, full_sup, preferred_element_type=F32)
+    silu_shared, slope_shared = silu_parts(shared_gpre)
+    shared_act = (silu_shared * shared_upre).astype(BF)
+    shared_part = jnp.dot(shared_act, full_sdown, preferred_element_type=F32)
+    grad_sact = dots(cotangent, full_sdown, ((1,), (1,)), ((), ()))
+    grad_sgate = (grad_sact * shared_upre * slope_shared).astype(BF)
+    grad_sup = (grad_sact * silu_shared).astype(BF)
+    own_rows = dots(grad_sgate, full_sgate, ((1,), (1,)), ((), ()))
+    own_rows = own_rows + dots(grad_sup, full_sup, ((1,), (1,)), ((), ()))
+    back = [lax.psum_scatter(v, EXPERT, scatter_dimension=0, tiled=True)
+            for v in (grad_rows, routed, dots_wide)]
+    grad_normed_two = lax.psum(back[0] + own_rows, TENSOR)
+    ffn_total = lax.psum(back[1] + shared_part, TENSOR)
+    dots_sum = lax.psum(back[2], TENSOR)
+    router_probs = lax.dynamic_slice_in_dim(
+        probs_all, here * normed_two.shape[0], normed_two.shape[0], axis=0)
+    return (hidden_one, normed_two, rows_all, router_probs, dots_sum, grad_normed_two, ffn_total,
+            act_t, ggp_t, gup_t, owner_grads, grad_sgate, grad_sup, shared_act.T)
+
+
+def plain_scatter(dense, lefts, rights, extra, exp_left, rows_all, owner_grads):
+    sums = []
+    for k, ((kind, _), left, right) in enumerate(zip(dense, lefts, rights)):
+        part = jnp.dot(left, right, preferred_element_type=F32)
+        if k == len(dense) - 1:
+            part = part + extra
+        dim = 0 if kind == "rows" else 1
+        sums.append(lax.psum_scatter(part, BOTH, scatter_dimension=dim, tiled=True))
+    for left, right in zip(exp_left, (rows_all, rows_all, owner_grads)):
+        dims = (((2,), (0,)), ((), ())) if right.ndim == 2 else (((2,), (1,)), ((0,), (0,)))
+        part = dots(left, right, *dims).astype(BF)
+        sums.append(lax.psum_scatter(part, DP, scatter_dimension=2, tiled=True).astype(F32))
+    return sums
 
 
 def body(
@@ -722,60 +1242,52 @@
     routes,
     cotangent,
 ):
-    both = ("dp", "expert")
+    seq_len = block_input.shape[0]
+    total_experts = router_weight.shape[1]
+    owners, here = lax.axis_size(EXPERT), lax.axis_index(EXPERT)
+    kernels = (output_weight.shape[1] % 128 == 0 and lax.axis_size(DP) == 4
+               and total_experts <= 128 and seq_len == 128)
+    expert_ids = jnp.arange(total_experts, dtype=jnp.int32)
+    named = jnp.any(routes[:, :, None] == expert_ids[None, None, :], axis=1)
     small = jnp.concatenate([router_weight, attn_gain[:, None], ffn_gain[:, None]], axis=1).T
     flip_gate, flip_up = jnp.swapaxes(expert_gate, 1, 2), jnp.swapaxes(expert_up, 1, 2)
-    kernels = output_weight.shape[1] % 128 == 0 and lax.axis_size("dp") == 4
+    named_low = named.astype(BF)
     if kernels:
         small = jnp.pad(small, ((0, -small.shape[0] % 32), (0, 0)))
-        arrays = (query_weight, key_weight, value_weight, output_weight, small, cotangent,
-                  shared_gate, shared_up, shared_down, flip_gate, flip_up, expert_down)
-        forms = ("rows",) * 3 + ("cols", "cols", "tokens", "rows", "rows", "cols") + ("expert",) * 3
-        firsts = ("xy",) * 7 + ("z",) * 2 + ("xy",) * 3
-        (full_query, full_key, full_value, full_output, full_small, grads_all,
-         full_sgate, full_sup, full_sdown, local_gate, local_up, local_down) = gather(
-            arrays, forms, firsts, lax.axis_size("expert"), gather_starts)
+        named_low = jnp.pad(named_low, ((0, 0), (0, 256 - total_experts)))
+        arrays = (query_weight, key_weight, value_weight, output_weight, small, cotangent, named_low)
+        forms = ("rows",) * 3 + ("cols", "cols", "tokens", "tokens")
+        firsts = ("z",) * 3 + ("xy", "z", "xy", "xy")
+        (full_query, full_key, full_value, full_output, full_small, grads_all, named_all) = gather(
+            arrays, forms, firsts, owners, gather_starts)
     else:
-        full_small = lax.all_gather(small, both, axis=1, tiled=True)
-        full_query = lax.all_gather(query_weight, both, axis=0, tiled=True)
-        full_key = lax.all_gather(key_weight, both, axis=0, tiled=True)
-        full_value = lax.all_gather(value_weight, both, axis=0, tiled=True)
-        full_output = lax.all_gather(output_weight, both, axis=1, tiled=True)
-        full_sgate = lax.all_gather(shared_gate, both, axis=0, tiled=True)
-        full_sup = lax.all_gather(shared_up, both, axis=0, tiled=True)
-        full_sdown = lax.all_gather(shared_down, both, axis=1, tiled=True)
-        grads_all = lax.all_gather(cotangent, "expert", axis=0, tiled=True)
-        local_gate = lax.all_gather(flip_gate, "dp", axis=2, tiled=True)
-        local_up = lax.all_gather(flip_up, "dp", axis=2, tiled=True)
-        local_down = lax.all_gather(expert_down, "dp", axis=2, tiled=True)
-    seq_len = block_input.shape[0]
-    total_experts = router_weight.shape[1]
-    experts_here = expert_gate.shape[0]
-    owners = lax.axis_size("expert")
-    here = lax.axis_index("expert")
-    all_rows = owners * seq_len
+        full_small = lax.all_gather(small, BOTH, axis=1, tiled=True)
+        full_query = lax.all_gather(query_weight, BOTH, axis=0, tiled=True)
+        full_key = lax.all_gather(key_weight, BOTH, axis=0, tiled=True)
+        full_value = lax.all_gather(value_weight, BOTH, axis=0, tiled=True)
+        full_output = lax.all_gather(output_weight, BOTH, axis=1, tiled=True)
+        grads_all = lax.all_gather(cotangent, EXPERT, axis=0, tiled=True)
+        named_all = lax.all_gather(named_low, EXPERT, axis=0, tiled=True)
+    named_all = named_all[:, :total_experts]
     router_rows = full_small[:total_experts]
-    gain_attn = full_small[total_experts]
-    gain_ffn = full_small[total_experts + 1]
-    routes_all = lax.all_gather(routes, "expert", axis=0, tiled=True)
+    gain_one = full_small[total_experts].astype(F32)
+    gain_two = full_small[total_experts + 1].astype(F32)
     heads_here = full_query.shape[1] // HD
-    gain_one = gain_attn.astype(jnp.float32)
-    gain_two = gain_ffn.astype(jnp.float32)
-    input_f = block_input.astype(jnp.float32)
+    input_f = block_input.astype(F32)
     scale_one = rms_scale(input_f)
-    normed_one = (input_f * scale_one * gain_one).astype(jnp.bfloat16)
+    normed_one = (input_f * scale_one * gain_one).astype(BF)
     cosine, sine_table = rope_tables(seq_len, HD)
-    query_pre = jnp.dot(normed_one, full_query, preferred_element_type=jnp.float32).reshape(
+    query_pre = jnp.dot(normed_one, full_query, preferred_element_type=F32).reshape(
         seq_len, heads_here, HD
     )
-    key_pre = jnp.dot(normed_one, full_key, preferred_element_type=jnp.float32).reshape(
+    key_pre = jnp.dot(normed_one, full_key, preferred_element_type=F32).reshape(
         seq_len, heads_here, HD
     )
-    query_rot = rotate(query_pre, cosine, sine_table).astype(jnp.bfloat16)
-    key_rot = rotate(key_pre, cosine, sine_table).astype(jnp.bfloat16)
+    query_rot = rotate(query_pre, cosine, sine_table).astype(BF)
+    key_rot = rotate(key_pre, cosine, sine_table).astype(BF)
     value_rows = (
-        jnp.dot(normed_one, full_value, preferred_element_type=jnp.float32)
-        .astype(jnp.bfloat16)
+        jnp.dot(normed_one, full_value, preferred_element_type=F32)
+        .astype(BF)
         .reshape(seq_len, heads_here, HD)
     )
     position = jnp.arange(seq_len)
@@ -788,73 +1300,42 @@
     shifted = jnp.exp(scores - top_score)
     row_total = jnp.sum(shifted, axis=-1, keepdims=True)
     log_total = top_score + jnp.log(row_total)
-    prob_low = (shifted / row_total).astype(jnp.bfloat16)
+    prob_low = (shifted / row_total).astype(BF)
     mixed_rows = (
         jnp.transpose(dots(prob_low, value_rows, ((2,), (0,)), ((0,), (1,))), (1, 0, 2))
-        .astype(jnp.bfloat16)
+        .astype(BF)
         .reshape(seq_len, heads_here * HD)
     )
-    attn_part = jnp.dot(mixed_rows, full_output, preferred_element_type=jnp.float32)
-    attn_total = lax.psum(attn_part, "tensor")
-    hidden_one = input_f + attn_total
+    attn_part = jnp.dot(mixed_rows, full_output, preferred_element_type=F32)
+    experts = (flip_gate, flip_up, expert_down)
+    if kernels:
+        first = here * expert_gate.shape[0]
+        router_pad = jnp.pad(turn(router_rows, first, 0), ((0, 128 - total_experts), (0, 0)))
+        named_pad = jnp.pad(turn(named_all, first, 1), ((0, 0), (0, 128 - total_experts)))
+        (hidden_one, normed_two, rows_all, logits, dots_sum, grad_normed_two, ffn_total, act_t, ggp_t, gup_t,
+         owner_grads, grad_sgate, grad_sup, shared_act_t) = middle(
+            attn_part, block_input, gain_two[None], router_pad, named_pad, grads_all, experts,
+            (shared_gate.T, shared_up.T, shared_down), owners, middle_order, 2)
+        grad_sgate = jnp.concatenate([grad_sgate[0], grad_sgate[1]], axis=1)
+        grad_sup = jnp.concatenate([grad_sup[0], grad_sup[1]], axis=1)
+        router_probs = jax.nn.softmax(
+            turn(logits[:, :total_experts], total_experts - first, 1), axis=-1)
+        dots_sum = dots_sum[:, :total_experts]
+    else:
+        (hidden_one, normed_two, rows_all, router_probs, dots_sum, grad_normed_two, ffn_total, act_t, ggp_t, gup_t,
+         owner_grads, grad_sgate, grad_sup, shared_act_t) = plain_middle(
+            attn_part, input_f, gain_two, router_rows, named_all.astype(F32), grads_all, cotangent,
+            tuple(lax.all_gather(w, DP, axis=2, tiled=True) for w in experts),
+            lax.all_gather(shared_gate, BOTH, axis=0, tiled=True),
+            lax.all_gather(shared_up, BOTH, axis=0, tiled=True),
+            lax.all_gather(shared_down, BOTH, axis=1, tiled=True))
     scale_two = rms_scale(hidden_one)
-    normed_two = (hidden_one * scale_two * gain_two).astype(jnp.bfloat16)
-    rows_all = lax.all_gather(normed_two, "expert", axis=0, tiled=True)
-    logits = dots(rows_all, router_rows, ((1,), (1,)), ((), ()))
-    probs_all = jax.nn.softmax(logits, axis=-1)
-    expert_ids = jnp.arange(total_experts, dtype=jnp.int32)
-    named = jnp.any(routes_all[:, :, None] == expert_ids[None, None, :], axis=1)
-    gates_all = jnp.where(named, probs_all, 0.0)
-    gates_here = lax.dynamic_slice_in_dim(gates_all, here * experts_here, experts_here, axis=1)
-    gate_pre = jnp.transpose(dots(rows_all, local_gate, ((1,), (2,)), ((), ())), (1, 0, 2))
-    up_pre = jnp.transpose(dots(rows_all, local_up, ((1,), (2,)), ((), ())), (1, 0, 2))
-    silu_gate, slope_gate = silu_parts(gate_pre)
-    act_rows = (silu_gate * up_pre).astype(jnp.bfloat16)
-    part_rows = dots(act_rows, local_down, ((2,), (1,)), ((0,), (0,))).astype(jnp.bfloat16)
-    routed_all = sum(
-        gates_here[:, j : j + 1] * part_rows[j].astype(F32) for j in range(experts_here)
-    )
-    shared_gpre = jnp.dot(normed_two, full_sgate, preferred_element_type=jnp.float32)
-    shared_upre = jnp.dot(normed_two, full_sup, preferred_element_type=jnp.float32)
-    silu_shared, slope_shared = silu_parts(shared_gpre)
-    shared_act = (silu_shared * shared_upre).astype(jnp.bfloat16)
-    shared_part = jnp.dot(shared_act, full_sdown, preferred_element_type=jnp.float32)
-    routed_part = lax.psum_scatter(routed_all, "expert", scatter_dimension=0, tiled=True)
-    ffn_total = lax.psum(shared_part + routed_part, "tensor")
-    block_output = (hidden_one + ffn_total).astype(jnp.bfloat16)
-    grad_out = cotangent.astype(jnp.float32)
-    grad_sact = dots(cotangent, full_sdown, ((1,), (1,)), ((), ()))
-    grad_sgate = (grad_sact * shared_upre * slope_shared).astype(jnp.bfloat16)
-    grad_sup = (grad_sact * silu_shared).astype(jnp.bfloat16)
-    grad_normed_two = dots(grad_sgate, full_sgate, ((1,), (1,)), ((), ()))
-    grad_normed_two = grad_normed_two + dots(grad_sup, full_sup, ((1,), (1,)), ((), ()))
-    grads_wide = grads_all.astype(jnp.float32)
-    owner_grads = (jnp.transpose(gates_here)[:, :, None] * grads_wide[None]).astype(jnp.bfloat16)
-    grad_act = dots(owner_grads, local_down, ((2,), (2,)), ((0,), (0,)))
-    grad_gate_pre = (grad_act * up_pre * slope_gate).astype(jnp.bfloat16)
-    grad_up_pre = (grad_act * silu_gate).astype(jnp.bfloat16)
-    grad_rows = dots(grad_gate_pre, local_gate, ((0, 2), (0, 1)), ((), ()))
-    grad_rows = grad_rows + dots(grad_up_pre, local_up, ((0, 2), (0, 1)), ((), ()))
-    gate_dots = jnp.sum(part_rows.astype(jnp.float32) * grads_wide[None], axis=-1)
-    dots_wide = jnp.zeros((all_rows, total_experts), jnp.float32)
-    dots_wide = lax.dynamic_update_slice(
-        dots_wide, jnp.transpose(gate_dots), (0, here * experts_here)
-    )
-    rows_back = lax.psum_scatter(
-        jnp.concatenate([grad_rows, dots_wide], axis=1),
-        "expert", scatter_dimension=0, tiled=True,
-    )
-    rows_back = jnp.concatenate(
-        [rows_back[:, :D] + grad_normed_two, rows_back[:, D:]], axis=1)
-    rows_back = lax.psum(rows_back, "tensor")
-    grad_normed_two = rows_back[:, :D]
-    named_own = jnp.any(routes[:, :, None] == expert_ids[None, None, :], axis=1)
-    grad_rprobs = jnp.where(named_own, rows_back[:, D:], 0.0)
-    router_probs = lax.dynamic_slice_in_dim(probs_all, here * seq_len, seq_len, axis=0)
+    block_output = (hidden_one + ffn_total).astype(BF)
+    grad_out = cotangent.astype(F32)
+    grad_rprobs = jnp.where(named, dots_sum, 0.0)
     grad_logits = (
         router_probs * (grad_rprobs - jnp.sum(grad_rprobs * router_probs, axis=-1, keepdims=True))
-    ).astype(jnp.bfloat16)
-    router_full = dots(normed_two, grad_logits, ((0,), (0,)), ((), ()))
+    ).astype(BF)
     grad_normed_two = grad_normed_two + dots(grad_logits, router_rows, ((1,), (0,)), ((), ()))
     ffn_gain_full = jnp.sum(grad_normed_two * hidden_one * scale_two, axis=0)
     weighted_two = grad_normed_two * gain_two
@@ -864,20 +1345,20 @@
         + scale_two * weighted_two
         - hidden_one * cube_two * jnp.mean(hidden_one * weighted_two, axis=-1, keepdims=True)
     )
-    grad_attn = grad_hidden.astype(jnp.bfloat16)
+    grad_attn = grad_hidden.astype(BF)
     grad_mixed = (
         dots(grad_attn, full_output, ((1,), (1,)), ((), ()))
-        .astype(jnp.bfloat16)
+        .astype(BF)
         .reshape(seq_len, heads_here, HD)
     )
     prob_again = jnp.exp(masked_scores(query_rot, key_rot, allowed) - log_total)
     grad_probs = dots(grad_mixed, value_rows, ((2,), (2,)), ((1,), (1,)))
     grad_scores = (
         prob_again * (grad_probs - jnp.sum(prob_again * grad_probs, axis=-1, keepdims=True))
-    ).astype(jnp.bfloat16)
+    ).astype(BF)
     value_grad_rows = (
-        jnp.transpose(dots(prob_again.astype(jnp.bfloat16), grad_mixed, ((1,), (0,)), ((0,), (1,))), (1, 0, 2))
-        .astype(jnp.bfloat16)
+        jnp.transpose(dots(prob_again.astype(BF), grad_mixed, ((1,), (0,)), ((0,), (1,))), (1, 0, 2))
+        .astype(BF)
         .reshape(seq_len, heads_here * HD)
     )
     inverse_root = 1.0 / math.sqrt(HD)
@@ -890,19 +1371,17 @@
         * inverse_root
     )
     grad_qpre = (
-        unrotate(grad_qrot, cosine, sine_table)
-        .astype(jnp.bfloat16)
-        .reshape(seq_len, heads_here * HD)
+        unrotate(grad_qrot, cosine, sine_table).astype(BF).reshape(seq_len, heads_here * HD)
     )
     grad_kpre = (
-        unrotate(grad_krot, cosine, sine_table)
-        .astype(jnp.bfloat16)
-        .reshape(seq_len, heads_here * HD)
+        unrotate(grad_krot, cosine, sine_table).astype(BF).reshape(seq_len, heads_here * HD)
     )
     grad_normed_one = dots(grad_qpre, full_query, ((1,), (1,)), ((), ()))
     grad_normed_one = grad_normed_one + dots(grad_kpre, full_key, ((1,), (1,)), ((), ()))
     grad_normed_one = grad_normed_one + dots(value_grad_rows, full_value, ((1,), (1,)), ((), ()))
-    grad_normed_one = lax.psum(grad_normed_one.astype(jnp.bfloat16), "tensor").astype(jnp.float32)
+    grad_normed_one = (
+        pair_sum(grad_normed_one, 3) if kernels else lax.psum(grad_normed_one, TENSOR)
+    )
     attn_gain_full = jnp.sum(grad_normed_one * input_f * scale_one, axis=0)
     weighted_one = grad_normed_one * gain_one
     cube_one = scale_one * scale_one * scale_one
@@ -911,45 +1390,34 @@
         + scale_one * weighted_one
         - input_f * cube_one * jnp.mean(input_f * weighted_one, axis=-1, keepdims=True)
     )
-    small_full = jnp.concatenate(
-        [router_full, attn_gain_full[:, None], ffn_gain_full[:, None]], axis=1)
-    small_grad = lax.psum_scatter(small_full, both, scatter_dimension=0, tiled=True)
-    router_grad = small_grad[:, :total_experts]
-    attn_gain_grad = small_grad[:, total_experts]
-    ffn_gain_grad = small_grad[:, total_experts + 1]
+    room = total_experts + 2 + (-(total_experts + 2) % 64)
+    logits_t = jnp.pad(grad_logits.T, ((0, room - total_experts), (0, 0)))
+    extra = jnp.concatenate([
+        jnp.zeros((total_experts, D), F32), attn_gain_full[None], ffn_gain_full[None],
+        jnp.zeros((room - total_experts - 2, D), F32)])
     one_t, two_t = normed_one.T, normed_two.T
-    lefts = (one_t, one_t, one_t, mixed_rows.T, two_t, two_t, shared_act.T)
-    rights = (grad_qpre, grad_kpre, value_grad_rows, grad_attn, grad_sgate, grad_sup, cotangent)
-    exp_left = tuple(jnp.swapaxes(v, 1, 2) for v in (grad_gate_pre, grad_up_pre, act_rows))
-    dense = (("rows", "z"),) * 3 + (("cols", "z"), ("rows", "z"), ("rows", "p"), ("cols", "p"))
+    lefts = (one_t, one_t, one_t, mixed_rows.T, two_t, two_t, shared_act_t, logits_t)
+    rights = (grad_qpre, grad_kpre, value_grad_rows, grad_attn, grad_sgate, grad_sup, cotangent, normed_two)
+    exp_left = (ggp_t, gup_t, act_t)
+    dense = ((("rows", "z"),) * 3
+             + (("cols", "z"), ("rows", "z"), ("rows", "p"), ("cols", "p"), ("cols", "z")))
     if kernels:
-        (query_grad, key_grad, value_grad, output_grad, shared_gate_grad, shared_up_grad,
-         shared_down_grad, expert_gate_grad, expert_up_grad, expert_down_grad) = scatter(
-            dense, lefts, rights, exp_left, rows_all, owner_grads, owners, scatter_order, 1)
+        sums = scatter(
+            dense, lefts, rights, extra, exp_left, rows_all, owner_grads, owners, scatter_order, 1)
     else:
-        sums = []
-        for (kind, _), left, right in zip(dense, lefts, rights):
-            part = jnp.dot(left, right, preferred_element_type=F32)
-            dim = 0 if kind == "rows" else 1
-            sums.append(lax.psum_scatter(part, both, scatter_dimension=dim, tiled=True))
-        for left, right in zip(exp_left, (rows_all, rows_all, owner_grads)):
-            dims = (((2,), (0,)), ((), ())) if right.ndim == 2 else (((2,), (1,)), ((0,), (0,)))
-            part = lax.dot_general(left, right, dims, preferred_element_type=F32)
-            part = lax.psum_scatter(
-                part.astype(jnp.bfloat16), "dp", scatter_dimension=2, tiled=True)
-            sums.append(part.astype(F32))
-        (query_grad, key_grad, value_grad, output_grad, shared_gate_grad, shared_up_grad,
-         shared_down_grad, expert_gate_grad, expert_up_grad, expert_down_grad) = sums
+        sums = plain_scatter(dense, lefts, rights, extra, exp_left, rows_all, owner_grads)
+    (query_grad, key_grad, value_grad, output_grad, shared_gate_grad, shared_up_grad,
+     shared_down_grad, small_grad, expert_gate_grad, expert_up_grad, expert_down_grad) = sums
     return (
         block_output,
         input_grad,
-        attn_gain_grad,
+        small_grad[total_experts],
         query_grad,
         key_grad,
         value_grad,
         output_grad,
-        ffn_gain_grad,
-        router_grad,
+        small_grad[total_experts + 1],
+        small_grad[:total_experts].T,
         jnp.swapaxes(expert_gate_grad, 1, 2),
         jnp.swapaxes(expert_up_grad, 1, 2),
         expert_down_grad,
@@ -964,40 +1432,40 @@
         body,
         mesh=mesh,
         in_specs=(
-            P(("dp", "expert"), None),
-            P(("dp", "expert")),
-            P(("dp", "expert"), "tensor"),
-            P(("dp", "expert"), "tensor"),
-            P(("dp", "expert"), "tensor"),
-            P("tensor", ("dp", "expert")),
-            P(("dp", "expert")),
-            P(("dp", "expert"), None),
-            P("expert", "dp", "tensor"),
-            P("expert", "dp", "tensor"),
-            P("expert", "tensor", "dp"),
-            P(("dp", "expert"), "tensor"),
-            P(("dp", "expert"), "tensor"),
-            P("tensor", ("dp", "expert")),
-            P(("dp", "expert"), None),
-            P(("dp", "expert"), None),
-            P(("dp", "expert"), None),
+            P((DP, EXPERT), None),
+            P((DP, EXPERT)),
+            P((DP, EXPERT), TENSOR),
+            P((DP, EXPERT), TENSOR),
+            P((DP, EXPERT), TENSOR),
+            P(TENSOR, (DP, EXPERT)),
+            P((DP, EXPERT)),
+            P((DP, EXPERT), None),
+            P(EXPERT, DP, TENSOR),
+            P(EXPERT, DP, TENSOR),
+            P(EXPERT, TENSOR, DP),
+            P((DP, EXPERT), TENSOR),
+            P((DP, EXPERT), TENSOR),
+            P(TENSOR, (DP, EXPERT)),
+            P((DP, EXPERT), None),
+            P((DP, EXPERT), None),
+            P((DP, EXPERT), None),
         ),
         out_specs=(
-            P(("dp", "expert"), None),
-            P(("dp", "expert"), None),
-            P(("dp", "expert")),
-            P(("dp", "expert"), "tensor"),
-            P(("dp", "expert"), "tensor"),
-            P(("dp", "expert"), "tensor"),
-            P("tensor", ("dp", "expert")),
-            P(("dp", "expert")),
-            P(("dp", "expert"), None),
-            P("expert", "dp", "tensor"),
-            P("expert", "dp", "tensor"),
-            P("expert", "tensor", "dp"),
-            P(("dp", "expert"), "tensor"),
-            P(("dp", "expert"), "tensor"),
-            P("tensor", ("dp", "expert")),
+            P((DP, EXPERT), None),
+            P((DP, EXPERT), None),
+            P((DP, EXPERT)),
+            P((DP, EXPERT), TENSOR),
+            P((DP, EXPERT), TENSOR),
+            P((DP, EXPERT), TENSOR),
+            P(TENSOR, (DP, EXPERT)),
+            P((DP, EXPERT)),
+            P((DP, EXPERT), None),
+            P(EXPERT, DP, TENSOR),
+            P(EXPERT, DP, TENSOR),
+            P(EXPERT, TENSOR, DP),
+            P((DP, EXPERT), TENSOR),
+            P((DP, EXPERT), TENSOR),
+            P(TENSOR, (DP, EXPERT)),
         ),
         check_vma=False,
     )

time: 1390 us -> 1150 us (0.83)
  waiting for transfers between devices: 182 us -> 0 us
  matrix products: 156 us -> 20.3 us
  Pallas kernels: 919 us -> 1050 us
  other arithmetic: 40.7 us -> 23.4 us
    pallas_call x0 -> x2, Pallas kernels: none -> 419 us  [the longest x1 414 us: middle(): pl.pallas_call(functools.partial(middle_kernel, n, order), out_shape=[s f...]
    pallas_call x1, Pallas kernels: 436 us -> 144 us  [gather(): pl.pallas_call(functools.partial(gather_kernel, leaves, n, starts), out_s...]
    dot_general x22 -> x11, matrix products: 135 us -> 14.1 us  [dots(): return lax.dot_general(left, right, dims, preferred_element_type=F32)]
    reduce_scatter x3 -> x0, waiting for transfers between devices: 107 us -> none  [the longest x1 79.2 us: body(): lax.psum_scatter(jnp.concatenate([grad_rows, dots_wide], axis=1), 'expert...]
    psum x3 -> x0, waiting for transfers between devices: 45.7 us -> none  [the longest x1 22.1 us: body(): attn_total = lax.psum(attn_part, 'tensor')]
    all_gather x1 -> x0, waiting for transfers between devices: 29.1 us -> none  [body(): rows_all = lax.all_gather(normed_two, 'expert', axis=0, tiled=True)]
    dot_general x7 -> x4, matrix products: 21.2 us -> 6.24 us  [the longest x1 2.95 us: body(): jnp.dot(normed_one, full_value, preferred_element_type=F32).astype(BF)]
    unnamed x131 -> x106, local copies, waits for them, and re-layouts: 40.5 us -> 29 us
  transfers between devices with their start and end apart: 7 -> 0, of which waited for: 6 -> 0; matrix products, arithmetic and copies ran while one was open for 6% -> 0% of each run, Pallas kernels for 35% -> 0%
where the time goes in v2:
time: 1150 us; the launch traced here: 1140 us
  Pallas kernels  1050 us (91%)
  local copies, waits for them, and re-layouts  44.8 us (4%)
  other arithmetic  23.4 us (2%)
  matrix products  20.3 us (2%)
    pallas_call x1, Pallas kernels, scatter(): pl.pallas_call(functools.partial(scatter_kernel, dense, units, n, order),...  490 us
    pallas_call x1, Pallas kernels, middle(): pl.pallas_call(functools.partial(middle_kernel, n, order), out_shape=[s f...  414 us
    pallas_call x1, Pallas kernels, gather(): pl.pallas_call(functools.partial(gather_kernel, leaves, n, starts), out_s...  144 us
    unnamed x106, local copies, waits for them, and re-layouts  29 us

profile of v2, /device:TPU:16, one launch (start us, length us, event | category | flops | bytes accessed | tf_op | source)
XLA Modules:
  0.0 1142.5 jit_solution(17189718848932768108)
XLA Ops:
  7.6 1.9 copy.98
  9.5 1.9 copy.99
  11.4 143.9 %shard_map.280 = (bf16[2048,1024]{1,0:T(8,128)(2,1)}, bf16[2048,1024]{1,0:T(8,128)(2,1)}, bf16[2048,1024]{1,0:T(8,128)(2,1)}, bf16[1024,2048]{1,0:T(8,128)(2,1)}...) custom-call(bf16[128,1024]{1,0:T(8,128)(2,1)} %refs_0_.1, ...), custom_call_target="tpu_custom_call" | custom-call | tf_op jit(solution)/shard_map/pallas_call | solution.py:238
  159.6 3.0 fusion.3
  169.6 1.7 fusion.46.refs_0_
  171.3 413.5 %shard_map.281 = (f32[128,2048]{1,0:T(8,128)}, bf16[128,2048]{1,0:T(8,128)(2,1)}, bf16[512,2048]{1,0:T(8,128)(2,1)}, f32[128,128]{1,0:T(8,128)}, f32[128,128]{1,...) custom-call(f32[128,2048]{1,0:T(8,128)} %fusion.46.refs_0_, ...), custom_call_target="tpu_custom_call" | custom-call | tf_op jit(solution)/shard_map/pallas_call | solution.py:1096
  589.7 2.3 multiply_reduce_fusion
  592.0 2.4 fusion.40
  594.5 1.5 convolution_convert_fusion.2
  599.3 1.7 multiply_reduce_fusion.3
  602.5 1.5 fusion.35
  604.2 1.5 convolution_add_fusion.1
  606.3 2.5 convolution_add_fusion.part
  609.6 5.0 shard_map.282
  615.5 2.1 fusion.11
  617.6 2.8 fusion.36
  626.9 490.0 %shard_map.283 = (f32[128,1024]{1,0:T(8,128)}, f32[128,1024]{1,0:T(8,128)}, f32[128,1024]{1,0:T(8,128)}, f32[1024,128]{1,0:T(8,128)}, f32[128,1408]{1,0:T(8,128)...) custom-call(bf16[2048,128]{1,0:T(8,128)(2,1)} %copy.115.refs_0_.refs, ...), custom_call_target="tpu_custom_call" | custom-call | tf_op jit(solution)/shard_map/pallas_call | solution.py:642
  1119.5 1.9 copy.167
  1121.4 1.9 copy.168
  1123.3 1.9 copy.169
  1125.1 1.9 copy.170
  1127.0 6.4 copy.171
  1133.4 2.7 copy.172
  1137.0 2.7 copy.173
  (157 shorter events, 42.4 us)
Async XLA Ops:
  0.6 158.9 %copy-start = (bf16[128,2048]{1,0:T(8,128)(2,1)S(1)}, bf16[128,2048]{1,0:T(8,128)(2,1)}, u32[]{:S(2)}) copy-start(bf16[128,2048]{1,0:T(8,128)(2,1)} %refs_1_.3) | copy-start | bytes 1572868
  3.6 160.7 %copy-start.40 = (f32[128]{0:T(128)}, f32[128]{0:T(128)S(1)}, u32[]{:S(2)}) copy-start(f32[128]{0:T(128)S(1)} %get-tuple-element.115) | copy-start | bytes 1540
  7.5 158.7 %copy-start.29 = (f32[128,64]{1,0:T(8,128)}, f32[128,64]{1,0:T(8,128)S(1)}, u32[]{:S(2)}) copy-start(f32[128,64]{1,0:T(8,128)S(1)} %get-tuple-element.118) | copy-start | bytes 98308
  7.5 158.7 %copy-start.31 = (f32[128,64]{1,0:T(8,128)}, f32[128,64]{1,0:T(8,128)S(1)}, u32[]{:S(2)}) copy-start(f32[128,64]{1,0:T(8,128)S(1)} %get-tuple-element.119) | copy-start | bytes 98308
  155.3 8.1 copy-start.7
  158.7 5.7 copy-start.34
  162.5 5.7 copy-start.25
  584.8 7.2 copy-start.11
  584.8 7.2 copy-start.13
  584.9 7.2 copy-start.36
  594.5 6.8 copy-start.14
  594.5 6.8 copy-start.20
  594.5 6.8 copy-start.22
  594.5 7.2 copy-start.16
  594.5 7.2 copy-start.18
  596.1 5.9 copy-start.30
  596.1 5.9 copy-start.32
  606.2 9.2 copy-start.1
  606.3 9.2 copy-start.35
  606.3 9.2 copy-start.41
  617.6 6.6 copy-start.33
  617.6 8.4 copy-start.23
  1127.0 6.4 copy-start.12
  1127.0 9.2 slice-start
  (22 other events, 65.9 us)

commit v3 on v2

--- a/solution.py
+++ b/solution.py
@@ -19,9 +19,9 @@
 epsilon = 1e-06
 rope_base = 10000.0
 masked_score = -1e30
-gather_starts = (1.91, 2.48, 3.88, 2.78, 2.0, 1.0, 1.1)
-scatter_order = (46, 77, 72, 73, 18, 10, 11, 93, 97, 98, 19, 54, 9, 83, 45, 36, 38, 82, 79, 20, 92, 99, 28, 55, 37, 12, 48, 30, 74, 56, 87, 27, 47, 75, 39, 88, 100, 14, 0, 63, 29, 13, 85, 78, 1, 64, 21, 41, 16, 57, 84, 40, 49, 95, 3, 66, 80, 58, 23, 43, 2, 65, 101, 31, 42, 94, 76, 51, 32, 59, 86, 22, 25, 50, 33, 96, 5, 68, 44, 61, 4, 67, 15, 60, 24, 52, 34, 89, 90, 6, 69, 17, 26, 81, 53, 62, 35, 7, 70, 91, 8, 71)
-middle_order = (49, 25, 26, 27, 33, 37, 45, 46, 5, 34, 50, 6, 35, 99, 7, 8, 21, 47, 53, 48, 57, 84, 100, 101, 13, 69, 17, 18, 70, 80, 88, 0, 1, 36, 102, 73, 51, 52, 38, 39, 89, 29, 30, 65, 61, 74, 114, 28, 41, 42, 43, 66, 129, 85, 81, 82, 9, 10, 11, 12, 95, 71, 72, 103, 40, 31, 32, 90, 91, 22, 19, 20, 44, 115, 23, 24, 75, 76, 62, 2, 118, 67, 68, 77, 3, 4, 78, 79, 54, 55, 56, 86, 87, 63, 64, 96, 97, 104, 110, 14, 15, 83, 92, 93, 94, 16, 119, 58, 59, 60, 105, 106, 116, 111, 98, 107, 108, 109, 125, 117, 112, 120, 113, 121, 122, 123, 124, 126, 130, 127, 131, 128, 132, 133)
+gather_starts = (1.91, 2.48, 3.88, 2.78, 2.0, 1.0)
+scatter_order = (97, 98, 73, 45, 9, 55, 2, 65, 72, 19, 100, 82, 1, 64, 46, 99, 39, 83, 54, 36, 78, 18, 38, 92, 75, 74, 37, 11, 87, 56, 77, 93, 10, 12, 47, 0, 63, 85, 94, 57, 3, 66, 84, 80, 27, 20, 41, 14, 28, 79, 13, 21, 5, 68, 40, 101, 29, 16, 43, 15, 22, 4, 67, 42, 88, 30, 48, 86, 95, 61, 17, 81, 76, 6, 69, 44, 58, 23, 7, 70, 89, 49, 90, 60, 31, 50, 96, 25, 32, 24, 8, 71, 51, 59, 52, 91, 34, 33, 26, 53, 62, 35)
+middle_order = (13, 8, 33, 113, 0, 9, 10, 14, 15, 57, 53, 91, 73, 37, 58, 59, 34, 35, 17, 18, 11, 12, 92, 19, 54, 55, 61, 77, 16, 3, 109, 99, 114, 81, 65, 66, 21, 25, 74, 67, 62, 36, 26, 27, 56, 69, 95, 100, 101, 82, 29, 30, 31, 93, 4, 115, 116, 110, 111, 20, 96, 97, 78, 28, 22, 23, 24, 94, 41, 63, 117, 5, 6, 7, 1, 68, 75, 76, 112, 98, 103, 32, 83, 84, 86, 60, 2, 70, 71, 72, 64, 102, 104, 127, 45, 42, 131, 38, 79, 80, 85, 87, 88, 89, 90, 105, 118, 135, 39, 40, 46, 49, 43, 128, 129, 106, 107, 108, 47, 121, 123, 44, 132, 119, 120, 122, 124, 125, 126, 136, 137, 50, 51, 52, 133, 134, 130, 139, 141, 48, 145, 138, 140, 142, 151, 143, 152, 144, 147, 146, 148, 149, 150, 153, 154)
 
 
 class Leaf:
@@ -75,9 +75,10 @@
 
 def gather_kernel(leaves, n, starts, *refs):
     m = len(leaves)
-    ins, outs = refs[:m], refs[m : 2 * m]
-    stages = refs[2 * m : 3 * m]
-    in_sem, out_sem, send_sem, recv_sem = refs[3 * m :]
+    ins, plain, refs = refs[:m], refs[m : m + 2], refs[m + 2 :]
+    outs, turned, refs = refs[:m], refs[m : m + 2], refs[m + 2 :]
+    stages = refs[:m]
+    in_sem, out_sem, send_sem, recv_sem = refs[m:]
     d, e, t = lax.axis_index(DP), lax.axis_index(EXPERT), lax.axis_index(TENSOR)
     dx = d + 1 - 2 * lax.rem(d, 2)
     dy = lax.rem(d + 2, 4)
@@ -208,6 +209,8 @@
                 plane(i, e + k, at + k + 0.5, ("pl", k), e + k < n, False)
 
     def settle():
+        for a, b in zip(plain, turned):
+            b[...] = a[...].astype(F32).T.astype(b.dtype)
         for i in range(m):
             pltpu.make_async_copy(ins[i], stages[i], in_sem.at[i]).wait()
             pltpu.make_async_copy(stages[i], leaves[i].view(outs[i], d, e), out_sem.at[i]).start()
@@ -224,7 +227,7 @@
     assert len(table) <= recv_sem.shape[0], len(table)
 
 
-def gather(arrays, forms, firsts, n, starts):
+def gather(arrays, forms, firsts, n, starts, plain):
     leaves = [Leaf(a.shape, a.dtype, f, o, n) for a, f, o in zip(arrays, forms, firsts)]
     total = 0
     for leaf in leaves:
@@ -234,22 +237,23 @@
             continue
         total += plane if leaf.form == "expert" else plane + 4 * line if leaf.first == "xy" else plane * (2 * n - 1) + line
     m = len(leaves)
-    anyspace = pl.BlockSpec(memory_space=pl.ANY)
+    anyspace, vmem = pl.BlockSpec(memory_space=pl.ANY), pl.BlockSpec(memory_space=pltpu.VMEM)
     return pl.pallas_call(
         functools.partial(gather_kernel, leaves, n, starts),
-        out_shape=[jax.ShapeDtypeStruct(leaf.out, leaf.dtype) for leaf in leaves],
-        in_specs=[anyspace] * m,
-        out_specs=[anyspace] * m,
+        out_shape=[jax.ShapeDtypeStruct(leaf.out, leaf.dtype) for leaf in leaves] + [
+            jax.ShapeDtypeStruct(v.shape[::-1], v.dtype) for v in plain],
+        in_specs=[anyspace] * m + [vmem] * 2,
+        out_specs=[anyspace] * m + [vmem] * 2,
         scratch_shapes=[pltpu.VMEM(leaf.shape, leaf.dtype) for leaf in leaves] + [
             pltpu.SemaphoreType.DMA((m,)), pltpu.SemaphoreType.DMA((m,)),
             pltpu.SemaphoreType.DMA((total,)), pltpu.SemaphoreType.DMA((total,))],
         compiler_params=pltpu.CompilerParams(
             collective_id=0, has_side_effects=True, vmem_limit_bytes=60 << 20),
-    )(*arrays)
+    )(*arrays, *plain)
 
 
 message_rows = 5632
-ring_slots = {"x": 3, "y": 3, "z": 4}
+ring_slots = {"x": 4, "y": 4, "z": 6}
 
 
 def scatter_items(dense, units, n):
@@ -265,12 +269,30 @@
     return items
 
 
-def scatter_kernel(dense, units, n, order, *refs):
+def scatter_kernel(dense, units, n, order, which, *refs):
     m = len(dense)
-    lefts, rights = refs[:m], refs[m : 2 * m]
-    exp_left = refs[2 * m : 2 * m + 3]
-    rows_all, grads_in, extra = refs[2 * m + 3 : 2 * m + 6]
-    refs = refs[2 * m + 6 :]
+    u_ = max(which) + 1
+    given, refs = refs[:u_], refs[u_:]
+    held_in, refs = refs[-u_ - 1 : -1], refs[: -u_ - 1] + refs[-1:]
+    in_sem, refs = refs[-1], refs[:-1]
+    seat = [held_in[w] for w in which]
+    lefts, rights = seat[:m], seat[m : 2 * m]
+    exp_left = seat[2 * m : 2 * m + 3]
+    rows_all, grads_in, extra = seat[2 * m + 3 : 2 * m + 6]
+    here_yet = set()
+
+    def need(*numbers):
+        for k in numbers:
+            w = which[k]
+            if w not in here_yet:
+                here_yet.add(w)
+                pltpu.make_async_copy(given[w], held_in[w], in_sem.at[w]).wait()
+
+    first_use = [k for it in ([scatter_items(dense, units, n)[o] for o in order] if order else scatter_items(dense, units, n))
+                 for k in ((it[1], m + it[1]) + ((2 * m + 5,) if it[1] == m - 1 else ()) if it[0] == "d"
+                           else (2 * m + it[1] // 2, 2 * m + 3 + (it[1] // 2 == 2)))]
+    for w in dict.fromkeys(which[k] for k in first_use):
+        pltpu.make_async_copy(given[w], held_in[w], in_sem.at[w]).start()
     outs, refs = refs[: m + 3], refs[m + 3 :]
     landed, refs = refs[: 3 * m + 2], refs[3 * m + 2 :]
     bufs = dict(zip("xyz", refs[:3]))
@@ -400,6 +422,9 @@
             out_busy.pop(which).wait()
 
     def dense_step(i, stage, arg):
+        need(i, m + i)
+        if i == m - 1:
+            need(2 * m + 5)
         z_land, first_land, second_land = landed[3 * i : 3 * i + 3]
         z_first = dense[i][1] == "z"
         hb = half_rows_of(i)
@@ -538,6 +563,7 @@
 
     def expert_step(u, stage, s):
         a, q = u // 2, u % 2
+        need(2 * m + a, 2 * m + 3 + (a == 2))
         rows, width = exp_left[a].shape[1], outs[m + a].shape[2]
         tiles = width // 128
         piece = rows * tiles
@@ -637,12 +663,15 @@
     piece = rows * width // 128
     landed += [jax.ShapeDtypeStruct((units, 2, 2 * piece, 128), bf),
                jax.ShapeDtypeStruct((units, 2, piece, 128), bf)]
-    anyspace, vmem = pl.BlockSpec(memory_space=pl.ANY), pl.BlockSpec(memory_space=pltpu.VMEM)
+    anyspace = pl.BlockSpec(memory_space=pl.ANY)
     count = m * (2 * n + 4) + 4 * units
+    taken = [*lefts, *rights, *exp_left, rows_all, grads_in, extra]
+    single = list({id(v): v for v in taken}.values())
+    which = tuple([id(v) for v in single].index(id(v)) for v in taken)
     res = pl.pallas_call(
-        functools.partial(scatter_kernel, dense, units, n, order),
+        functools.partial(scatter_kernel, dense, units, n, order, which),
         out_shape=outs + landed,
-        in_specs=[vmem] * (2 * m + 6),
+        in_specs=[anyspace] * len(single),
         out_specs=[anyspace] * (len(outs) + len(landed)),
         scratch_shapes=[pltpu.VMEM((ring_slots[s], message_rows, 128), bf) for s in "xyz"] + [
             pltpu.VMEM((4, message_rows, 128), bf),
@@ -650,10 +679,11 @@
             pltpu.VMEM((128, max(o.shape[1] for o in outs[:m])), F32),
             pltpu.SemaphoreType.DMA((3,)), pltpu.SemaphoreType.DMA((8,)),
             pltpu.SemaphoreType.DMA((count,)),
-        ] + [pltpu.SemaphoreType.DMA((ring_slots[s],)) for s in "xyz"],
+        ] + [pltpu.SemaphoreType.DMA((ring_slots[s],)) for s in "xyz"] + [
+            pltpu.VMEM(v.shape, v.dtype) for v in single] + [pltpu.SemaphoreType.DMA((len(single),))],
         compiler_params=pltpu.CompilerParams(
-            collective_id=cid, has_side_effects=True, vmem_limit_bytes=60 << 20),
-    )(*lefts, *rights, *exp_left, rows_all, grads_in, extra)
+            collective_id=cid, has_side_effects=True, vmem_limit_bytes=67043328),
+    )(*single)
     return res[: m + 3]
 
 
@@ -702,33 +732,33 @@
 
 
 def middle_items(n, here):
-    items = [("join",)]
-    for k in range(1, n):
-        items.append(("rows", k))
-    items.append(("gates",))
+    items = [("join",), ("gates",), ("settle",)]
+    for q in range(2):
+        items += [("tok", q, k) for k in range(n)] + [("tokend", q)]
     for i in range(3):
         items += [("plane", 12 + i, s) for s in range(4)]
         items += [("line", i, b, k) for b in range(4) for k in range(n)]
     for j in range(here):
         for a in range(3):
             items += [("plane", 3 * j + a, s) for s in range(4)]
-        items += [("load", j), ("front", j), ("back", j)]
-    items += [("shared_load", v) for v in range(2)] + [("shared", v) for v in range(2)]
-    return items + [("settle",), ("fold_start",), ("fold_lines",), ("fold_shared",), ("fold_end",)]
+        items += [(name, j) for name in ("load", "load_down", "pre", "front", "back", "rows")]
+    for v in range(2):
+        items += [("shared_load", v), ("shared", v), ("fold_start", v), ("fold_lines", v)]
+    return items + [("fold_shared",), ("fold_end",)]
 
 
 def middle_kernel(n, order, *refs):
-    (part, inp, gain, router, named, cot, gate_in, up_in, down_in, sg_in, su_in, sd_in) = refs[:12]
-    refs = refs[12:]
+    (part, inp, gain, router, named, cot_own, one, mixed, gate_in, up_in, down_in, sg_in, su_in, sd_in) = refs[:14]
+    refs = refs[14:]
     (hidden, normed, rows_all, probs, few, gn2, ffn, act_t, ggp_t, gup_t, copies_out,
-     gsg, gsu, sact_t) = refs[:14]
-    exp_land, sh_land = refs[14:17], refs[17:20]
-    refs = refs[20:]
+     gsg, gsu, sact_t, one_t, two_t, mixed_t) = refs[:17]
+    exp_land, sh_land = refs[17:20], refs[20:23]
+    refs = refs[23:]
     (other, weights, gates, back, routed, gpre, upre, act, grad, copy_buf, turned, eye,
      sh_stage, dot_sums, fold_other, fold_own, fold_out, fold_in, few_other, few_out, few_in,
-     ffn_own, gn_own) = refs[:23]
+     ffn_own, gn_own, cot) = refs[:24]
     (pair_send, pair_recv, row_send, row_recv, plane_send, plane_recv, line_send, line_recv,
-     load_sem, out_sem, stage_sem, zsend, zrecv) = refs[23:]
+     load_sem, out_sem, stage_sem, zsend, zrecv) = refs[24:]
     ins = (gate_in, up_in, down_in)
     sh_ins = (sg_in, su_in, sd_in)
     here, hid, width = gate_in.shape
@@ -787,20 +817,41 @@
             rows = (h * scale * gain[...]).astype(jnp.bfloat16)
             normed[p, :] = rows
             rows_all[pl.ds(pl.multiple_of(e * toks + k * (toks // 2), toks // 2), toks // 2), :] = rows
-        for k, p in enumerate(peers):
-            remote(normed.at[:, mine], rows_all.at[block(e), mine], row_send.at[k], row_recv.at[k], {EXPERT: p})
-
-    def rows_step(k):
-        o = lax.rem(e + n - k, n)
-        view = rows_all.at[block(o), mine]
-        remote(view, view, row_send.at[k - 1], row_recv.at[k - 1], near["c"], start=False).wait_recv()
-        remote(view, view, row_send.at[n - 1 + k - 1], row_recv.at[n - 1 + k - 1], near["c"])
+        two_t[...] = normed[...].astype(F32).T.astype(jnp.bfloat16)
+
+    def along(k):
+        return (("r", e - k, e >= k, after, 0), ("l", e + k, e + k < n, before, 1))
+
+    def tok_step(q, k):
+        every = (rows_all, cot)[q]
+        base = 4 * (n - 1) * q
+        if k == 0:
+            src = (normed, cot_own)[q]
+            for side, has, w in (("r", after, 0), ("l", before, 1)):
+                s = base + (n - 1) * w
+                remote(src.at[:, mine], every.at[block(e), mine], row_send.at[s], row_recv.at[s], near[side], has)
+            return
+        for side, o, there, has, w in along(k):
+            view = every.at[block(o), mine]
+            s = base + (n - 1) * w + k - 1
+            when(there, remote(view, view, row_send.at[s], row_recv.at[s], near[side], start=False).wait_recv)
+            if k < n - 1:
+                remote(view, view, row_send.at[s + 1], row_recv.at[s + 1], near[side], jnp.logical_and(there, has))
+            s += 2 * (n - 1)
+            remote(view, view, row_send.at[s], row_recv.at[s], near["c"], there)
+
+    def tok_end(q):
+        every = (rows_all, cot)[q]
+        for k in range(1, n):
+            for side, o, there, has, w in along(k):
+                view = every.at[block(o), theirs]
+                s = 4 * (n - 1) * q + (n - 1) * (2 + w) + k - 1
+                when(there, remote(view, view, row_send.at[s], row_recv.at[s], near["c"], start=False).wait_recv)
 
     def gates_step():
-        for k in range(1, n):
-            o = lax.rem(e + n - k, n)
-            view = rows_all.at[block(o), theirs]
-            remote(view, view, row_send.at[n - 1 + k - 1], row_recv.at[n - 1 + k - 1], near["c"], start=False).wait_recv()
+        cot[block(e), :] = cot_own[...]
+        one_t[...] = one[...].astype(F32).T.astype(jnp.bfloat16)
+        mixed_t[...] = mixed[...].astype(F32).T.astype(jnp.bfloat16)
         logits = across(rows_all[...], router[...])
         lane = lax.broadcasted_iota(jnp.int32, logits.shape, 1)
         logits = jnp.where(lane < 4 * n, logits, -1e30)
@@ -881,16 +932,19 @@
 
     loads = {}
 
-    def load(j):
+    def load(j, arrays=(0, 1)):
         cs = []
-        for a in range(3):
+        for a in arrays:
             for q, o in enumerate((d, dx, dy, dd)):
                 cols = pl.ds(pl.multiple_of(o * width, width), width)
                 src = ins[a].at[j] if q == 0 else exp_land[a].at[j, :, cols]
                 c = pltpu.make_async_copy(src, weights.at[j % 2, a, :, cols], load_sem.at[j % 2, 4 * a + q])
                 c.start()
                 cs.append(c)
-        loads[j] = cs
+        loads[j, arrays] = cs
+
+    def load_down(j):
+        load(j, (2,))
 
     writes = []
     waiting = {}
@@ -917,11 +971,14 @@
             return 0
         lax.fori_loop(0, count // step, pre, 0)
 
+    def pre_step(j):
+        for c in loads.pop((j, (0, 1))):
+            c.wait()
+        ffn_front(rows_all, alltoks, lambda a: weights[j % 2, a])
+
     def front(j):
-        for c in loads.pop(j):
+        for c in loads.pop((j, (2,))):
             c.wait()
-        w = lambda a: weights[j % 2, a]
-        ffn_front(rows_all, alltoks, w)
         free(3)
         lane = lax.broadcasted_iota(jnp.int32, (256, 128), 1)
         def out(k, _):
@@ -956,6 +1013,8 @@
 
     def back_step(j):
         ffn_back(copy_buf, alltoks, lambda a: weights[j % 2, a])
+
+    def rows_step(j):
         def out(k, _):
             m, c = k // 4, k % 4
             r = pl.ds(pl.multiple_of(m * 256, 256), 256)
@@ -1003,13 +1062,13 @@
         for i in range(3):
             pltpu.make_async_copy(sh_stage.at[i], line_view(i, d, e), stage_sem.at[i]).wait()
 
-    def fold_start():
+    def fold_start(q):
+        src, base = ((back, 2), (routed, 2 + 2 * n))[q]
         for k, p in enumerate(peers + [e]):
-            remote(back.at[block(p), theirs], fold_other.at[0, block(p)], pair_send.at[2 + k], pair_recv.at[2 + k], near["c"])
-            remote(dot_sums.at[block(p)], few_other.at[block(p)], pair_send.at[2 + n + k], pair_recv.at[2 + n + k], near["c"])
-        base = 2 + 2 * n
-        for k, p in enumerate(peers + [e]):
-            remote(routed.at[block(p), theirs], fold_other.at[1, block(p)], pair_send.at[base + k], pair_recv.at[base + k], near["c"])
+            remote(src.at[block(p), theirs], fold_other.at[q, block(p)], pair_send.at[base + k], pair_recv.at[base + k], near["c"])
+            if q == 1:
+                s = 2 + n + k
+                remote(dot_sums.at[block(p)], few_other.at[block(p)], pair_send.at[s], pair_recv.at[s], near["c"])
 
     def got(view, k):
         remote(view, view, pair_send.at[k], pair_recv.at[k], near["c"], start=False).wait_recv()
@@ -1019,18 +1078,18 @@
         for q, src in enumerate((gn_own, ffn_own)):
             remote(src.at[:, theirs], fold_own.at[q], pair_send.at[base + q], pair_recv.at[base + q], near["c"])
 
-    def fold_lines():
+    def fold_lines(q):
+        src, base = ((back, 2), (routed, 2 + 2 * n))[q]
         for k, p in enumerate(peers):
-            got(fold_other.at[0, block(p)], 2 + k)
-            got(few_other.at[block(p)], 2 + n + k)
-            fold_out[0, k] = (back[block(p), mine] + fold_other[0, block(p), :]).astype(jnp.bfloat16)
-            few_out[k] = (dot_sums[block(p), :] + few_other[block(p), :]).astype(jnp.bfloat16)
-            remote(fold_out.at[0, k], fold_in.at[0, k], zsend.at[k], zrecv.at[k], {EXPERT: p})
-            remote(few_out.at[k], few_in.at[k], zsend.at[n - 1 + k], zrecv.at[n - 1 + k], {EXPERT: p})
-        for k, p in enumerate(peers):
-            got(fold_other.at[1, block(p)], 2 + 2 * n + k)
-            fold_out[1, k] = (routed[block(p), mine] + fold_other[1, block(p), :]).astype(jnp.bfloat16)
-            remote(fold_out.at[1, k], fold_in.at[1, k], zsend.at[2 * (n - 1) + k], zrecv.at[2 * (n - 1) + k], {EXPERT: p})
+            got(fold_other.at[q, block(p)], base + k)
+            fold_out[q, k] = (src[block(p), mine] + fold_other[q, block(p), :]).astype(jnp.bfloat16)
+            s = 2 * (n - 1) * q + k
+            remote(fold_out.at[q, k], fold_in.at[q, k], zsend.at[s], zrecv.at[s], {EXPERT: p})
+            if q == 1:
+                got(few_other.at[block(p)], 2 + n + k)
+                few_out[k] = (dot_sums[block(p), :] + few_other[block(p), :]).astype(jnp.bfloat16)
+                s = n - 1 + k
+                remote(few_out.at[k], few_in.at[k], zsend.at[s], zrecv.at[s], {EXPERT: p})
 
     def fold_end():
         for src, q, base in ((back, 0, 2), (routed, 1, 2 + 2 * n)):
@@ -1054,8 +1113,8 @@
         for q, dst in ((0, gn2), (1, ffn)):
             got(dst.at[:, theirs], 2 + 3 * n + 2 + q)
 
-    steps = {"join": join, "rows": rows_step, "gates": gates_step, "plane": plane_step, "line": line_step,
-             "load": load, "front": front, "back": back_step, "shared_load": shared_load, "shared": shared,
+    steps = {"join": join, "tok": tok_step, "tokend": tok_end, "gates": gates_step, "plane": plane_step, "line": line_step,
+             "load": load, "load_down": load_down, "pre": pre_step, "front": front, "back": back_step, "rows": rows_step, "shared_load": shared_load, "shared": shared,
              "settle": settle, "fold_start": fold_start, "fold_shared": fold_shared, "fold_lines": fold_lines,
              "fold_end": fold_end}
     items = middle_items(n, here)
@@ -1067,7 +1126,7 @@
         when(cond, c.wait_send)
 
 
-def middle(part, inp, gain, router, named, cot, experts, shared_t, n, order, cid):
+def middle(part, inp, gain, router, named, cot, one, mixed, experts, shared_t, n, order, cid):
     bf, dma, vm = jnp.bfloat16, pltpu.SemaphoreType.DMA, pltpu.VMEM
     toks, width = inp.shape
     here, hid, cut = experts[0].shape
@@ -1081,6 +1140,7 @@
         (S((toks, width), F32), vmem), (S((here, hid, al), bf), anyspace), (S((here, hid, al), bf), anyspace),
         (S((here, hid, al), bf), anyspace), (S((here, al, width), bf), anyspace),
         (S((2, toks, hid), bf), vmem), (S((2, toks, hid), bf), vmem), (S((2 * hid, toks), bf), vmem),
+        (S((width, toks), bf), vmem), (S((width, toks), bf), vmem), (S((mixed.shape[1], toks), bf), vmem),
     ] + [(S((here, hid, width), bf), anyspace)] * 3 + [(S((sh, width), bf), anyspace)] * 3
     scratch = [
         vm((toks, width), F32), vm((2, 3, hid, width), bf), vm((al, 128), F32), vm((al, width), F32),
@@ -1088,20 +1148,20 @@
         vm((al, width), bf), vm((3, hid, al), bf), vm((hid, hid), bf), vm((3, sh, 128), bf), vm((al, 128), F32),
         vm((2, al, width // 2), F32), vm((2, toks, width // 2), F32), vm((2, n - 1, toks, width // 2), bf),
         vm((2, n - 1, toks, width // 2), bf), vm((al, 128), F32), vm((n - 1, toks, 128), bf),
-        vm((n - 1, toks, 128), bf), vm((toks, width), F32), vm((toks, width), F32),
-        dma((6 + 3 * n,)), dma((6 + 3 * n,)), dma((2 * n,)), dma((2 * n,)), dma((90,)), dma((90,)),
+        vm((n - 1, toks, 128), bf), vm((toks, width), F32), vm((toks, width), F32), vm((al, width), bf),
+        dma((6 + 3 * n,)), dma((6 + 3 * n,)), dma((8 * (n - 1),)), dma((8 * (n - 1),)), dma((90,)), dma((90,)),
         dma((24 * (n - 1),)), dma((24 * (n - 1),)), dma((2, 12)), dma((4,)), dma((3,)),
         dma((3 * (n - 1),)), dma((3 * (n - 1),)),
     ]
     res = pl.pallas_call(
         functools.partial(middle_kernel, n, order),
         out_shape=[s for s, _ in outs], out_specs=[b for _, b in outs],
-        in_specs=[vmem] * 6 + [anyspace] * 6,
+        in_specs=[vmem] * 8 + [anyspace] * 6,
         scratch_shapes=scratch,
         compiler_params=pltpu.CompilerParams(
             collective_id=cid, has_side_effects=True, vmem_limit_bytes=67043328),
-    )(part, inp, gain, router, named, cot, *experts, *shared_t)
-    return res[:14]
+    )(part, inp, gain, router, named, cot, one, mixed, *experts, *shared_t)
+    return res[:17]
 
 
 def rms_scale(vector):
@@ -1255,18 +1315,17 @@
     if kernels:
         small = jnp.pad(small, ((0, -small.shape[0] % 32), (0, 0)))
         named_low = jnp.pad(named_low, ((0, 0), (0, 256 - total_experts)))
-        arrays = (query_weight, key_weight, value_weight, output_weight, small, cotangent, named_low)
-        forms = ("rows",) * 3 + ("cols", "cols", "tokens", "tokens")
-        firsts = ("z",) * 3 + ("xy", "z", "xy", "xy")
-        (full_query, full_key, full_value, full_output, full_small, grads_all, named_all) = gather(
-            arrays, forms, firsts, owners, gather_starts)
+        arrays = (query_weight, key_weight, value_weight, output_weight, small, named_low)
+        forms = ("rows",) * 3 + ("cols", "cols", "tokens")
+        firsts = ("z",) * 3 + ("xy", "z", "xy")
+        (full_query, full_key, full_value, full_output, full_small, named_all, sgate_t, sup_t) = gather(
+            arrays, forms, firsts, owners, gather_starts, (shared_gate, shared_up))
     else:
         full_small = lax.all_gather(small, BOTH, axis=1, tiled=True)
         full_query = lax.all_gather(query_weight, BOTH, axis=0, tiled=True)
         full_key = lax.all_gather(key_weight, BOTH, axis=0, tiled=True)
         full_value = lax.all_gather(value_weight, BOTH, axis=0, tiled=True)
         full_output = lax.all_gather(output_weight, BOTH, axis=1, tiled=True)
-        grads_all = lax.all_gather(cotangent, EXPERT, axis=0, tiled=True)
         named_all = lax.all_gather(named_low, EXPERT, axis=0, tiled=True)
     named_all = named_all[:, :total_experts]
     router_rows = full_small[:total_experts]
@@ -1313,9 +1372,9 @@
         router_pad = jnp.pad(turn(router_rows, first, 0), ((0, 128 - total_experts), (0, 0)))
         named_pad = jnp.pad(turn(named_all, first, 1), ((0, 0), (0, 128 - total_experts)))
         (hidden_one, normed_two, rows_all, logits, dots_sum, grad_normed_two, ffn_total, act_t, ggp_t, gup_t,
-         owner_grads, grad_sgate, grad_sup, shared_act_t) = middle(
-            attn_part, block_input, gain_two[None], router_pad, named_pad, grads_all, experts,
-            (shared_gate.T, shared_up.T, shared_down), owners, middle_order, 2)
+         owner_grads, grad_sgate, grad_sup, shared_act_t, one_t, two_t, mixed_t) = middle(
+            attn_part, block_input, gain_two[None], router_pad, named_pad, cotangent, normed_one,
+            mixed_rows, experts, (sgate_t, sup_t, shared_down), owners, middle_order, 2)
         grad_sgate = jnp.concatenate([grad_sgate[0], grad_sgate[1]], axis=1)
         grad_sup = jnp.concatenate([grad_sup[0], grad_sup[1]], axis=1)
         router_probs = jax.nn.softmax(
@@ -1324,11 +1383,13 @@
     else:
         (hidden_one, normed_two, rows_all, router_probs, dots_sum, grad_normed_two, ffn_total, act_t, ggp_t, gup_t,
          owner_grads, grad_sgate, grad_sup, shared_act_t) = plain_middle(
-            attn_part, input_f, gain_two, router_rows, named_all.astype(F32), grads_all, cotangent,
+            attn_part, input_f, gain_two, router_rows, named_all.astype(F32),
+            lax.all_gather(cotangent, EXPERT, axis=0, tiled=True), cotangent,
             tuple(lax.all_gather(w, DP, axis=2, tiled=True) for w in experts),
             lax.all_gather(shared_gate, BOTH, axis=0, tiled=True),
             lax.all_gather(shared_up, BOTH, axis=0, tiled=True),
             lax.all_gather(shared_down, BOTH, axis=1, tiled=True))
+        one_t, two_t, mixed_t = normed_one.T, normed_two.T, mixed_rows.T
     scale_two = rms_scale(hidden_one)
     block_output = (hidden_one + ffn_total).astype(BF)
     grad_out = cotangent.astype(F32)
@@ -1395,8 +1456,7 @@
     extra = jnp.concatenate([
         jnp.zeros((total_experts, D), F32), attn_gain_full[None], ffn_gain_full[None],
         jnp.zeros((room - total_experts - 2, D), F32)])
-    one_t, two_t = normed_one.T, normed_two.T
-    lefts = (one_t, one_t, one_t, mixed_rows.T, two_t, two_t, shared_act_t, logits_t)
+    lefts = (one_t, one_t, one_t, mixed_t, two_t, two_t, shared_act_t, logits_t)
     rights = (grad_qpre, grad_kpre, value_grad_rows, grad_attn, grad_sgate, grad_sup, cotangent, normed_two)
     exp_left = (ggp_t, gup_t, act_t)
     dense = ((("rows", "z"),) * 3

time: 1150 us -> 1100 us (0.957)
  Pallas kernels: 1050 us -> 1000 us
    pallas_call x1, Pallas kernels: 414 us -> 392 us  [middle(): pl.pallas_call(functools.partial(middle_kernel, n, order), out_shape=[s f...]
    pallas_call x1, Pallas kernels: 144 us -> 130 us  [gather(): pl.pallas_call(functools.partial(gather_kernel, leaves, n, starts), out_s...]
    pallas_call x1, Pallas kernels: 490 us -> 477 us  [scatter(): pl.pallas_call(functools.partial(scatter_kernel, dense, units, n, order,...]
    unnamed x106 -> x104, local copies, waits for them, and re-layouts: 29 us -> 26.2 us
where the time goes in v3:
time: 1100 us; the launch traced here: 1090 us
  Pallas kernels  1000 us (91%)
  local copies, waits for them, and re-layouts  38.8 us (4%)
  other arithmetic  22.8 us (2%)
  matrix products  20.9 us (2%)
    pallas_call x1, Pallas kernels, scatter(): pl.pallas_call(functools.partial(scatter_kernel, dense, units, n, order,...  477 us
    pallas_call x1, Pallas kernels, middle(): pl.pallas_call(functools.partial(middle_kernel, n, order), out_shape=[s f...  392 us
    pallas_call x1, Pallas kernels, gather(): pl.pallas_call(functools.partial(gather_kernel, leaves, n, starts), out_s...  130 us
    unnamed x104, local copies, waits for them, and re-layouts  26.2 us

profile of v3, /device:TPU:16, one launch (start us, length us, event | category | flops | bytes accessed | tf_op | source)
XLA Modules:
  0.0 1087.6 jit_solution(7554276751917212482)
XLA Ops:
  7.5 129.6 %shard_map.280 = (bf16[2048,1024]{1,0:T(8,128)(2,1)}, bf16[2048,1024]{1,0:T(8,128)(2,1)}, bf16[2048,1024]{1,0:T(8,128)(2,1)}, bf16[1024,2048]{1,0:T(8,128)(2,1)}...) custom-call(bf16[128,1024]{1,0:T(8,128)(2,1)} %refs_0_.1, ...), custom_call_target="tpu_custom_call" | custom-call | tf_op jit(solution)/shard_map/pallas_call | solution.py:241
  139.1 1.4 slice_convert_fusion
  142.5 3.1 fusion.3
  146.6 1.4 copy-done
  152.6 3.9 fusion.42.refs_0_
  156.5 391.9 %shard_map.281 = (f32[128,2048]{1,0:T(8,128)}, bf16[128,2048]{1,0:T(8,128)(2,1)}, bf16[512,2048]{1,0:T(8,128)(2,1)}, f32[128,128]{1,0:T(8,128)}, f32[128,128]{1,...) custom-call(f32[128,2048]{1,0:T(8,128)} %fusion.42.refs_0_, ...), custom_call_target="tpu_custom_call" | custom-call | tf_op jit(solution)/shard_map/pallas_call | solution.py:1156
  548.5 1.5 multiply_reduce_fusion.2
  553.3 2.3 multiply_reduce_fusion
  555.6 2.4 fusion.36
  558.9 1.5 convolution_convert_fusion.2
  564.2 1.5 fusion.35
  565.9 1.5 convolution_add_fusion.1
  568.0 2.5 convolution_add_fusion.part
  571.4 5.3 shard_map.282
  577.6 1.5 fusion.11
  579.1 2.5 fusion.8
  585.2 476.9 %shard_map.283 = (f32[128,1024]{1,0:T(8,128)}, f32[128,1024]{1,0:T(8,128)}, f32[128,1024]{1,0:T(8,128)}, f32[1024,128]{1,0:T(8,128)}, f32[128,1408]{1,0:T(8,128)...) custom-call(bf16[2048,128]{1,0:T(8,128)(2,1)} %get-tuple-element.64., ...), custom_call_target="tpu_custom_call" | custom-call | tf_op jit(solution)/shard_map/pallas_call | solution.py:671
  1064.6 1.9 copy.153
  1066.5 1.9 copy.154
  1068.4 1.9 copy.155
  1070.3 1.9 copy.156
  1072.2 6.4 copy.157
  1078.6 2.7 copy.158
  1082.1 2.7 copy.159
  (155 shorter events, 35.8 us)
Async XLA Ops:
  0.6 141.7 %copy-start.9 = (bf16[128,2048]{1,0:T(8,128)(2,1)S(1)}, bf16[128,2048]{1,0:T(8,128)(2,1)}, u32[]{:S(2)}) copy-start(bf16[128,2048]{1,0:T(8,128)(2,1)} %refs_1_.3) | copy-start | bytes 1572868
  3.6 142.0 %copy-start.39 = (f32[128]{0:T(128)}, f32[128]{0:T(128)S(1)}, u32[]{:S(2)}) copy-start(f32[128]{0:T(128)S(1)} %get-tuple-element.121) | copy-start | bytes 1540
  4.3 141.3 %copy-start.38 = (pred[128,16]{0,1:T(8,128)(4,1)}, pred[128,16]{0,1:T(8,128)(4,1)S(1)}, u32[]{:S(2)}) copy-start(pred[128,16]{0,1:T(8,128)(4,1)S(1)} %fusion.27) | copy-start | bytes 6148
  7.5 141.6 %copy-start.28 = (f32[128,64]{1,0:T(8,128)}, f32[128,64]{1,0:T(8,128)S(1)}, u32[]{:S(2)}) copy-start(f32[128,64]{1,0:T(8,128)S(1)} %get-tuple-element.124) | copy-start | bytes 98308
  7.5 141.6 %copy-start.30 = (f32[128,64]{1,0:T(8,128)}, f32[128,64]{1,0:T(8,128)S(1)}, u32[]{:S(2)}) copy-start(f32[128,64]{1,0:T(8,128)S(1)} %get-tuple-element.125) | copy-start | bytes 98308
  137.2 8.5 copy-start.3
  140.5 5.9 copy-start.34
  145.7 5.5 copy-start.23
  548.5 7.1 copy-start.11
  548.5 7.1 copy-start.13
  548.5 7.1 copy-start.36
  553.3 5.6 copy-start.5
  558.9 4.4 copy-start.18
  568.0 9.6 copy-start.10
  568.0 9.6 copy-start.35
  568.0 9.6 copy-start.40
  568.0 11.1 %copy-start.41 = (f32[128]{0:T(128)S(1)}, f32[128]{0:T(128)}, u32[]{:S(2)}) copy-start(f32[128]{0:T(128)} %get-tuple-element.120) | copy-start | bytes 1540
  571.3 11.1 %copy-start.33 = (bf16[2,128,704]{2,1,0:T(8,128)(2,1)S(1)}, bf16[2,128,704]{2,1,0:T(8,128)(2,1)}, u32[]{:S(2)}) copy-start(bf16[2,128,704]{2,1,0:T(8,128)(2,1)} %get-tuple-element.68) | copy-start | bytes 1081348
  576.7 6.7 copy-start.32
  577.5 6.7 copy-start.42
  577.5 6.7 copy-start.43
  1072.2 6.4 copy-start.12
  1072.2 9.2 slice-start
  1082.1 4.4 copy-start.25
  (22 other events, 62.2 us)

commit v4 on v3

--- a/solution.py
+++ b/solution.py
@@ -1,5 +1,6 @@
 import functools
 import math
+import types
 
 import jax
 import jax.numpy as jnp
@@ -20,7 +21,7 @@
 rope_base = 10000.0
 masked_score = -1e30
 gather_starts = (1.91, 2.48, 3.88, 2.78, 2.0, 1.0)
-scatter_order = (97, 98, 73, 45, 9, 55, 2, 65, 72, 19, 100, 82, 1, 64, 46, 99, 39, 83, 54, 36, 78, 18, 38, 92, 75, 74, 37, 11, 87, 56, 77, 93, 10, 12, 47, 0, 63, 85, 94, 57, 3, 66, 84, 80, 27, 20, 41, 14, 28, 79, 13, 21, 5, 68, 40, 101, 29, 16, 43, 15, 22, 4, 67, 42, 88, 30, 48, 86, 95, 61, 17, 81, 76, 6, 69, 44, 58, 23, 7, 70, 89, 49, 90, 60, 31, 50, 96, 25, 32, 24, 8, 71, 51, 59, 52, 91, 34, 33, 26, 53, 62, 35)
+scatter_order = (102, 91, 81, 101, 87, 49, 76, 82, 92, 50, 51, 0, 1, 31, 32, 22, 97, 41, 7, 58, 104, 42, 77, 96, 83, 59, 61, 86, 24, 13, 14, 40, 103, 52, 78, 89, 99, 2, 3, 67, 70, 98, 4, 79, 69, 68, 23, 5, 53, 43, 60, 72, 54, 16, 105, 15, 55, 71, 25, 74, 100, 34, 56, 33, 73, 6, 93, 94, 45, 80, 62, 18, 44, 27, 75, 63, 36, 38, 17, 29, 28, 88, 84, 95, 9, 35, 8, 64, 47, 26, 20, 46, 37, 65, 19, 90, 57, 85, 21, 30, 11, 10, 39, 66, 48, 12)
 middle_order = (13, 8, 33, 113, 0, 9, 10, 14, 15, 57, 53, 91, 73, 37, 58, 59, 34, 35, 17, 18, 11, 12, 92, 19, 54, 55, 61, 77, 16, 3, 109, 99, 114, 81, 65, 66, 21, 25, 74, 67, 62, 36, 26, 27, 56, 69, 95, 100, 101, 82, 29, 30, 31, 93, 4, 115, 116, 110, 111, 20, 96, 97, 78, 28, 22, 23, 24, 94, 41, 63, 117, 5, 6, 7, 1, 68, 75, 76, 112, 98, 103, 32, 83, 84, 86, 60, 2, 70, 71, 72, 64, 102, 104, 127, 45, 42, 131, 38, 79, 80, 85, 87, 88, 89, 90, 105, 118, 135, 39, 40, 46, 49, 43, 128, 129, 106, 107, 108, 47, 121, 123, 44, 132, 119, 120, 122, 124, 125, 126, 136, 137, 50, 51, 52, 133, 134, 130, 139, 141, 48, 145, 138, 140, 142, 151, 143, 152, 144, 147, 146, 148, 149, 150, 153, 154)
 
 
@@ -258,7 +259,7 @@
 
 def scatter_items(dense, units, n):
     ends = [k // 2 if k % 2 == 0 else n - 1 - k // 2 for k in range(n)]
-    items = []
+    items = [("a", k, "", 0) for k in range(4)]
     for i, (_, first) in enumerate(dense):
         names = [("z", t) for t in ends] if first == "z" else []
         names += [("p", s) for s in ("y1", "x1", "x2", "y2")]
@@ -269,50 +270,70 @@
     return items
 
 
-def scatter_kernel(dense, units, n, order, which, *refs):
+def scatter_uses(item, m):
+    kind, i = item[:2]
+    if kind == "a":
+        return (("hidden", "back", "few", "named", "gain_two", "router", "cot", "normed"),
+                ("q", "k", "v", "cos", "sin", "mask"), (), ("inp", "gain_one"))[i]
+    if kind == "e":
+        return (("ggp", "rows_all"), ("gup", "rows_all"), ("act", "cot_all", "gates"))[i // 2]
+    return (("one_t",), ("one_t",), ("one_t",), ("mixed_t",), ("two_t", "gsg"), ("two_t", "gsu"),
+            ("sact_t", "cot"), ("normed",))[i]
+
+
+def scatter_kernel(dense, units, n, order, names, experts, *refs):
     m = len(dense)
-    u_ = max(which) + 1
-    given, refs = refs[:u_], refs[u_:]
-    held_in, refs = refs[-u_ - 1 : -1], refs[: -u_ - 1] + refs[-1:]
-    in_sem, refs = refs[-1], refs[:-1]
-    seat = [held_in[w] for w in which]
-    lefts, rights = seat[:m], seat[m : 2 * m]
-    exp_left = seat[2 * m : 2 * m + 3]
-    rows_all, grads_in, extra = seat[2 * m + 3 : 2 * m + 6]
+    c_ = len(names)
+    given = dict(zip(names, refs[:c_]))
+    w_out, w_qkv = refs[c_], refs[c_ + 1 : c_ + 4]
+    refs = refs[c_ + 4 :]
+    box, refs = types.SimpleNamespace(**dict(zip(names, refs[-c_:]))), refs[:-c_]
+    (in_sem, logits_t, gq, gk, gv, gattn, extra, gm, wbuf, gh, part, other, rhs, w_sem, pair_send, pair_recv,
+     small_out) = refs[-17:]
+    refs = refs[:-17]
+    own_grads = (gq, gk, gv)
+    lefts = (box.one_t,) * 3 + (box.mixed_t, box.two_t, box.two_t, box.sact_t, logits_t)
+    rights = own_grads + (gattn, box.gsg, box.gsu, box.cot, box.normed)
+    exp_left = (box.ggp, box.gup, box.act)
+    rows_all = box.rows_all
     here_yet = set()
 
-    def need(*numbers):
-        for k in numbers:
-            w = which[k]
-            if w not in here_yet:
-                here_yet.add(w)
-                pltpu.make_async_copy(given[w], held_in[w], in_sem.at[w]).wait()
-
-    first_use = [k for it in ([scatter_items(dense, units, n)[o] for o in order] if order else scatter_items(dense, units, n))
-                 for k in ((it[1], m + it[1]) + ((2 * m + 5,) if it[1] == m - 1 else ()) if it[0] == "d"
-                           else (2 * m + it[1] // 2, 2 * m + 3 + (it[1] // 2 == 2)))]
-    for w in dict.fromkeys(which[k] for k in first_use):
-        pltpu.make_async_copy(given[w], held_in[w], in_sem.at[w]).start()
+    def fetch(name):
+        k = names.index(name)
+        return pltpu.make_async_copy(given[name], getattr(box, name), in_sem.at[k])
+
+    def need(item):
+        for name in scatter_uses(item, m):
+            if name not in here_yet:
+                here_yet.add(name)
+                fetch(name).wait()
+
+    steps = scatter_items(dense, units, n)
+    steps = [steps[k] for k in order] if order else steps
+    for name in dict.fromkeys(v for it in steps for v in scatter_uses(it, m)):
+        fetch(name).start()
+    input_out, refs = refs[m + 3], refs[: m + 3] + refs[m + 4 :]
     outs, refs = refs[: m + 3], refs[m + 3 :]
     landed, refs = refs[: 3 * m + 2], refs[3 * m + 2 :]
     bufs = dict(zip("xyz", refs[:3]))
     held, tall, wide = refs[3:6]
     stage_sem, load_sem, recv_sem = refs[6:9]
     send_sems = dict(zip("xyz", refs[9:12]))
-    d, e = lax.axis_index(DP), lax.axis_index(EXPERT)
+    d, e = lax.axis_index("dp"), lax.axis_index("expert")
     dx = d + 1 - 2 * lax.rem(d, 2)
     dy = lax.rem(d + 2, 4)
     dd = lax.rem(dx + 2, 4)
     after, before = e < n - 1, e > 0
 
     barrier = pltpu.get_barrier_semaphore()
-    for dev in ({DP: dx}, {DP: dy}):
+    partner = {"tensor": 1 - lax.axis_index("tensor")}
+    for dev in ({"dp": dx}, {"dp": dy}, partner):
         pl.semaphore_signal(barrier, inc=1, device_id=dev, device_id_type=MESH)
-    for cond, dev in ((after, {EXPERT: e + 1}), (before, {EXPERT: e - 1})):
+    for cond, dev in ((after, {"expert": e + 1}), (before, {"expert": e - 1})):
         @pl.when(cond)
         def _():
             pl.semaphore_signal(barrier, inc=1, device_id=dev, device_id_type=MESH)
-    pl.semaphore_wait(barrier, 2 + after.astype(jnp.int32) + before.astype(jnp.int32))
+    pl.semaphore_wait(barrier, 3 + after.astype(jnp.int32) + before.astype(jnp.int32))
     held[...] = jnp.zeros_like(held)
 
     def when(cond, f):
@@ -355,7 +376,7 @@
         seen.add(key)
         c = pltpu.make_async_remote_copy(
             src_ref=view, dst_ref=view, send_sem=recv_sem.at[sem], recv_sem=recv_sem.at[sem],
-            device_id={DP: dx}, device_id_type=MESH)
+            device_id={"dp": dx}, device_id_type=MESH)
         when(cond, c.wait_recv)
 
     class Loads:
@@ -422,9 +443,6 @@
             out_busy.pop(which).wait()
 
     def dense_step(i, stage, arg):
-        need(i, m + i)
-        if i == m - 1:
-            need(2 * m + 5)
         z_land, first_land, second_land = landed[3 * i : 3 * i + 3]
         z_first = dense[i][1] == "z"
         hb = half_rows_of(i)
@@ -485,11 +503,11 @@
                 for s in ("y1", "x1", "x2", "y2"):
                     plane_arrived(s)
             pl.when(cond)(go)
-            send("z", k, z_rows, z_land.at[side, t], z_sem + side * n + t, {EXPERT: e - 1 + 2 * side}, cond)
+            send("z", k, z_rows, z_land.at[side, t], z_sem + side * n + t, {"expert": e - 1 + 2 * side}, cond)
         elif stage == "p":
             s = arg
             link = s[0]
-            dev = {DP: dy if link == "y" else dx}
+            dev = {"dp": dy if link == "y" else dx}
             half = 0 if s in ("y1", "x2") else 1
             k = slot(link)
             ld = Loads()
@@ -536,7 +554,7 @@
                     ld.add(z_land.at[side, e], side, 0, there)
                 plane_out(ld, e)
             rows = dense[i][0] == "rows"
-            which = "wide" if rows else "tall"
+            which = "wide" if rows else "slim"
             out_wait(which)
             ld.wait()
             def one(h, _):
@@ -547,15 +565,15 @@
                         r = value.shape[0]
                         wide[pl.ds(pl.multiple_of(h * r, r), r), col : col + 128] = value
                     else:
-                        tall[0, pl.ds(pl.multiple_of(h * hb + row, 16), value.shape[0]), 0:128] = value
+                        small_out[pl.ds(pl.multiple_of(h * hb + row, 16), value.shape[0]), :] = value
                 dense_piece(i, d, e, h, put)
                 return 0
             lax.fori_loop(0, 2, one, 0)
             if rows:
                 src = wide.at[:, pl.ds(0, outs[i].shape[1])]
             else:
-                src = tall.at[0, pl.ds(0, outs[i].shape[0]), pl.ds(0, 128)]
-            c = pltpu.make_async_copy(src, outs[i], stage_sem.at[0 if rows else 1])
+                src = small_out.at[pl.ds(0, outs[i].shape[0])]
+            c = pltpu.make_async_copy(src, outs[i], stage_sem.at[0 if rows else 3])
             c.start()
             out_busy[which] = c
 
@@ -563,7 +581,6 @@
 
     def expert_step(u, stage, s):
         a, q = u // 2, u % 2
-        need(2 * m + a, 2 * m + 3 + (a == 2))
         rows, width = exp_left[a].shape[1], outs[m + a].shape[2]
         tiles = width // 128
         piece = rows * tiles
@@ -578,10 +595,15 @@
             return land.at[u, which, pl.ds(sub * piece, piece)]
 
         def one_piece(j, d_, put):
+            if a == 2:
+                for r in range(0, rhs.shape[0], 128):
+                    gate = box.gates[r : r + 128, :][:, j : j + 1]
+                    ct = box.cot_all[r : r + 128, pl.ds(pl.multiple_of(d_ * width, 128), width)]
+                    rhs[r : r + 128, :] = (gate * ct.astype(F32)).astype(jnp.bfloat16)
             def body(r, _):
                 left = exp_left[a][j, pl.ds(pl.multiple_of(r * step, 16), step), :]
                 cols = pl.ds(pl.multiple_of(d_ * width, 128), width)
-                right = grads_in[j, :, cols] if a == 2 else rows_all[:, cols]
+                right = rhs[...] if a == 2 else rows_all[:, cols]
                 res = jnp.dot(left, right, preferred_element_type=F32)
                 for c in range(tiles):
                     put(c * rows + r * step, res[:, c * 128 : (c + 1) * 128], (r * step, c * 128))
@@ -594,7 +616,7 @@
         ld = Loads()
         if stage == "p":
             link = s[0]
-            dev = {DP: dy if link == "y" else dx}
+            dev = {"dp": dy if link == "y" else dx}
             j = q if s in ("y1", "x2") else q + 2
             k = slot(link)
             if s in ("y1", "x1"):
@@ -632,9 +654,109 @@
                         c.wait()
             out_busy["tall"] = Both()
 
-    items = scatter_items(dense, units, n)
-    for kind, i, stage, arg in [items[k] for k in order] if order else items:
-        (dense_step if kind == "d" else expert_step)(i, stage, arg)
+    width_all = gh.shape[1]
+    chunk = wbuf.shape[1]
+    plan = [w_out.at[:, pl.ds(c * chunk, chunk)] for c in range(width_all // chunk)]
+    plan += [w.at[pl.ds(c * chunk, chunk)] for c in range(width_all // chunk) for w in w_qkv]
+
+    def weight(k):
+        return pltpu.make_async_copy(plan[k], wbuf.at[k % 2], w_sem.at[k % 2])
+
+    def a_t_b(a, b):
+        return lax.dot_general(a, b, (((1,), (1,)), ((), ())), preferred_element_type=F32)
+
+    def attn_step(k):
+        if k == 0:
+            weight(0).start()
+            weight(1).start()
+            logits = a_t_b(box.normed[...], box.router[...])
+            lane = lax.broadcasted_iota(jnp.int32, logits.shape, 1)
+            logits = jnp.where(lane < experts, logits, -1e30)
+            ex = jnp.exp(logits - jnp.max(logits, axis=-1, keepdims=True))
+            probs = ex / jnp.sum(ex, axis=-1, keepdims=True)
+            grads = jnp.where(box.named[...] > 0.0, box.few[...], 0.0)
+            grads = probs * (grads - jnp.sum(grads * probs, axis=-1, keepdims=True))
+            logits_t[...] = grads.T[: logits_t.shape[0], :].astype(jnp.bfloat16)
+            extra[...] = jnp.zeros_like(extra)
+            gains = jnp.zeros((1, width_all), F32)
+            for r in range(0, gh.shape[0], 32):
+                p = slice(r, r + 32)
+                low = grads[p].astype(jnp.bfloat16)
+                gn = box.back[p, :] + jnp.dot(low, box.router[...], preferred_element_type=F32)
+                h = box.hidden[p, :]
+                scale = lax.rsqrt(jnp.mean(h * h, axis=-1, keepdims=True) + epsilon)
+                gains = gains + jnp.sum(gn * h * scale, axis=0, keepdims=True)
+                w = gn * box.gain_two[...]
+                g = (box.cot[p, :].astype(F32) + scale * w
+                     - h * (scale * scale * scale) * jnp.mean(h * w, axis=-1, keepdims=True))
+                gh[p, :] = g
+                gattn[p, :] = g.astype(jnp.bfloat16)
+            extra[experts + 1 : experts + 2, :] = gains
+        elif k == 1:
+            count = width_all // chunk
+            for c in range(count):
+                weight(c).wait()
+                piece = a_t_b(gattn[:, c * chunk : (c + 1) * chunk], wbuf[c % 2])
+                weight(c + 2).start()
+                part[:, : piece.shape[1]] = piece if c == 0 else part[:, : piece.shape[1]] + piece
+            gm[...] = part[:, : gm.shape[1]].astype(jnp.bfloat16)
+            root = 1.0 / math.sqrt(HD)
+            for h in range(gm.shape[1] // HD):
+                cols = slice(h * HD, (h + 1) * HD)
+                q, kk, v, g = box.q[:, cols], box.k[:, cols], box.v[:, cols], gm[:, cols]
+                scores = a_t_b(q, kk) / math.sqrt(HD)
+                scores = jnp.where(box.mask[...] > 0.0, scores, masked_score)
+                ex = jnp.exp(scores - jnp.max(scores, axis=-1, keepdims=True))
+                prob = ex / jnp.sum(ex, axis=-1, keepdims=True)
+                gp = a_t_b(g, v)
+                gs = prob * (gp - jnp.sum(prob * gp, axis=-1, keepdims=True))
+                gv[:, cols] = jnp.dot(prob.T.astype(jnp.bfloat16), g, preferred_element_type=F32).astype(jnp.bfloat16)
+                for dst, left, right in ((gq, gs, kk), (gk, gs.T, q)):
+                    u = jnp.dot(left.astype(jnp.bfloat16), right, preferred_element_type=F32) * root
+                    u = u * box.cos[...] + pltpu.roll(u, HD // 2, 1) * box.sin[...]
+                    dst[:, cols] = u.astype(jnp.bfloat16)
+        elif k == 2:
+            base = width_all // chunk
+            for c in range(width_all // chunk):
+                cols = slice(c * chunk, (c + 1) * chunk)
+                for j in range(3):
+                    i = base + 3 * c + j
+                    weight(i).wait()
+                    piece = a_t_b(own_grads[j][...], wbuf[i % 2])
+                    if i + 2 < len(plan):
+                        weight(i + 2).start()
+                    part[:, cols] = piece if j == 0 else part[:, cols] + piece
+            pair_copy().start()
+        else:
+            pair_copy().wait_recv()
+            gains = jnp.zeros((1, width_all), F32)
+            for r in range(0, gh.shape[0], 32):
+                p = slice(r, r + 32)
+                gn = part[p, :] + other[p, :]
+                x = box.inp[p, :].astype(F32)
+                scale = lax.rsqrt(jnp.mean(x * x, axis=-1, keepdims=True) + epsilon)
+                gains = gains + jnp.sum(gn * x * scale, axis=0, keepdims=True)
+                w = gn * box.gain_one[...]
+                gh[p, :] = (gh[p, :] + scale * w
+                            - x * (scale * scale * scale) * jnp.mean(x * w, axis=-1, keepdims=True))
+            extra[experts : experts + 1, :] = gains
+            c = pltpu.make_async_copy(gh, input_out, stage_sem.at[4])
+            c.start()
+            out_busy["input"] = c
+
+    def pair_copy():
+        return pltpu.make_async_remote_copy(
+            src_ref=part, dst_ref=other, send_sem=pair_send, recv_sem=pair_recv,
+            device_id=partner, device_id_type=MESH)
+
+    for item in steps:
+        kind, i, stage, arg = item
+        need(item)
+        if kind == "a":
+            attn_step(i)
+        else:
+            (dense_step if kind == "d" else expert_step)(i, stage, arg)
+    pair_copy().wait_send()
     for c, cond in pending.values():
         when(cond, c.wait_send)
     for which in list(out_busy):
@@ -642,85 +764,56 @@
     assert sum(c for _, c in sems.values()) <= recv_sem.shape[0]
 
 
-def scatter(dense, lefts, rights, extra, exp_left, rows_all, grads_in, n, order, cid):
+def scatter(dense, given, weights, experts, n, order, cid):
     m, units = len(dense), 6
-    bf = jnp.bfloat16
+    bf, dma, vm = jnp.bfloat16, pltpu.SemaphoreType.DMA, pltpu.VMEM
+    toks, width = given["hidden"].shape
+    heads = given["q"].shape[1]
+    room = experts + 2 + (-(experts + 2) % 64)
+    left = dict(zip(range(m), ("one_t", "one_t", "one_t", "mixed_t", "two_t", "two_t", "sact_t")))
     outs, landed = [], []
-    for (kind, first), a, b in zip(dense, lefts, rights):
+    for i, (kind, first) in enumerate(dense):
+        rows = given[left[i]].shape[0] if i in left else room
         if kind == "rows":
-            r = a.shape[0] // (4 * n)
-            shape, hb = (r, b.shape[1]), r // 2 * b.shape[1] // 128
+            r = rows // (4 * n)
+            cols = heads if i < 3 else given["gsg"].shape[1]
+            shape, hb = (r, cols), r // 2 * cols // 128
         else:
-            shape, hb = (a.shape[0], 128), a.shape[0] // 2
+            shape, hb = (rows, 128), rows // 2
         outs.append(jax.ShapeDtypeStruct(shape, F32))
         g, z = (1, 8) if first == "z" else (n, 2)
         landed += [jax.ShapeDtypeStruct((2, n, z * hb, 128), bf),
                    jax.ShapeDtypeStruct((2, g * 2 * hb, 128), bf),
                    jax.ShapeDtypeStruct((2, g * hb, 128), bf)]
-    here, rows = exp_left[0].shape[:2]
-    width = rows_all.shape[1] // 4
-    outs += [jax.ShapeDtypeStruct((here, rows, width), F32)] * 3
-    piece = rows * width // 128
+    here, rows = given["act"].shape[:2]
+    cut = width // 4
+    tall_rows = max(o.shape[0] for o in outs)
+    wide_cols = max(o.shape[1] for o in outs)
+    outs += [jax.ShapeDtypeStruct((here, rows, cut), F32)] * 3
+    outs.append(jax.ShapeDtypeStruct((toks, width), F32))
+    piece = rows * cut // 128
     landed += [jax.ShapeDtypeStruct((units, 2, 2 * piece, 128), bf),
                jax.ShapeDtypeStruct((units, 2, piece, 128), bf)]
     anyspace = pl.BlockSpec(memory_space=pl.ANY)
     count = m * (2 * n + 4) + 4 * units
-    taken = [*lefts, *rights, *exp_left, rows_all, grads_in, extra]
-    single = list({id(v): v for v in taken}.values())
-    which = tuple([id(v) for v in single].index(id(v)) for v in taken)
+    names = tuple(given)
     res = pl.pallas_call(
-        functools.partial(scatter_kernel, dense, units, n, order, which),
+        functools.partial(scatter_kernel, dense, units, n, order, names, experts),
         out_shape=outs + landed,
-        in_specs=[anyspace] * len(single),
+        in_specs=[anyspace] * (len(names) + 4),
         out_specs=[anyspace] * (len(outs) + len(landed)),
-        scratch_shapes=[pltpu.VMEM((ring_slots[s], message_rows, 128), bf) for s in "xyz"] + [
-            pltpu.VMEM((4, message_rows, 128), bf),
-            pltpu.VMEM((2, max(rows, max(o.shape[0] for o in outs[:m])), width), F32),
-            pltpu.VMEM((128, max(o.shape[1] for o in outs[:m])), F32),
-            pltpu.SemaphoreType.DMA((3,)), pltpu.SemaphoreType.DMA((8,)),
-            pltpu.SemaphoreType.DMA((count,)),
-        ] + [pltpu.SemaphoreType.DMA((ring_slots[s],)) for s in "xyz"] + [
-            pltpu.VMEM(v.shape, v.dtype) for v in single] + [pltpu.SemaphoreType.DMA((len(single),))],
+        scratch_shapes=[vm((ring_slots[s], message_rows, 128), bf) for s in "xyz"] + [
+            vm((4, message_rows, 128), bf), vm((2, rows, cut), F32), vm((128, wide_cols), F32),
+            dma((5,)), dma((8,)), dma((count,))] + [dma((ring_slots[s],)) for s in "xyz"] + [
+            dma((len(names),)), vm((room, toks), bf)] + [vm((toks, heads), bf)] * 3 + [
+            vm((toks, width), bf), vm((room, width), F32), vm((toks, heads), bf),
+            vm((2, width // 2, heads), bf), vm((toks, width), F32), vm((toks, width), F32),
+            vm((toks, width), F32), vm((n * toks, cut), bf), dma((2,)), dma, dma, vm((tall_rows, 128), F32),
+        ] + [vm(v.shape, v.dtype) for v in given.values()],
         compiler_params=pltpu.CompilerParams(
             collective_id=cid, has_side_effects=True, vmem_limit_bytes=67043328),
-    )(*single)
-    return res[: m + 3]
-
-
-def pair_kernel(part, total, other, send_sem, recv_sem):
-    t = lax.axis_index(TENSOR)
-    partner = {TENSOR: 1 - t}
-    barrier = pltpu.get_barrier_semaphore()
-    pl.semaphore_signal(barrier, inc=1, device_id=partner, device_id_type=MESH)
-    pl.semaphore_wait(barrier, 1)
-    rows = part.shape[0] // 4
-    copies = []
-    for k in range(4):
-        piece = pl.ds(k * rows, rows)
-        c = pltpu.make_async_remote_copy(
-            src_ref=part.at[piece], dst_ref=other.at[piece], send_sem=send_sem.at[k],
-            recv_sem=recv_sem.at[k], device_id=partner, device_id_type=MESH)
-        c.start()
-        copies.append(c)
-    for k, c in enumerate(copies):
-        c.wait_recv()
-        piece = pl.ds(k * rows, rows)
-        total[piece, :] = part[piece, :].astype(F32) + other[piece, :].astype(F32)
-    for c in copies:
-        c.wait_send()
-
-
-def pair_sum(part, cid):
-    vmem = pl.BlockSpec(memory_space=pltpu.VMEM)
-    return pl.pallas_call(
-        pair_kernel,
-        out_shape=jax.ShapeDtypeStruct(part.shape, F32),
-        in_specs=[vmem],
-        out_specs=vmem,
-        scratch_shapes=[pltpu.VMEM(part.shape, part.dtype),
-                        pltpu.SemaphoreType.DMA((4,)), pltpu.SemaphoreType.DMA((4,))],
-        compiler_params=pltpu.CompilerParams(collective_id=cid, has_side_effects=True),
-    )(part)
+    )(*given.values(), *weights)
+    return res[: m + 4]
 
 
 def across(a, b):
@@ -750,15 +843,15 @@
 def middle_kernel(n, order, *refs):
     (part, inp, gain, router, named, cot_own, one, mixed, gate_in, up_in, down_in, sg_in, su_in, sd_in) = refs[:14]
     refs = refs[14:]
-    (hidden, normed, rows_all, probs, few, gn2, ffn, act_t, ggp_t, gup_t, copies_out,
+    (hidden, normed, rows_all, few, gn2, ffn, act_t, ggp_t, gup_t, gates, cot,
      gsg, gsu, sact_t, one_t, two_t, mixed_t) = refs[:17]
     exp_land, sh_land = refs[17:20], refs[20:23]
     refs = refs[23:]
-    (other, weights, gates, back, routed, gpre, upre, act, grad, copy_buf, turned, eye,
+    (other, weights, back, routed, gpre, upre, act, grad, copy_buf, turned, eye,
      sh_stage, dot_sums, fold_other, fold_own, fold_out, fold_in, few_other, few_out, few_in,
-     ffn_own, gn_own, cot) = refs[:24]
+     ffn_own, gn_own) = refs[:22]
     (pair_send, pair_recv, row_send, row_recv, plane_send, plane_recv, line_send, line_recv,
-     load_sem, out_sem, stage_sem, zsend, zrecv) = refs[24:]
+     load_sem, out_sem, stage_sem, zsend, zrecv) = refs[22:]
     ins = (gate_in, up_in, down_in)
     sh_ins = (sg_in, su_in, sd_in)
     here, hid, width = gate_in.shape
@@ -867,8 +960,6 @@
         r = lax.broadcasted_iota(jnp.int32, eye.shape, 0)
         c = lax.broadcasted_iota(jnp.int32, eye.shape, 1)
         eye[...] = jnp.where(r == c, 1.0, 0.0).astype(jnp.bfloat16)
-        own = block(e)
-        probs[...] = (across(rows_all[own, :], router[...]))
 
     def plane_view(i, o, h):
         if i < 12:
@@ -979,7 +1070,6 @@
     def front(j):
         for c in loads.pop((j, (2,))):
             c.wait()
-        free(3)
         lane = lax.broadcasted_iota(jnp.int32, (256, 128), 1)
         def out(k, _):
             m, c = k // 4, k % 4
@@ -994,7 +1084,6 @@
             copy_buf[r, cols] = (gt * ct).astype(jnp.bfloat16)
             return 0
         lax.fori_loop(0, alltoks // 256 * 4, out, 0)
-        write(copy_buf, copies_out.at[j], 3)
         free(0)
         turned[0] = across(eye[...], act[...]).astype(jnp.bfloat16)
         write(turned.at[0], act_t.at[j], 0)
@@ -1039,7 +1128,6 @@
     def shared(v):
         for c in loads.pop(("s", v)):
             c.wait()
-        free(3)
         w = lambda a: weights[v, a]
         own = block(e)
         ffn_front(normed, toks, w)
@@ -1052,8 +1140,8 @@
             gn_own[:, c * 512 : (c + 1) * 512] += (
                 times(grad[0, 0:toks, :], weights[v, 0, :, c * 512 : (c + 1) * 512])
                 + times(grad[1, 0:toks, :], weights[v, 1, :, c * 512 : (c + 1) * 512]))
-        gsg[v] = grad[0, 0:toks, :]
-        gsu[v] = grad[1, 0:toks, :]
+        gsg[:, v * hid : (v + 1) * hid] = grad[0, 0:toks, :]
+        gsu[:, v * hid : (v + 1) * hid] = grad[1, 0:toks, :]
 
     def settle():
         for i in range(3):
@@ -1136,19 +1224,19 @@
     vmem, anyspace = pl.BlockSpec(memory_space=pltpu.VMEM), pl.BlockSpec(memory_space=pl.ANY)
     outs = [
         (S((toks, width), F32), vmem), (S((toks, width), bf), vmem), (S((al, width), bf), vmem),
-        (S((toks, 128), F32), vmem), (S((toks, 128), F32), vmem), (S((toks, width), F32), vmem),
+        (S((toks, 128), F32), vmem), (S((toks, width), F32), vmem),
         (S((toks, width), F32), vmem), (S((here, hid, al), bf), anyspace), (S((here, hid, al), bf), anyspace),
-        (S((here, hid, al), bf), anyspace), (S((here, al, width), bf), anyspace),
-        (S((2, toks, hid), bf), vmem), (S((2, toks, hid), bf), vmem), (S((2 * hid, toks), bf), vmem),
+        (S((here, hid, al), bf), anyspace), (S((al, 128), F32), vmem), (S((al, width), bf), vmem),
+        (S((toks, 2 * hid), bf), vmem), (S((toks, 2 * hid), bf), vmem), (S((2 * hid, toks), bf), vmem),
         (S((width, toks), bf), vmem), (S((width, toks), bf), vmem), (S((mixed.shape[1], toks), bf), vmem),
     ] + [(S((here, hid, width), bf), anyspace)] * 3 + [(S((sh, width), bf), anyspace)] * 3
     scratch = [
-        vm((toks, width), F32), vm((2, 3, hid, width), bf), vm((al, 128), F32), vm((al, width), F32),
+        vm((toks, width), F32), vm((2, 3, hid, width), bf), vm((al, width), F32),
         vm((al, width), F32), vm((al, hid), F32), vm((al, hid), F32), vm((al, hid), bf), vm((2, al, hid), bf),
         vm((al, width), bf), vm((3, hid, al), bf), vm((hid, hid), bf), vm((3, sh, 128), bf), vm((al, 128), F32),
         vm((2, al, width // 2), F32), vm((2, toks, width // 2), F32), vm((2, n - 1, toks, width // 2), bf),
         vm((2, n - 1, toks, width // 2), bf), vm((al, 128), F32), vm((n - 1, toks, 128), bf),
-        vm((n - 1, toks, 128), bf), vm((toks, width), F32), vm((toks, width), F32), vm((al, width), bf),
+        vm((n - 1, toks, 128), bf), vm((toks, width), F32), vm((toks, width), F32),
         dma((6 + 3 * n,)), dma((6 + 3 * n,)), dma((8 * (n - 1),)), dma((8 * (n - 1),)), dma((90,)), dma((90,)),
         dma((24 * (n - 1),)), dma((24 * (n - 1),)), dma((2, 12)), dma((4,)), dma((3,)),
         dma((3 * (n - 1),)), dma((3 * (n - 1),)),
@@ -1281,6 +1369,86 @@
         part = dots(left, right, *dims).astype(BF)
         sums.append(lax.psum_scatter(part, DP, scatter_dimension=2, tiled=True).astype(F32))
     return sums
+
+
+def plain_backward(
+    dense, cotangent, block_input, named, router_probs, dots_sum, grad_normed_two, router_rows,
+    hidden_one, gain_two, gain_one, full_query, full_key, full_value, full_output, query_rot, key_rot,
+    value_rows, allowed, log_total, cosine, sine_table, one_t, two_t, mixed_t, shared_act_t,
+    grad_sgate, grad_sup, normed_two, ggp_t, gup_t, act_t, rows_all, owner_grads,
+):
+    total_experts = router_rows.shape[0]
+    seq_len, heads_here = query_rot.shape[:2]
+    input_f = block_input.astype(F32)
+    scale_one = rms_scale(input_f)
+    scale_two = rms_scale(hidden_one)
+    grad_out = cotangent.astype(F32)
+    grad_rprobs = jnp.where(named, dots_sum, 0.0)
+    grad_logits = (
+        router_probs * (grad_rprobs - jnp.sum(grad_rprobs * router_probs, axis=-1, keepdims=True))
+    ).astype(BF)
+    grad_normed_two = grad_normed_two + dots(grad_logits, router_rows, ((1,), (0,)), ((), ()))
+    ffn_gain_full = jnp.sum(grad_normed_two * hidden_one * scale_two, axis=0)
+    weighted_two = grad_normed_two * gain_two
+    cube_two = scale_two * scale_two * scale_two
+    grad_hidden = (
+        grad_out
+        + scale_two * weighted_two
+        - hidden_one * cube_two * jnp.mean(hidden_one * weighted_two, axis=-1, keepdims=True)
+    )
+    grad_attn = grad_hidden.astype(BF)
+    grad_mixed = (
+        dots(grad_attn, full_output, ((1,), (1,)), ((), ()))
+        .astype(BF)
+        .reshape(seq_len, heads_here, HD)
+    )
+    prob_again = jnp.exp(masked_scores(query_rot, key_rot, allowed) - log_total)
+    grad_probs = dots(grad_mixed, value_rows, ((2,), (2,)), ((1,), (1,)))
+    grad_scores = (
+        prob_again * (grad_probs - jnp.sum(prob_again * grad_probs, axis=-1, keepdims=True))
+    ).astype(BF)
+    value_grad_rows = (
+        jnp.transpose(dots(prob_again.astype(BF), grad_mixed, ((1,), (0,)), ((0,), (1,))), (1, 0, 2))
+        .astype(BF)
+        .reshape(seq_len, heads_here * HD)
+    )
+    inverse_root = 1.0 / math.sqrt(HD)
+    grad_qrot = (
+        jnp.transpose(dots(grad_scores, key_rot, ((2,), (0,)), ((0,), (1,))), (1, 0, 2))
+        * inverse_root
+    )
+    grad_krot = (
+        jnp.transpose(dots(grad_scores, query_rot, ((1,), (0,)), ((0,), (1,))), (1, 0, 2))
+        * inverse_root
+    )
+    grad_qpre = (
+        unrotate(grad_qrot, cosine, sine_table).astype(BF).reshape(seq_len, heads_here * HD)
+    )
+    grad_kpre = (
+        unrotate(grad_krot, cosine, sine_table).astype(BF).reshape(seq_len, heads_here * HD)
+    )
+    grad_normed_one = dots(grad_qpre, full_query, ((1,), (1,)), ((), ()))
+    grad_normed_one = grad_normed_one + dots(grad_kpre, full_key, ((1,), (1,)), ((), ()))
+    grad_normed_one = grad_normed_one + dots(value_grad_rows, full_value, ((1,), (1,)), ((), ()))
+    grad_normed_one = lax.psum(grad_normed_one, TENSOR)
+    attn_gain_full = jnp.sum(grad_normed_one * input_f * scale_one, axis=0)
+    weighted_one = grad_normed_one * gain_one
+    cube_one = scale_one * scale_one * scale_one
+    input_grad = (
+        grad_hidden
+        + scale_one * weighted_one
+        - input_f * cube_one * jnp.mean(input_f * weighted_one, axis=-1, keepdims=True)
+    )
+    room = total_experts + 2 + (-(total_experts + 2) % 64)
+    logits_t = jnp.pad(grad_logits.T, ((0, room - total_experts), (0, 0)))
+    extra = jnp.concatenate([
+        jnp.zeros((total_experts, D), F32), attn_gain_full[None], ffn_gain_full[None],
+        jnp.zeros((room - total_experts - 2, D), F32)])
+    lefts = (one_t, one_t, one_t, mixed_t, two_t, two_t, shared_act_t, logits_t)
+    rights = (grad_qpre, grad_kpre, value_grad_rows, grad_attn, grad_sgate, grad_sup, cotangent, normed_two)
+    exp_left = (ggp_t, gup_t, act_t)
+    sums = plain_scatter(dense, lefts, rights, extra, exp_left, rows_all, owner_grads)
+    return sums, input_grad
 
 
 def body(
@@ -1371,15 +1539,10 @@
         first = here * expert_gate.shape[0]
         router_pad = jnp.pad(turn(router_rows, first, 0), ((0, 128 - total_experts), (0, 0)))
         named_pad = jnp.pad(turn(named_all, first, 1), ((0, 0), (0, 128 - total_experts)))
-        (hidden_one, normed_two, rows_all, logits, dots_sum, grad_normed_two, ffn_total, act_t, ggp_t, gup_t,
-         owner_grads, grad_sgate, grad_sup, shared_act_t, one_t, two_t, mixed_t) = middle(
+        (hidden_one, normed_two, rows_all, dots_sum, back, ffn_total, act_t, ggp_t, gup_t, gates, cot_all,
+         grad_sgate, grad_sup, shared_act_t, one_t, two_t, mixed_t) = middle(
             attn_part, block_input, gain_two[None], router_pad, named_pad, cotangent, normed_one,
             mixed_rows, experts, (sgate_t, sup_t, shared_down), owners, middle_order, 2)
-        grad_sgate = jnp.concatenate([grad_sgate[0], grad_sgate[1]], axis=1)
-        grad_sup = jnp.concatenate([grad_sup[0], grad_sup[1]], axis=1)
-        router_probs = jax.nn.softmax(
-            turn(logits[:, :total_experts], total_experts - first, 1), axis=-1)
-        dots_sum = dots_sum[:, :total_experts]
     else:
         (hidden_one, normed_two, rows_all, router_probs, dots_sum, grad_normed_two, ffn_total, act_t, ggp_t, gup_t,
          owner_grads, grad_sgate, grad_sup, shared_act_t) = plain_middle(
@@ -1390,82 +1553,30 @@
             lax.all_gather(shared_up, BOTH, axis=0, tiled=True),
             lax.all_gather(shared_down, BOTH, axis=1, tiled=True))
         one_t, two_t, mixed_t = normed_one.T, normed_two.T, mixed_rows.T
-    scale_two = rms_scale(hidden_one)
     block_output = (hidden_one + ffn_total).astype(BF)
-    grad_out = cotangent.astype(F32)
-    grad_rprobs = jnp.where(named, dots_sum, 0.0)
-    grad_logits = (
-        router_probs * (grad_rprobs - jnp.sum(grad_rprobs * router_probs, axis=-1, keepdims=True))
-    ).astype(BF)
-    grad_normed_two = grad_normed_two + dots(grad_logits, router_rows, ((1,), (0,)), ((), ()))
-    ffn_gain_full = jnp.sum(grad_normed_two * hidden_one * scale_two, axis=0)
-    weighted_two = grad_normed_two * gain_two
-    cube_two = scale_two * scale_two * scale_two
-    grad_hidden = (
-        grad_out
-        + scale_two * weighted_two
-        - hidden_one * cube_two * jnp.mean(hidden_one * weighted_two, axis=-1, keepdims=True)
-    )
-    grad_attn = grad_hidden.astype(BF)
-    grad_mixed = (
-        dots(grad_attn, full_output, ((1,), (1,)), ((), ()))
-        .astype(BF)
-        .reshape(seq_len, heads_here, HD)
-    )
-    prob_again = jnp.exp(masked_scores(query_rot, key_rot, allowed) - log_total)
-    grad_probs = dots(grad_mixed, value_rows, ((2,), (2,)), ((1,), (1,)))
-    grad_scores = (
-        prob_again * (grad_probs - jnp.sum(prob_again * grad_probs, axis=-1, keepdims=True))
-    ).astype(BF)
-    value_grad_rows = (
-        jnp.transpose(dots(prob_again.astype(BF), grad_mixed, ((1,), (0,)), ((0,), (1,))), (1, 0, 2))
-        .astype(BF)
-        .reshape(seq_len, heads_here * HD)
-    )
-    inverse_root = 1.0 / math.sqrt(HD)
-    grad_qrot = (
-        jnp.transpose(dots(grad_scores, key_rot, ((2,), (0,)), ((0,), (1,))), (1, 0, 2))
-        * inverse_root
-    )
-    grad_krot = (
-        jnp.transpose(dots(grad_scores, query_rot, ((1,), (0,)), ((0,), (1,))), (1, 0, 2))
-        * inverse_root
-    )
-    grad_qpre = (
-        unrotate(grad_qrot, cosine, sine_table).astype(BF).reshape(seq_len, heads_here * HD)
-    )
-    grad_kpre = (
-        unrotate(grad_krot, cosine, sine_table).astype(BF).reshape(seq_len, heads_here * HD)
-    )
-    grad_normed_one = dots(grad_qpre, full_query, ((1,), (1,)), ((), ()))
-    grad_normed_one = grad_normed_one + dots(grad_kpre, full_key, ((1,), (1,)), ((), ()))
-    grad_normed_one = grad_normed_one + dots(value_grad_rows, full_value, ((1,), (1,)), ((), ()))
-    grad_normed_one = (
-        pair_sum(grad_normed_one, 3) if kernels else lax.psum(grad_normed_one, TENSOR)
-    )
-    attn_gain_full = jnp.sum(grad_normed_one * input_f * scale_one, axis=0)
-    weighted_one = grad_normed_one * gain_one
-    cube_one = scale_one * scale_one * scale_one
-    input_grad = (
-        grad_hidden
-        + scale_one * weighted_one
-        - input_f * cube_one * jnp.mean(input_f * weighted_one, axis=-1, keepdims=True)
-    )
-    room = total_experts + 2 + (-(total_experts + 2) % 64)
-    logits_t = jnp.pad(grad_logits.T, ((0, room - total_experts), (0, 0)))
-    extra = jnp.concatenate([
-        jnp.zeros((total_experts, D), F32), attn_gain_full[None], ffn_gain_full[None],
-        jnp.zeros((room - total_experts - 2, D), F32)])
-    lefts = (one_t, one_t, one_t, mixed_t, two_t, two_t, shared_act_t, logits_t)
-    rights = (grad_qpre, grad_kpre, value_grad_rows, grad_attn, grad_sgate, grad_sup, cotangent, normed_two)
-    exp_left = (ggp_t, gup_t, act_t)
-    dense = ((("rows", "z"),) * 3
-             + (("cols", "z"), ("rows", "z"), ("rows", "p"), ("cols", "p"), ("cols", "z")))
+    dense = ((("rows", "z"),) + (("rows", "p"),) * 2
+             + (("cols", "p"),) + (("rows", "z"),) * 2 + (("cols", "z"),) * 2)
     if kernels:
-        sums = scatter(
-            dense, lefts, rights, extra, exp_left, rows_all, owner_grads, owners, scatter_order, 1)
+        pair = lambda first, last: jnp.concatenate([first, last], axis=-1)[:, 0]
+        flat = lambda v: v.reshape(seq_len, heads_here * HD)
+        given = dict(
+            one_t=one_t, mixed_t=mixed_t, two_t=two_t, sact_t=shared_act_t, gsg=grad_sgate, gsu=grad_sup,
+            cot=cotangent, normed=normed_two, ggp=ggp_t, gup=gup_t, act=act_t, rows_all=rows_all,
+            cot_all=cot_all, gates=gates, hidden=hidden_one, back=back, few=dots_sum,
+            named=jnp.pad(named.astype(F32), ((0, 0), (0, 128 - total_experts))),
+            gain_two=gain_two[None], gain_one=gain_one[None], inp=block_input,
+            q=flat(query_rot), k=flat(key_rot), v=flat(value_rows), cos=pair(cosine, cosine),
+            sin=pair(sine_table, -sine_table), mask=allowed.astype(F32),
+            router=jnp.pad(router_rows, ((0, 128 - total_experts), (0, 0))))
+        *sums, input_grad = scatter(
+            dense, given, (full_output, full_query, full_key, full_value), total_experts, owners,
+            scatter_order, 1)
     else:
-        sums = plain_scatter(dense, lefts, rights, extra, exp_left, rows_all, owner_grads)
+        sums, input_grad = plain_backward(
+            dense, cotangent, block_input, named, router_probs, dots_sum, grad_normed_two, router_rows,
+            hidden_one, gain_two, gain_one, full_query, full_key, full_value, full_output, query_rot, key_rot,
+            value_rows, allowed, log_total, cosine, sine_table, one_t, two_t, mixed_t, shared_act_t,
+            grad_sgate, grad_sup, normed_two, ggp_t, gup_t, act_t, rows_all, owner_grads)
     (query_grad, key_grad, value_grad, output_grad, shared_gate_grad, shared_up_grad,
      shared_down_grad, small_grad, expert_gate_grad, expert_up_grad, expert_down_grad) = sums
     return (

time: 1100 us -> 1070 us (0.973)
  other arithmetic: 22.8 us -> 11.3 us
    dot_general x11 -> x2, matrix products: 12.4 us -> 0.59 us  [dots(): return lax.dot_general(left, right, dims, preferred_element_type=F32)]
    unnamed x104 -> x37, local copies, waits for them, and re-layouts: 26.2 us -> 23.9 us
where the time goes in v4:
time: 1070 us; the launch traced here: 1050 us
  Pallas kernels  992 us (93%)
  local copies, waits for them, and re-layouts  34.7 us (3%)
  matrix products  11.4 us (1%)
  other arithmetic  11.3 us (1%)
    pallas_call x1, Pallas kernels, scatter(): pl.pallas_call(functools.partial(scatter_kernel, dense, units, n, order,...  471 us
    pallas_call x1, Pallas kernels, middle(): pl.pallas_call(functools.partial(middle_kernel, n, order), out_shape=[s f...  392 us
    pallas_call x1, Pallas kernels, gather(): pl.pallas_call(functools.partial(gather_kernel, leaves, n, starts), out_s...  130 us
    unnamed x37, local copies, waits for them, and re-layouts  23.9 us

profile of v4, /device:TPU:16, one launch (start us, length us, event | category | flops | bytes accessed | tf_op | source)
XLA Modules:
  0.0 1050.5 jit_solution(4336149205485006705)
XLA Ops:
  0.7 1.3 fusion.4
  4.8 1.4 fusion.16
  7.6 129.6 %shard_map.280 = (bf16[2048,1024]{1,0:T(8,128)(2,1)}, bf16[2048,1024]{1,0:T(8,128)(2,1)}, bf16[2048,1024]{1,0:T(8,128)(2,1)}, bf16[1024,2048]{1,0:T(8,128)(2,1)}...) custom-call(bf16[128,1024]{1,0:T(8,128)(2,1)} %refs_0_.1, ...), custom_call_target="tpu_custom_call" | custom-call | tf_op jit(solution)/shard_map/pallas_call | solution.py:242
  137.2 0.9 slice.40
  139.0 1.4 slice_convert_fusion
  143.3 3.1 convolution_convert_fusion.1.refs_23_
  146.6 3.0 convolution_bitcast_fusion
  155.1 3.9 fusion.21.refs_0_
  159.0 392.0 %shard_map.281 = (f32[128,2048]{1,0:T(8,128)}, bf16[128,2048]{1,0:T(8,128)(2,1)}, bf16[512,2048]{1,0:T(8,128)(2,1)}, f32[128,128]{1,0:T(8,128)}, f32[128,2048]{1...) custom-call(f32[128,2048]{1,0:T(8,128)} %fusion.21.refs_0_, ...), custom_call_target="tpu_custom_call" | custom-call | tf_op jit(solution)/shard_map/pallas_call | solution.py:1244
  550.9 2.5 add_convert_fusion
  553.4 470.5 %shard_map.282 = (f32[128,1024]{1,0:T(8,128)}, f32[128,1024]{1,0:T(8,128)}, f32[128,1024]{1,0:T(8,128)}, f32[1024,128]{1,0:T(8,128)}, f32[128,1408]{1,0:T(8,128)...) custom-call(bf16[2048,128]{1,0:T(8,128)(2,1)} %get-tuple-element.62., ...), custom_call_target="tpu_custom_call" | custom-call | tf_op jit(solution)/shard_map/pallas_call | solution.py:800
  1023.9 1.4 slice_bitcast_fusion.1
  1025.3 1.6 slice_bitcast_fusion
  1026.9 2.3 copy.101
  1029.2 1.9 copy.102
  1031.1 1.9 copy.103
  1033.0 1.9 copy.104
  1034.9 1.9 copy.105
  1036.7 2.9 copy.106
  1039.7 1.8 copy-done.3
  1041.5 2.8 copy.107
  1045.0 2.7 copy.108
  1047.7 0.9 copy.109
  1048.6 0.9 copy.110
  (57 shorter events, 15.2 us)
Async XLA Ops:
  0.6 142.4 %copy-start.2 = (bf16[128,2048]{1,0:T(8,128)(2,1)S(1)}, bf16[128,2048]{1,0:T(8,128)(2,1)}, u32[]{:S(2)}) copy-start(bf16[128,2048]{1,0:T(8,128)(2,1)} %refs_20_.1) | copy-start | bytes 1572868
  140.5 2.6 copy-start.9
  143.2 6.5 copy-start.1
  146.4 4.4 copy-start.5
  146.5 3.5 copy-start
  1023.9 12.8 %copy-start.4 = (f32[4,704,512]{2,1,0:T(8,128)S(1)}, f32[4,704,512]{2,1,0:T(8,128)}, u32[]{:S(2)}) copy-start(f32[4,704,512]{2,1,0:T(8,128)} %get-tuple-element.83) | copy-start | bytes 17301508
  1036.7 4.7 copy-start.3
  1036.7 7.5 slice-start
  1041.5 3.6 slice-start.1
  1045.0 2.7 copy-start.8
  1045.0 3.5 copy-start.7
  1045.0 4.4 copy-start.6

commit v5 on v4

--- a/solution.py
+++ b/solution.py
@@ -21,7 +21,7 @@
 rope_base = 10000.0
 masked_score = -1e30
 gather_starts = (1.91, 2.48, 3.88, 2.78, 2.0, 1.0)
-scatter_order = (102, 91, 81, 101, 87, 49, 76, 82, 92, 50, 51, 0, 1, 31, 32, 22, 97, 41, 7, 58, 104, 42, 77, 96, 83, 59, 61, 86, 24, 13, 14, 40, 103, 52, 78, 89, 99, 2, 3, 67, 70, 98, 4, 79, 69, 68, 23, 5, 53, 43, 60, 72, 54, 16, 105, 15, 55, 71, 25, 74, 100, 34, 56, 33, 73, 6, 93, 94, 45, 80, 62, 18, 44, 27, 75, 63, 36, 38, 17, 29, 28, 88, 84, 95, 9, 35, 8, 64, 47, 26, 20, 46, 37, 65, 19, 90, 57, 85, 21, 30, 11, 10, 39, 66, 48, 12)
+scatter_order = (91, 92, 86, 87, 49, 60, 102, 0, 96, 31, 93, 59, 1, 13, 14, 22, 23, 50, 43, 94, 32, 58, 52, 101, 82, 4, 88, 76, 33, 40, 51, 97, 25, 6, 15, 81, 41, 24, 16, 42, 34, 103, 53, 95, 5, 54, 99, 27, 83, 61, 26, 84, 45, 17, 98, 56, 35, 28, 2, 19, 55, 47, 77, 7, 104, 89, 62, 85, 44, 3, 67, 68, 69, 70, 9, 18, 57, 37, 20, 63, 78, 8, 21, 36, 72, 29, 100, 71, 38, 79, 105, 65, 90, 46, 30, 11, 73, 64, 39, 10, 74, 48, 80, 66, 75, 12)
 middle_order = (13, 8, 33, 113, 0, 9, 10, 14, 15, 57, 53, 91, 73, 37, 58, 59, 34, 35, 17, 18, 11, 12, 92, 19, 54, 55, 61, 77, 16, 3, 109, 99, 114, 81, 65, 66, 21, 25, 74, 67, 62, 36, 26, 27, 56, 69, 95, 100, 101, 82, 29, 30, 31, 93, 4, 115, 116, 110, 111, 20, 96, 97, 78, 28, 22, 23, 24, 94, 41, 63, 117, 5, 6, 7, 1, 68, 75, 76, 112, 98, 103, 32, 83, 84, 86, 60, 2, 70, 71, 72, 64, 102, 104, 127, 45, 42, 131, 38, 79, 80, 85, 87, 88, 89, 90, 105, 118, 135, 39, 40, 46, 49, 43, 128, 129, 106, 107, 108, 47, 121, 123, 44, 132, 119, 120, 122, 124, 125, 126, 136, 137, 50, 51, 52, 133, 134, 130, 139, 141, 48, 145, 138, 140, 142, 151, 143, 152, 144, 147, 146, 148, 149, 150, 153, 154)
 
 

time: 1070 us -> 1070 us (level)
  no operation moved by 1% of the time
where the time goes in v5:
time: 1070 us; the launch traced here: 1060 us
  Pallas kernels  997 us (93%)
  local copies, waits for them, and re-layouts  34.7 us (3%)
  matrix products  11.4 us (1%)
  other arithmetic  11.3 us (1%)
    pallas_call x1, Pallas kernels, scatter(): pl.pallas_call(functools.partial(scatter_kernel, dense, units, n, order,...  475 us
    pallas_call x1, Pallas kernels, middle(): pl.pallas_call(functools.partial(middle_kernel, n, order), out_shape=[s f...  393 us
    pallas_call x1, Pallas kernels, gather(): pl.pallas_call(functools.partial(gather_kernel, leaves, n, starts), out_s...  130 us
    unnamed x37, local copies, waits for them, and re-layouts  23.9 us

profile of v5, /device:TPU:16, one launch (start us, length us, event | category | flops | bytes accessed | tf_op | source)
XLA Modules:
  0.0 1055.7 jit_solution(2003882424673219504)
XLA Ops:
  0.7 1.3 fusion.4
  4.8 1.4 fusion.16
  7.6 129.6 %shard_map.280 = (bf16[2048,1024]{1,0:T(8,128)(2,1)}, bf16[2048,1024]{1,0:T(8,128)(2,1)}, bf16[2048,1024]{1,0:T(8,128)(2,1)}, bf16[1024,2048]{1,0:T(8,128)(2,1)}...) custom-call(bf16[128,1024]{1,0:T(8,128)(2,1)} %refs_0_.1, ...), custom_call_target="tpu_custom_call" | custom-call | tf_op jit(solution)/shard_map/pallas_call | solution.py:242
  137.2 0.9 slice.40
  139.0 1.4 slice_convert_fusion
  143.3 3.1 convolution_convert_fusion.1.refs_23_
  146.6 3.0 convolution_bitcast_fusion
  155.1 3.9 fusion.21.refs_0_
  159.0 392.7 %shard_map.281 = (f32[128,2048]{1,0:T(8,128)}, bf16[128,2048]{1,0:T(8,128)(2,1)}, bf16[512,2048]{1,0:T(8,128)(2,1)}, f32[128,128]{1,0:T(8,128)}, f32[128,2048]{1...) custom-call(f32[128,2048]{1,0:T(8,128)} %fusion.21.refs_0_, ...), custom_call_target="tpu_custom_call" | custom-call | tf_op jit(solution)/shard_map/pallas_call | solution.py:1244
  551.7 2.5 add_convert_fusion
  554.1 474.9 %shard_map.282 = (f32[128,1024]{1,0:T(8,128)}, f32[128,1024]{1,0:T(8,128)}, f32[128,1024]{1,0:T(8,128)}, f32[1024,128]{1,0:T(8,128)}, f32[128,1408]{1,0:T(8,128)...) custom-call(bf16[2048,128]{1,0:T(8,128)(2,1)} %get-tuple-element.62., ...), custom_call_target="tpu_custom_call" | custom-call | tf_op jit(solution)/shard_map/pallas_call | solution.py:800
  1029.1 1.4 slice_bitcast_fusion.1
  1030.4 1.6 slice_bitcast_fusion
  1032.0 2.3 copy.101
  1034.3 1.9 copy.102
  1036.2 1.9 copy.103
  1038.1 1.9 copy.104
  1040.0 1.9 copy.105
  1041.9 2.9 copy.106
  1044.8 1.8 copy-done.3
  1046.6 2.8 copy.107
  1050.2 2.7 copy.108
  1052.9 0.9 copy.109
  1053.7 0.9 copy.110
  (57 shorter events, 15.2 us)
Async XLA Ops:
  0.6 142.4 %copy-start.2 = (bf16[128,2048]{1,0:T(8,128)(2,1)S(1)}, bf16[128,2048]{1,0:T(8,128)(2,1)}, u32[]{:S(2)}) copy-start(bf16[128,2048]{1,0:T(8,128)(2,1)} %refs_20_.1) | copy-start | bytes 1572868
  140.5 2.6 copy-start.9
  143.2 6.5 copy-start.1
  146.4 4.4 copy-start.5
  146.5 3.5 copy-start
  1029.1 12.8 %copy-start.4 = (f32[4,704,512]{2,1,0:T(8,128)S(1)}, f32[4,704,512]{2,1,0:T(8,128)}, u32[]{:S(2)}) copy-start(f32[4,704,512]{2,1,0:T(8,128)} %get-tuple-element.83) | copy-start | bytes 17301508
  1041.9 4.7 copy-start.3
  1041.9 7.5 slice-start
  1046.6 3.6 slice-start.1
  1050.2 2.7 copy-start.8
  1050.2 3.5 copy-start.7
  1050.2 4.4 copy-start.6
